TPU v7x, 8 devices: a whole 2x2x1 slice. The times are simulated.
8 devices in a mesh: dp: 1 (over z), tp: 2 (over y), ep: 4 (over x, core).
Axes of the slice: x: 2, y: 2, z: 1, core: 2. Of those that a mesh axis runs over, the one named last changes fastest.
Arguments:
- hidden: bfloat16 [1024, 768], P(('dp', 'ep'))
- write_pos: int32 [1024], P(('dp', 'ep'))
- enc_mask: int32 [1024, 32], P(('dp', 'ep'))
- expert_idx: int32 [1024], P(('dp', 'ep'))
- self_keys: bfloat16 [2, 1024, 12, 64, 64], P(None, ('dp', 'ep'), 'tp')
- self_values: bfloat16 [2, 1024, 12, 64, 64], P(None, ('dp', 'ep'), 'tp')
- cross_keys: bfloat16 [2, 1024, 12, 32, 64], P(None, ('dp', 'ep'), 'tp')
- cross_values: bfloat16 [2, 1024, 12, 32, 64], P(None, ('dp', 'ep'), 'tp')
- rel_bias: float32 [12, 64], P('tp')
- norm_scale: float32 [2, 3, 768], replicated
- w_query: bfloat16 [2, 768, 768], P(None, None, 'tp')
- w_key: bfloat16 [2, 768, 768], P(None, None, 'tp')
- w_value: bfloat16 [2, 768, 768], P(None, None, 'tp')
- w_out: bfloat16 [2, 768, 768], P(None, 'tp')
- w_cross_query: bfloat16 [2, 768, 768], P(None, None, 'tp')
- w_cross_out: bfloat16 [2, 768, 768], P(None, 'tp')
- dense_gate: bfloat16 [768, 3072], P(None, 'tp')
- dense_up: bfloat16 [768, 3072], P(None, 'tp')
- dense_down: bfloat16 [3072, 768], P('tp')
- router: float32 [768, 32], replicated
- exp_gate: bfloat16 [32, 768, 3072], P('ep', None, 'tp')
- exp_up: bfloat16 [32, 768, 3072], P('ep', None, 'tp')
- exp_down: bfloat16 [32, 3072, 768], P('ep', 'tp')
Outputs:
- output 1: bfloat16 [1024, 768], P(('dp', 'ep'))
- output 2: bfloat16 [2, 1024, 12, 64, 64], P(None, ('dp', 'ep'), 'tp')
- output 3: bfloat16 [2, 1024, 12, 64, 64], P(None, ('dp', 'ep'), 'tp')
All inputs are finite; a program needn't handle non-finite values.
Results may differ from a plain program's by a relative error of at most 0.02.
Values are sent between devices in bfloat16 or wider.
A program may use at most 1 GiB of HBM per device.

v0:
```python
import jax
import jax.numpy as jnp
from jax import lax
from jax.sharding import PartitionSpec as P

EPS = 1e-6
NEG_BIG = -1e9


def rms_norm(h_cur, scale):
    h_float = h_cur.astype(jnp.float32)
    inv_rms = lax.rsqrt(jnp.mean(h_float * h_float, axis=-1, keepdims=True) + EPS)
    return (h_float * inv_rms * scale).astype(jnp.bfloat16)


def add_residual(h_cur, delta):
    return (h_cur.astype(jnp.float32) + delta.astype(jnp.float32)).astype(jnp.bfloat16)


def project(normed, weight):
    return jnp.dot(normed, weight, preferred_element_type=jnp.float32)


def self_attention(normed, write_pos, keys, values, w_query, w_key, w_value, w_out, rel_bias):
    tokens = normed.shape[0]
    heads, cache_len = rel_bias.shape
    head_dim = keys.shape[-1]
    query = project(normed, w_query).astype(jnp.bfloat16).reshape(tokens, heads, head_dim)
    key_new = project(normed, w_key).astype(jnp.bfloat16).reshape(tokens, heads, head_dim)
    value_new = project(normed, w_value).astype(jnp.bfloat16).reshape(tokens, heads, head_dim)
    distance = write_pos[:, None] - jnp.arange(cache_len)[None, :]
    at_slot = (distance == 0)[:, None, :, None]
    keys = jnp.where(at_slot, key_new[:, :, None, :], keys)
    values = jnp.where(at_slot, value_new[:, :, None, :], values)
    scores = jnp.einsum('thd,thld->thl', query, keys, preferred_element_type=jnp.float32)
    bias = jnp.take(rel_bias, jnp.maximum(distance, 0), axis=1)
    scores = jnp.where((distance >= 0)[:, None, :], scores + jnp.swapaxes(bias, 0, 1), NEG_BIG)
    attn_prob = jax.nn.softmax(scores, axis=-1).astype(jnp.bfloat16)
    context = jnp.einsum('thl,thld->thd', attn_prob, values, preferred_element_type=jnp.float32).astype(jnp.bfloat16)
    return project(context.reshape(tokens, heads * head_dim), w_out), keys, values


def cross_attention(normed, enc_mask, keys, values, w_query, w_out):
    tokens = normed.shape[0]
    heads = keys.shape[1]
    head_dim = keys.shape[-1]
    query = project(normed, w_query).astype(jnp.bfloat16).reshape(tokens, heads, head_dim)
    scores = jnp.einsum('thd,thsd->ths', query, keys, preferred_element_type=jnp.float32)
    scores = jnp.where((enc_mask > 0)[:, None, :], scores, NEG_BIG)
    attn_prob = jax.nn.softmax(scores, axis=-1).astype(jnp.bfloat16)
    context = jnp.einsum('ths,thsd->thd', attn_prob, values, preferred_element_type=jnp.float32).astype(jnp.bfloat16)
    return project(context.reshape(tokens, heads * head_dim), w_out)


def gated_ffn(normed, w_gate, w_up, w_down):
    product = (jax.nn.gelu(project(normed, w_gate)) * project(normed, w_up)).astype(jnp.bfloat16)
    return project(product, w_down)


def switch_layer(normed, expert_idx, router, exp_gate, exp_up, exp_down):
    tokens = normed.shape[0]
    experts = router.shape[1]
    capacity = (2 * tokens + experts - 1) // experts
    logits = jnp.dot(normed.astype(jnp.float32), router, preferred_element_type=jnp.float32)
    route_prob = jax.nn.softmax(logits, axis=-1)
    onehot = (expert_idx[:, None] == jnp.arange(experts)[None, :]).astype(jnp.int32)
    gate = jnp.sum(route_prob * onehot, axis=-1)
    slot = jnp.sum((jnp.cumsum(onehot, axis=0) - onehot) * onehot, axis=-1)
    dispatch = (onehot[:, :, None] * (slot[:, None, None] == jnp.arange(capacity)[None, None, :])).astype(jnp.bfloat16)
    buffers = jnp.einsum('tec,td->ecd', dispatch, normed, preferred_element_type=jnp.float32).astype(jnp.bfloat16)
    received = lax.all_to_all(buffers, 'ep', 0, 1, tiled=True)
    gate_in = jnp.einsum('ecd,edf->ecf', received, exp_gate, preferred_element_type=jnp.float32)
    lin_in = jnp.einsum('ecd,edf->ecf', received, exp_up, preferred_element_type=jnp.float32)
    product = (jax.nn.gelu(gate_in) * lin_in).astype(jnp.bfloat16)
    expert_out = jnp.einsum('ecf,efd->ecd', product, exp_down, preferred_element_type=jnp.float32).astype(jnp.bfloat16)
    expert_out = lax.psum(expert_out, 'tp')
    returned = lax.all_to_all(expert_out, 'ep', 1, 0, tiled=True)
    combined = jnp.einsum('tec,ecd->td', dispatch, returned, preferred_element_type=jnp.float32)
    return gate[:, None] * combined


def decode_body(hidden, write_pos, enc_mask, expert_idx, self_keys, self_values, cross_keys, cross_values, rel_bias, norm_scale, w_query, w_key, w_value, w_out, w_cross_query, w_cross_out, dense_gate, dense_up, dense_down, router, exp_gate, exp_up, exp_down):
    h_cur = hidden
    keys_list = []
    values_list = []
    for layer in range(2):
        normed = rms_norm(h_cur, norm_scale[layer, 0])
        attn_part, keys_new, values_new = self_attention(normed, write_pos, self_keys[layer], self_values[layer], w_query[layer], w_key[layer], w_value[layer], w_out[layer], rel_bias)
        h_cur = add_residual(h_cur, lax.psum(attn_part.astype(jnp.bfloat16), 'tp'))
        keys_list.append(keys_new)
        values_list.append(values_new)
        normed = rms_norm(h_cur, norm_scale[layer, 1])
        cross_part = cross_attention(normed, enc_mask, cross_keys[layer], cross_values[layer], w_cross_query[layer], w_cross_out[layer])
        h_cur = add_residual(h_cur, lax.psum(cross_part.astype(jnp.bfloat16), 'tp'))
        normed = rms_norm(h_cur, norm_scale[layer, 2])
        if layer == 0:
            ffn_part = gated_ffn(normed, dense_gate, dense_up, dense_down)
            h_cur = add_residual(h_cur, lax.psum(ffn_part.astype(jnp.bfloat16), 'tp'))
        else:
            h_cur = add_residual(h_cur, switch_layer(normed, expert_idx, router, exp_gate, exp_up, exp_down))
    return h_cur, jnp.stack(keys_list), jnp.stack(values_list)


def solution(mesh):
    batch = ('dp', 'ep')
    row_spec = P(batch, None)
    vec_spec = P(batch)
    cache_spec = P(None, batch, 'tp', None, None)
    col_spec = P(None, None, 'tp')
    out_rows = P(None, 'tp', None)
    in_specs = (row_spec, vec_spec, row_spec, vec_spec, cache_spec, cache_spec, cache_spec, cache_spec, P('tp', None), P(), col_spec, col_spec, col_spec, out_rows, col_spec, out_rows, P(None, 'tp'), P(None, 'tp'), P('tp', None), P(), P('ep', None, 'tp'), P('ep', None, 'tp'), P('ep', 'tp', None))
    out_specs = (row_spec, cache_spec, cache_spec)
    return jax.shard_map(decode_body, mesh=mesh, in_specs=in_specs, out_specs=out_specs, check_vma=False)
```

profile of v0, /device:TPU:0, one launch (start us, length us, event | category | flops | bytes accessed | tf_op | source)
XLA Modules:
  0.0 452.7 jit_solution(8486272298993469960)
XLA Ops:
  10.2 1.4 slice_reduce_fusion.1
  12.6 1.6 convolution_convert_fusion.12
  14.4 1.6 convolution_convert_fusion.11
  16.1 1.6 convolution_convert_fusion.13
  18.7 11.0 %multiply_reduce_fusion.3 = f32[256,6,64]{0,2,1:T(8,128)S(1)} fusion(f32[256,6,64]{0,2,1:T(8,128)} %convert, pred[256,64]{0,1:T(8,128)(4,1)S(1)} %copy.76, bf16[2,256,6,64,64]{1,4,3,2,0:T(8,128)(2,1)} %param.29, bf16[256,6,64]{0,2,1:T(8,128)(2,1)S(1)} %bitcast.165), kind=kLoop, calls=%fused_computation.14 | loop fusion | flops 25067520 | bytes 13582336
  29.7 7.8 %copy.97 = f32[256,6,64]{1,2,0:T(8,128)} copy(f32[256,6,64]{0,2,1:T(8,128)S(1)} %multiply_reduce_fusion.3) | data formatting | bytes 786432 | tf_op jit(solution)/shard_map/thd,thld->thl/dot_general | solution.py:35
  37.6 54.9 %gather_fusion = f32[16384,6]{1,0:T(8,128)} fusion(f32[6,64]{0,1:T(8,128)S(1)} %copy.78, s32[16384]{0:T(1024)S(1)} %broadcast_clamp_fusion), kind=kCustom, calls=%fused_computation.clone | custom fusion | bytes 851968 | tf_op jit(solution)/shard_map/jit(_take)/gather | solution.py:36
  92.4 12.8 %fusion.12 = f32[256,6,64]{1,2,0:T(8,128)} fusion(f32[256,6,64]{1,2,0:T(8,128)} %copy.97, f32[256,64,6]{2,1,0:T(8,128)} %bitcast.182, pred[256,64]{1,0:T(8,128)(4,1)S(1)} %get-tuple-element.23, pred[256,64]{1,0:T(8,128)(4,1)S(1)} %get-tuple-element.22), kind=kOutput, calls=%fused_computation.38 | output fusion | flops 691326 | bytes 1212416 | tf_op jit(solution)/shard_map/div | solution.py:38
  105.2 6.4 %copy.138 = f32[256,6,64]{0,2,1:T(8,128)S(1)} copy(f32[256,6,64]{1,2,0:T(8,128)} %fusion.12) | data formatting | bytes 786432
  111.7 9.4 %multiply_reduce_fusion.2 = bf16[256,6,64]{0,2,1:T(8,128)(2,1)} fusion(f32[256,6,64]{0,2,1:T(8,128)S(1)} %copy.138, pred[256,64]{0,1:T(8,128)(4,1)S(1)} %copy.76, bf16[2,256,6,64,64]{1,4,3,2,0:T(8,128)(2,1)} %param.30, bf16[256,6,64]{0,2,1:T(8,128)(2,1)S(1)} %bitcast.167), kind=kLoop, calls=%fused_computation.13 | loop fusion | flops 25067520 | bytes 13385728 | tf_op jit(solution)/shard_map/thl,thld->thd/dot_general | solution.py:39
  121.1 2.3 convolution_convert_fusion.5
  124.0 1.4 broadcast_compare_fusion.1
  125.4 21.0 %all-reduce.7.cloned.1.call-done = bf16[256,768]{1,0:T(8,128)(2,1)} async-done(((bf16[256,768]{1,0:T(8,128)(2,1)}), bf16[256,768]{1,0:T(8,128)(2,1)}) %all-reduce.7.cloned.1.call-update) | async-done | bytes 393232 | tf_op jit(solution)/shard_map/psum | solution.py:89
  146.4 1.2 fusion.57
  147.6 1.6 convolution_convert_fusion.10
  151.0 5.8 %multiply_reduce_fusion.7 = f32[256,6,32]{0,2,1:T(8,128)} fusion(f32[256,6,64]{0,2,1:T(8,128)S(1)} %convert.4, bf16[2,256,6,32,64]{1,4,3,2,0:T(8,128)(2,1)} %param.31), kind=kLoop, calls=%fused_computation.24 | loop fusion | flops 9388032 | bytes 6881280 | tf_op jit(solution)/shard_map/thd,thsd->ths/dot_general | solution.py:48
  157.8 4.3 multiply_reduce_fusion.6
  162.1 2.2 convolution_convert_fusion.4
  164.4 20.1 %all-reduce.9.cloned.1.call-done = bf16[256,768]{1,0:T(8,128)(2,1)} async-done(((bf16[256,768]{1,0:T(8,128)(2,1)}), bf16[256,768]{1,0:T(8,128)(2,1)}) %all-reduce.9.cloned.1.call-update) | async-done | bytes 393232 | tf_op jit(solution)/shard_map/psum | solution.py:94
  184.5 1.4 fusion.61
  185.9 2.7 fusion.121
  188.6 5.3 %convolution_convert_fusion.1 = bf16[256,768]{1,0:T(8,128)(2,1)} fusion(bf16[1536,768]{1,0:T(8,128)(2,1)} %param.43, bf16[768,1536]{1,0:T(8,128)(2,1)} %param.42, f32[256,1536]{1,0:T(8,128)} %fusion.121, bf16[256,768]{1,0:T(8,128)(2,1)S(1)} %get-tuple-element.15, f32[768]{0:T(1024)} %get-tuple-element.6, f32[256]{0:T(256)S(1)} %add_rsqrt_fusion.3), kind=kOutput, calls=%fused_computation.72 | convolution fusion | flops 1212874752 | bytes 7081984 | tf_op jit(solution)/shard_map/dot_general | solution.py:21
  195.4 18.7 %all-reduce.11.cloned.1.call-done = bf16[256,768]{1,0:T(8,128)(2,1)} async-done(((bf16[256,768]{1,0:T(8,128)(2,1)}), bf16[256,768]{1,0:T(8,128)(2,1)}) %all-reduce.11.cloned.1.call-update) | async-done | bytes 393232 | tf_op jit(solution)/shard_map/psum | solution.py:98
  214.0 1.2 fusion.65
  215.7 1.5 convolution_convert_fusion.7
  217.2 1.5 convolution_convert_fusion.9
  219.2 10.9 %multiply_reduce_fusion.1 = f32[256,6,64]{0,2,1:T(8,128)S(1)} fusion(f32[256,6,64]{0,2,1:T(8,128)S(1)} %convert.8, pred[256,64]{0,1:T(8,128)(4,1)S(1)} %copy.76, bf16[2,256,6,64,64]{1,4,3,2,0:T(8,128)(2,1)} %param.29, bf16[256,6,64]{0,2,1:T(8,128)(2,1)S(1)} %bitcast.169), kind=kLoop, calls=%fused_computation.12 | loop fusion | flops 25067520 | bytes 13582336
  230.1 7.6 %copy.120 = f32[256,6,64]{1,2,0:T(8,128)} copy(f32[256,6,64]{0,2,1:T(8,128)S(1)} %multiply_reduce_fusion.1) | data formatting | bytes 786432 | tf_op jit(solution)/shard_map/thd,thld->thl/dot_general | solution.py:35
  237.7 12.8 %fusion.13 = f32[256,6,64]{1,2,0:T(8,128)} fusion(f32[256,6,64]{1,2,0:T(8,128)} %copy.120, f32[256,64,6]{2,1,0:T(8,128)} %bitcast.183, pred[256,64]{1,0:T(8,128)(4,1)S(1)} %copy-done.12, pred[256,64]{1,0:T(8,128)(4,1)S(1)} %copy-done.10), kind=kOutput, calls=%fused_computation.39 | output fusion | flops 691326 | bytes 1212416 | tf_op jit(solution)/shard_map/div | solution.py:38
  250.5 6.6 %copy.142 = f32[256,6,64]{0,2,1:T(8,128)S(1)} copy(f32[256,6,64]{1,2,0:T(8,128)} %fusion.13) | data formatting | bytes 786432
  257.2 8.7 %multiply_reduce_fusion = bf16[256,6,64]{0,2,1:T(8,128)(2,1)S(1)} fusion(f32[256,6,64]{0,2,1:T(8,128)S(1)} %copy.142, pred[256,64]{0,1:T(8,128)(4,1)S(1)} %copy.76, bf16[2,256,6,64,64]{1,4,3,2,0:T(8,128)(2,1)} %param.30, bf16[256,6,64]{0,2,1:T(8,128)(2,1)S(1)} %bitcast.171), kind=kLoop, calls=%fused_computation.11 | loop fusion | flops 25067520 | bytes 13385728 | tf_op jit(solution)/shard_map/thl,thld->thd/dot_general | solution.py:39
  267.5 19.7 %all-reduce.13.cloned.1.call-done = bf16[256,768]{1,0:T(8,128)(2,1)} async-done(((bf16[256,768]{1,0:T(8,128)(2,1)}), bf16[256,768]{1,0:T(8,128)(2,1)}) %all-reduce.13.cloned.1.call-update) | async-done | bytes 393232 | tf_op jit(solution)/shard_map/psum | solution.py:89
  288.5 1.6 convolution_convert_fusion.6
  290.3 5.2 %multiply_reduce_fusion.5 = f32[256,6,32]{0,2,1:T(8,128)S(1)} fusion(f32[256,6,64]{0,2,1:T(8,128)S(1)} %convert.12, bf16[2,256,6,32,64]{1,4,3,2,0:T(8,128)(2,1)} %param.31), kind=kLoop, calls=%fused_computation.22 | loop fusion | flops 9388032 | bytes 6881280 | tf_op jit(solution)/shard_map/thd,thsd->ths/dot_general | solution.py:48
  296.2 4.3 multiply_reduce_fusion.4
  300.5 2.2 convolution_convert_fusion.2
  303.4 19.5 %all-reduce.15.cloned.1.call-done = bf16[256,768]{1,0:T(8,128)(2,1)} async-done(((bf16[256,768]{1,0:T(8,128)(2,1)}), bf16[256,768]{1,0:T(8,128)(2,1)}) %all-reduce.15.cloned.1.call-update) | async-done | bytes 393232 | tf_op jit(solution)/shard_map/psum | solution.py:94
  322.9 1.3 fusion.73
  325.5 14.4 %all_to_all.36 = bf16[32,16,768]{2,1,0:T(8,128)(2,1)S(1)} all-to-all(bf16[32,16,768]{2,1,0:T(8,128)(2,1)S(1)} %convolution_convert_fusion), channel_id=1, replica_groups=mesh['dp'=1,'tp'=2,'ep'=4] {'ep'}, dimensions={0} | all-to-all | bytes 1572864 | tf_op jit(solution)/shard_map/all_to_all | solution.py:71
  339.9 11.4 %fusion.177 = f32[8,64,1536]{2,1,0:T(8,128)} fusion(bf16[8,64,768]{2,1,0:T(8,128)(2,1)S(1)} %bitcast.162, bf16[8,768,1536]{2,1,0:T(8,128)(2,1)} %param.45), kind=kOutput, calls=%fused_computation.235 | convolution fusion | flops 1207959552 | bytes 22806528 | tf_op jit(solution)/shard_map/ecd,edf->ecf/dot_general | solution.py:72
  351.3 16.9 %fusion.39 = bf16[8,64,768]{2,1,0:T(8,128)(2,1)} fusion(bf16[8,1536,768]{2,1,0:T(8,128)(2,1)} %param.47, bf16[8,64,768]{2,1,0:T(8,128)(2,1)S(1)} %bitcast.163, bf16[8,768,1536]{2,1,0:T(8,128)(2,1)} %param.46, f32[8,64,1536]{2,1,0:T(8,128)} %fusion.177), kind=kOutput, calls=%fused_computation.67 | convolution fusion | flops 2424176640 | bytes 42467328 | tf_op jit(solution)/shard_map/ecf,efd->ecd/dot_general | solution.py:75
  368.3 33.3 %broadcast_select_fusion.1 = (bf16[1,256,6,64,64]{1,4,3,2,0:T(8,128)(2,1)}, bf16[1,256,6,64,64]{1,4,3,2,0:T(8,128)(2,1)}, bf16[1,256,6,64,64]{1,4,3,2,0:T(8,128)(2,1)}, bf16[1,256,6,64,64]{1,4,3,2,0:T(8,128)(2,1)}) fusion(pred[256,64]{0,1:T(8,128)(4,1)S(1)} %copy.76, bf16[2,256,6,64,64]{1,4,3,2,0:T(8,128)(2,1)} %param.30, ...), kind=kLoop, calls=%fused_computation.26 | loop fusion | flops 25165824 | bytes 101466112 | tf_op jit(solution)/shard_map/jit(_where)/select_n | solution.py:34
  401.6 2.5 copy.88
  404.1 3.5 all-to-all-start.1
  407.6 33.2 %pad_maximum_fusion = (bf16[2,256,6,64,64]{1,4,3,2,0:T(8,128)(2,1)}, bf16[2,256,6,64,64]{1,4,3,2,0:T(8,128)(2,1)}) fusion(bf16[1,256,6,64,64]{1,4,3,2,0:T(8,128)(2,1)} %get-tuple-element.20, bf16[1,256,6,64,64]{1,4,3,2,0:T(8,128)(2,1)} %get-tuple-element.21, bf16[1,256,6,64,64]{1,4,3,2,0:T(8,128)(2,1)} %get-tuple-element.17, ...), kind=kLoop, calls=%fused_computation.9 | loop fusion | flops 25165824 | bytes 100663296 | tf_op jit(solution)/shard_map/stack | solution.py:101
  440.9 1.3 fusion.172
  442.2 1.3 multiply_reduce_fusion.8
  443.5 1.9 fusion.42
  (96 shorter events, 16.8 us)
Async XLA Ops:
  7.2 178.7 %copy-start = (bf16[768,1536]{1,0:T(8,128)(2,1)S(1)}, bf16[768,1536]{1,0:T(8,128)(2,1)}, u32[]{:S(2)}) copy-start(bf16[768,1536]{1,0:T(8,128)(2,1)} %param.41) | copy-start | bytes 7077892
  7.2 139.2 %all-reduce.7.cloned.1.call-start = ((), (), s32[]{:S(2)}) async-start(), calls=%async_computation.2 | async-start | bytes 786432 | tf_op jit(solution)/shard_map/psum | solution.py:89
  8.2 84.2 %copy-start.9 = (pred[256,64]{1,0:T(8,128)(4,1)}, pred[256,64]{1,0:T(8,128)(4,1)S(1)}, u32[]{:S(2)}) copy-start(pred[256,64]{1,0:T(8,128)(4,1)S(1)} %get-tuple-element.22) | copy-start | bytes 49156
  8.2 84.2 %copy-start.11 = (pred[256,64]{1,0:T(8,128)(4,1)}, pred[256,64]{1,0:T(8,128)(4,1)S(1)}, u32[]{:S(2)}) copy-start(pred[256,64]{1,0:T(8,128)(4,1)S(1)} %get-tuple-element.23) | copy-start | bytes 49156
  111.7 34.7 %copy-start.2 = (bf16[256,768]{1,0:T(8,128)(2,1)S(1)}, bf16[256,768]{1,0:T(8,128)(2,1)}, u32[]{:S(2)}) copy-start(bf16[256,768]{1,0:T(8,128)(2,1)} %param.25) | copy-start | bytes 1179652
  123.4 61.1 %all-reduce.9.cloned.1.call-start = ((), (), s32[]{:S(2)}) async-start(), calls=%async_computation.3 | async-start | bytes 786432 | tf_op jit(solution)/shard_map/psum | solution.py:94
  164.4 49.7 %all-reduce.11.cloned.1.call-start = ((), (), s32[]{:S(2)}) async-start(), calls=%async_computation.4 | async-start | bytes 786432 | tf_op jit(solution)/shard_map/psum | solution.py:98
  188.6 26.7 %copy-start.17 = (f32[768]{0:T(1024)S(1)}, f32[768]{0:T(1024)}, u32[]{:S(2)}) copy-start(f32[768]{0:T(1024)} %get-tuple-element.5) | copy-start | bytes 9220
  188.6 26.7 %copy-start.18 = (bf16[2,768,384]{2,1,0:T(8,128)(2,1)S(1)}, bf16[2,768,384]{2,1,0:T(8,128)(2,1)}, u32[]{:S(2)}) copy-start(bf16[2,768,384]{2,1,0:T(8,128)(2,1)} %param.36) | copy-start | bytes 3538948
  193.9 93.3 %all-reduce.13.cloned.1.call-start = ((), (), s32[]{:S(2)}) async-start(), calls=%async_computation.5 | async-start | bytes 786432 | tf_op jit(solution)/shard_map/psum | solution.py:89
  219.2 18.5 %copy-start.10 = (pred[256,64]{1,0:T(8,128)(4,1)S(1)}, pred[256,64]{1,0:T(8,128)(4,1)}, u32[]{:S(2)}) copy-start(pred[256,64]{1,0:T(8,128)(4,1)} %copy-done.9) | copy-start | bytes 49156
  219.2 18.5 %copy-start.12 = (pred[256,64]{1,0:T(8,128)(4,1)S(1)}, pred[256,64]{1,0:T(8,128)(4,1)}, u32[]{:S(2)}) copy-start(pred[256,64]{1,0:T(8,128)(4,1)} %copy-done.11) | copy-start | bytes 49156
  257.1 8.8 %copy-start.19 = (bf16[2,384,768]{2,1,0:T(8,128)(2,1)S(1)}, bf16[2,384,768]{2,1,0:T(8,128)(2,1)}, u32[]{:S(2)}) copy-start(bf16[2,384,768]{2,1,0:T(8,128)(2,1)} %param.38) | copy-start | bytes 3538948
  257.1 10.2 %copy-start.14 = (s32[256]{0:T(256)S(1)}, s32[256]{0:T(256)}, u32[]{:S(2)}) copy-start(s32[256]{0:T(256)} %param.28) | copy-start | bytes 3076
  257.2 31.3 %copy-start.16 = (f32[768]{0:T(1024)S(1)}, f32[768]{0:T(1024)}, u32[]{:S(2)}) copy-start(f32[768]{0:T(1024)} %get-tuple-element.9) | copy-start | bytes 9220
  267.1 55.8 %all-reduce.15.cloned.1.call-start = ((), (), s32[]{:S(2)}) async-start(), calls=%async_computation.6 | async-start | bytes 786432 | tf_op jit(solution)/shard_map/psum | solution.py:94
  267.5 35.3 %copy-start.6 = (s32[256,32]{0,1:T(8,128)}, s32[256,32]{0,1:T(8,128)S(1)}, u32[]{:S(2)}) copy-start(s32[256,32]{0,1:T(8,128)S(1)} %fusion.133) | copy-start | bytes 98308
  290.3 32.6 %copy-start.3 = (bf16[256,768]{1,0:T(8,128)(2,1)S(1)}, bf16[256,768]{1,0:T(8,128)(2,1)}, u32[]{:S(2)}) copy-start(bf16[256,768]{1,0:T(8,128)(2,1)} %all-reduce.13.cloned.1.call-done) | copy-start | bytes 1179652
  290.3 34.6 %copy-start.13 = (f32[768]{0:T(1024)S(1)}, f32[768]{0:T(1024)}, u32[]{:S(2)}) copy-start(f32[768]{0:T(1024)} %get-tuple-element.4) | copy-start | bytes 9220
  302.8 98.9 %all-reduce.17.cloned.1.call-start = ((), (), s32[]{:S(2)}) async-start(), calls=%async_computation.7 | async-start | bytes 1572864 | tf_op jit(solution)/shard_map/psum | solution.py:76
  302.8 0.6 copy-start.7
  324.2 0.7 copy-start.4
  324.2 0.7 copy-start.15
  404.1 39.4 %all-to-all-start.1 = ((bf16[8,64,768]{2,0,1:T(8,128)(2,1)}), bf16[8,64,768]{2,0,1:T(8,128)(2,1)S(1)}, u32[]{:S(2)}, u32[]{:S(2)}) async-start(bf16[8,64,768]{2,0,1:T(8,128)(2,1)} %copy.88), calls=%async_computation.1 | async-start | bytes 1572864 | tf_op jit(solution)/shard_map/all_to_all | solution.py:77
  407.6 33.3 %copy-start.5 = (bf16[256,768]{1,0:T(8,128)(2,1)S(1)}, bf16[256,768]{1,0:T(8,128)(2,1)}, u32[]{:S(2)}) copy-start(bf16[256,768]{1,0:T(8,128)(2,1)} %copy-done.4) | copy-start | bytes 1179652
  407.6 35.9 %copy-start.8 = (s32[256,16]{0,1:T(8,128)S(1)}, s32[256,16]{0,1:T(8,128)}, u32[]{:S(2)}) copy-start(s32[256,16]{0,1:T(8,128)} %copy-done.7) | copy-start | bytes 49156
  407.6 37.8 %copy-start.1 = (bf16[768,1536]{1,0:T(8,128)(2,1)S(1)}, bf16[768,1536]{1,0:T(8,128)(2,1)}, u32[]{:S(2)}) copy-start(bf16[768,1536]{1,0:T(8,128)(2,1)} %param.41) | copy-start | bytes 7077892
Sparse Core Ops, SparseCore 0:
  123.6 22.8 all-reduce.6
  164.5 19.9 all-reduce.8
  194.0 19.9 all-reduce.10
  267.2 19.9 all-reduce.12
  302.9 19.9 all-reduce.14
  368.4 27.6 all-reduce.16
where the time goes:
time: 461 us; the launch traced here: 453 us
  other arithmetic  169 us (37%)
  waiting for transfers between devices  99.1 us (21%)
  local copies, waits for them, and re-layouts  91.6 us (20%)
  matrix products  59.3 us (13%)
  between operations  15 us (3%)
  blocking collectives  14.4 us (3%)
    gather x1, local copies, waits for them, and re-layouts, self_attention(): bias = jnp.take(rel_bias, jnp.maximum(distance, 0), axis=1)  54.9 us
    psum x2, waiting for transfers between devices, decode_body(): h_cur = add_residual(h_cur, lax.psum(attn_part.astype(jnp.bfloat16), 'tp'))  40.8 us
    psum x2, waiting for transfers between devices, decode_body(): h_cur = add_residual(h_cur, lax.psum(cross_part.astype(jnp.bfloat16), 'tp'))  39.6 us
    select_n x1, other arithmetic, self_attention(): values = jnp.where(at_slot, value_new[:, :, None, :], values)  33.3 us
    another operation x1, other arithmetic, decode_body(): return (h_cur, jnp.stack(keys_list), jnp.stack(values_list))  33.2 us
    dot_general x14, matrix products, project(): return jnp.dot(normed, weight, preferred_element_type=jnp.float32)  27.3 us
    div x2, other arithmetic, self_attention(): attn_prob = jax.nn.softmax(scores, axis=-1).astype(jnp.bfloat16)  25.7 us
    unnamed x6, other arithmetic  23.7 us
  transfers between devices with their start and end apart: 7, of which 5 were waited for; matrix products, arithmetic and copies ran while one was open for 16% of the time, Pallas kernels for 0%

commit v1 on v0

v1 whole, which is shorter than its diff:
```python
import functools

import jax
import jax.numpy as jnp
from jax import lax
from jax.experimental import pallas as pl
from jax.experimental.pallas import tpu as pltpu
from jax.sharding import PartitionSpec as P

EPS = 1e-6
NEG_BIG = -1e9
F32 = jnp.float32
BF16 = jnp.bfloat16
CHUNKS = 2
VMEM_SPEC = pl.BlockSpec(memory_space=pltpu.VMEM)
ANY_SPEC = pl.BlockSpec(memory_space=pl.ANY)
SWAP = [(0, 1), (1, 0)]


def rms_norm(h_cur, scale):
    h_float = h_cur.astype(F32)
    inv_rms = lax.rsqrt(jnp.mean(h_float * h_float, axis=-1, keepdims=True) + EPS)
    return (h_float * inv_rms * scale).astype(BF16)


def project(normed, weight):
    return jnp.dot(normed, weight, preferred_element_type=F32)


def add_parts(h_cur, own, peer):
    total = (own.astype(F32) + peer.astype(F32)).astype(BF16)
    return (h_cur.astype(F32) + total.astype(F32)).astype(BF16)


def softmax_rows(scores):
    top = jnp.max(scores, axis=0, keepdims=True)
    weight = jnp.exp(scores - top)
    return weight / jnp.sum(weight, axis=0, keepdims=True)


def self_kernel(layer, residual, *refs):
    if residual:
        h_ref, own_ref, peer_ref = refs[:3]
        refs = refs[3:]
    else:
        h_ref = refs[0]
        refs = refs[1:]
    pos_ref, scale_ref, bias_ref, wq_ref, wk_ref, wv_ref, wo_ref, k_ref, v_ref = refs[:9]
    refs = refs[9:]
    if len(refs) == 12 + residual:
        refs = refs[2:]
    if residual:
        h_out, refs = refs[0], refs[1:]
    part_ref, ko_ref, vo_ref, q_t, k_t, v_t, ctx_t, prob, posb = refs[:9]
    hot = refs[9]
    head = pl.program_id(0)
    slots, head_dim = k_ref.shape[0], k_ref.shape[1]

    @pl.when(head == 0)
    def _():
        h_cur = h_ref[...]
        if residual:
            h_cur = add_parts(h_cur, own_ref[...], peer_ref[...])
            h_out[...] = h_cur
        x = rms_norm(h_cur, scale_ref[0:1, :])
        q_t[...] = jnp.transpose(project(x, wq_ref[...])).astype(BF16).astype(F32)
        k_t[...] = jnp.transpose(project(x, wk_ref[...])).astype(BF16)
        v_t[...] = jnp.transpose(project(x, wv_ref[...])).astype(BF16)
        pos = pos_ref[...]
        posb[...] = jnp.broadcast_to(pos.astype(F32), posb.shape).astype(BF16)
        rows = lax.broadcasted_iota(jnp.int32, hot.shape, 0)
        hot[...] = (rows == pos).astype(F32)

    rows = pl.ds(pl.multiple_of(head * head_dim, head_dim), head_dim)
    q = q_t[rows, :]
    k_new = k_t[rows, :]
    posv = posb[...]
    for s8 in range(0, slots, 8):
        out_rows = []
        for s in range(s8, s8 + 8):
            cur = jnp.where(posv == jnp.asarray(s, BF16), k_new, k_ref[s])
            ko_ref[s] = cur
            out_rows.append(jnp.sum(cur.astype(F32) * q, axis=0, keepdims=True))
        prob[s8:s8 + 8, :] = jnp.concatenate(out_rows, axis=0)
    line = jnp.broadcast_to(bias_ref[pl.ds(head, 1), :], (slots, 128))
    table = pltpu.roll(line, 0, 1, stride=1, stride_axis=0)
    bias = jnp.dot(table, hot[...], precision=lax.Precision.HIGHEST, preferred_element_type=F32)
    slot_id = lax.broadcasted_iota(jnp.int32, bias.shape, 0)
    scores = jnp.where(slot_id <= pos_ref[...], prob[...] + bias, NEG_BIG)
    prob[...] = softmax_rows(scores).astype(BF16).astype(F32)
    v_new = v_t[rows, :]
    acc = jnp.zeros(q.shape, F32)
    for s in range(slots):
        cur = jnp.where(posv == jnp.asarray(s, BF16), v_new, v_ref[s])
        vo_ref[s] = cur
        acc = acc + prob[s:s + 1, :] * cur.astype(F32)
    ctx_t[rows, :] = acc

    @pl.when(head == pl.num_programs(0) - 1)
    def _():
        ctx = jnp.transpose(ctx_t[...]).astype(BF16)
        part_ref[...] = project(ctx, wo_ref[...]).astype(BF16)


def self_call(layer, chunk, h_cur, parts, pos, scale, bias, wq, wk, wv, wo, keys, values, outs):
    heads, slots, head_dim, tokens = keys.shape[1:]
    tc = tokens // CHUNKS
    dim = wq.shape[1]
    width = wq.shape[2]
    residual = parts is not None

    def whole(rows, cols):
        return pl.BlockSpec((None, rows, cols), lambda i: (layer, 0, 0))

    row_spec = pl.BlockSpec((tc, dim), lambda i: (chunk if h_cur.shape[0] != tc else 0, 0))
    fixed = pl.BlockSpec((tc, dim), lambda i: (0, 0))
    cache = pl.BlockSpec((None, None, slots, head_dim, tc), lambda i: (layer, i, 0, 0, chunk))
    in_specs = [row_spec] + ([fixed, fixed] if residual else [])
    in_specs += [pl.BlockSpec((1, tc), lambda i: (0, chunk)), whole(3, dim), pl.BlockSpec(bias.shape, lambda i: (0, 0)), whole(dim, width), whole(dim, width), whole(dim, width), whole(width, dim), cache, cache]
    args = [h_cur] + (list(parts) if residual else []) + [pos, scale, bias, wq, wk, wv, wo, keys, values]
    out_shape = [jax.ShapeDtypeStruct((tc, dim), BF16)] * (1 + residual)
    out_specs = [fixed] * (1 + residual)
    aliases = {}
    if outs is not None:
        aliases = {len(args): len(out_shape), len(args) + 1: len(out_shape) + 1}
        args += list(outs)
        in_specs += [ANY_SPEC, ANY_SPEC]
    out_shape += [jax.ShapeDtypeStruct(keys.shape, BF16)] * 2
    out_specs += [cache, cache]
    size = heads * slots * head_dim * tc
    return pl.pallas_call(
        functools.partial(self_kernel, layer, residual),
        grid=(heads,),
        in_specs=in_specs,
        out_specs=out_specs,
        out_shape=out_shape,
        input_output_aliases=aliases,
        scratch_shapes=[
            pltpu.VMEM((width, tc), F32),
            pltpu.VMEM((width, tc), BF16),
            pltpu.VMEM((width, tc), BF16),
            pltpu.VMEM((width, tc), F32),
            pltpu.VMEM((slots, tc), F32),
            pltpu.VMEM((head_dim, tc), BF16),
            pltpu.VMEM((128, tc), F32),
        ],
        compiler_params=pltpu.CompilerParams(dimension_semantics=("arbitrary",), vmem_limit_bytes=40 << 20),
        cost_estimate=pl.CostEstimate(flops=size * 400, bytes_accessed=size * 8, transcendentals=0),
        name=f"self{layer}_{chunk}",
    )(*args)


def cross_kernel(h_ref, own_ref, peer_ref, mask_ref, scale_ref, wq_ref, wo_ref, k_ref, v_ref, h_out, part_ref, q_t, ctx_t, prob):
    step = pl.program_id(0)
    per, slots, head_dim, _ = k_ref.shape

    @pl.when(step == 0)
    def _():
        h_cur = add_parts(h_ref[...], own_ref[...], peer_ref[...])
        h_out[...] = h_cur
        x = rms_norm(h_cur, scale_ref[1:2, :])
        q_t[...] = jnp.transpose(project(x, wq_ref[...])).astype(BF16).astype(F32)

    valid = mask_ref[...] > 0
    for j in range(per):
        rows = pl.ds(pl.multiple_of((step * per + j) * head_dim, head_dim), head_dim)
        q = q_t[rows, :]
        for s8 in range(0, slots, 8):
            out_rows = []
            for s in range(s8, s8 + 8):
                out_rows.append(jnp.sum(k_ref[j, s].astype(F32) * q, axis=0, keepdims=True))
            prob[s8:s8 + 8, :] = jnp.concatenate(out_rows, axis=0)
        scores = jnp.where(valid, prob[...], NEG_BIG)
        prob[...] = softmax_rows(scores).astype(BF16).astype(F32)
        acc = jnp.zeros(q.shape, F32)
        for s in range(slots):
            acc = acc + prob[s:s + 1, :] * v_ref[j, s].astype(F32)
        ctx_t[rows, :] = acc

    @pl.when(step == pl.num_programs(0) - 1)
    def _():
        ctx = jnp.transpose(ctx_t[...]).astype(BF16)
        part_ref[...] = project(ctx, wo_ref[...]).astype(BF16)


def cross_call(layer, chunk, h_cur, parts, mask, scale, wq, wo, keys, values, per=2):
    heads, slots, head_dim, tokens = keys.shape[1:]
    tc = tokens // CHUNKS
    dim = wq.shape[1]
    width = wq.shape[2]

    def whole(rows, cols):
        return pl.BlockSpec((None, rows, cols), lambda i: (layer, 0, 0))

    row_spec = pl.BlockSpec((tc, dim), lambda i: (chunk if h_cur.shape[0] != tc else 0, 0))
    fixed = pl.BlockSpec((tc, dim), lambda i: (0, 0))
    cache = pl.BlockSpec((None, per, slots, head_dim, tc), lambda i: (layer, i, 0, 0, chunk))
    size = heads * slots * head_dim * tc
    return pl.pallas_call(
        cross_kernel,
        grid=(heads // per,),
        in_specs=[row_spec, fixed, fixed, pl.BlockSpec((slots, tc), lambda i: (0, chunk)), whole(3, dim), whole(dim, width), whole(width, dim), cache, cache],
        out_specs=[fixed, fixed],
        out_shape=[jax.ShapeDtypeStruct((tc, dim), BF16)] * 2,
        scratch_shapes=[pltpu.VMEM((width, tc), F32), pltpu.VMEM((width, tc), F32), pltpu.VMEM((slots, tc), F32)],
        compiler_params=pltpu.CompilerParams(dimension_semantics=("arbitrary",), vmem_limit_bytes=32 << 20),
        cost_estimate=pl.CostEstimate(flops=size * 400, bytes_accessed=size * 4, transcendentals=0),
        name=f"cross{layer}_{chunk}",
    )(h_cur, *parts, mask, scale, wq, wo, keys, values)


def dense_kernel(h_ref, own_ref, peer_ref, scale_ref, wg_ref, wu_ref, wd_ref, h_out, part_ref, x_scr, acc):
    step = pl.program_id(0)

    @pl.when(step == 0)
    def _():
        h_cur = add_parts(h_ref[...], own_ref[...], peer_ref[...])
        h_out[...] = h_cur
        x_scr[...] = rms_norm(h_cur, scale_ref[2:3, :])
        acc[...] = jnp.zeros_like(acc)

    x = x_scr[...]
    product = (jax.nn.gelu(project(x, wg_ref[...])) * project(x, wu_ref[...])).astype(BF16)
    acc[...] += project(product, wd_ref[...])

    @pl.when(step == pl.num_programs(0) - 1)
    def _():
        part_ref[...] = acc[...].astype(BF16)


def dense_call(chunk, h_cur, parts, scale, wg, wu, wd, tile=512):
    tc, dim = h_cur.shape
    width = wg.shape[1]
    fixed = pl.BlockSpec((tc, dim), lambda i: (0, 0))
    return pl.pallas_call(
        dense_kernel,
        grid=(width // tile,),
        in_specs=[fixed, fixed, fixed, pl.BlockSpec((None, 3, dim), lambda i: (0, 0, 0)), pl.BlockSpec((dim, tile), lambda i: (0, i)), pl.BlockSpec((dim, tile), lambda i: (0, i)), pl.BlockSpec((tile, dim), lambda i: (i, 0))],
        out_specs=[fixed, fixed],
        out_shape=[jax.ShapeDtypeStruct((tc, dim), BF16)] * 2,
        scratch_shapes=[pltpu.VMEM((tc, dim), BF16), pltpu.VMEM((tc, dim), F32)],
        compiler_params=pltpu.CompilerParams(dimension_semantics=("arbitrary",), vmem_limit_bytes=32 << 20),
        cost_estimate=pl.CostEstimate(flops=6 * tc * dim * width, bytes_accessed=6 * dim * width, transcendentals=0),
        name=f"dense_{chunk}",
    )(h_cur, *parts, scale, wg, wu, wd)


def switch_layer(normed, expert_idx, router, exp_gate, exp_up, exp_down):
    tokens = normed.shape[0]
    experts = router.shape[1]
    capacity = (2 * tokens + experts - 1) // experts
    logits = jnp.dot(normed.astype(F32), router, preferred_element_type=F32)
    route_prob = jax.nn.softmax(logits, axis=-1)
    onehot = (expert_idx[:, None] == jnp.arange(experts)[None, :]).astype(jnp.int32)
    gate = jnp.sum(route_prob * onehot, axis=-1)
    slot = jnp.sum((jnp.cumsum(onehot, axis=0) - onehot) * onehot, axis=-1)
    dispatch = (onehot[:, :, None] * (slot[:, None, None] == jnp.arange(capacity)[None, None, :])).astype(BF16)
    buffers = jnp.einsum('tec,td->ecd', dispatch, normed, preferred_element_type=F32).astype(BF16)
    received = lax.all_to_all(buffers, 'ep', 0, 1, tiled=True)
    gate_in = jnp.einsum('ecd,edf->ecf', received, exp_gate, preferred_element_type=F32)
    lin_in = jnp.einsum('ecd,edf->ecf', received, exp_up, preferred_element_type=F32)
    product = (jax.nn.gelu(gate_in) * lin_in).astype(BF16)
    expert_out = jnp.einsum('ecf,efd->ecd', product, exp_down, preferred_element_type=F32).astype(BF16)
    returned = lax.all_to_all(expert_out, 'ep', 1, 0, tiled=True)
    combined = jnp.einsum('tec,ecd->td', dispatch, returned, preferred_element_type=F32).astype(BF16)
    peer = lax.ppermute(combined, 'tp', SWAP)
    return gate[:, None] * (combined.astype(F32) + peer.astype(F32))


def swap(part):
    return part, lax.ppermute(part, 'tp', SWAP)


def decode_body(hidden, write_pos, enc_mask, expert_idx, self_keys, self_values, cross_keys, cross_values, rel_bias, norm_scale, w_query, w_key, w_value, w_out, w_cross_query, w_cross_out, dense_gate, dense_up, dense_down, router, exp_gate, exp_up, exp_down):
    order = (0, 2, 3, 4, 1)
    keys, values = jnp.transpose(self_keys, order), jnp.transpose(self_values, order)
    ckeys, cvalues = jnp.transpose(cross_keys, order), jnp.transpose(cross_values, order)
    pos = write_pos.reshape(1, -1)
    mask = enc_mask.T
    bias = jnp.pad(rel_bias, ((0, 8 - rel_bias.shape[0]), (0, 128 - rel_bias.shape[1])))
    outs = None
    h_cur = [hidden] * CHUNKS
    parts = [None] * CHUNKS
    for layer in range(2):
        for c in range(CHUNKS):
            res = self_call(layer, c, h_cur[c], parts[c], pos, norm_scale, bias, w_query, w_key, w_value, w_out, keys, values, outs)
            if parts[c] is not None:
                h_cur[c] = res[0]
            parts[c] = swap(res[-3])
            outs = res[-2:]
        for c in range(CHUNKS):
            h_cur[c], part = cross_call(layer, c, h_cur[c], parts[c], mask, norm_scale, w_cross_query, w_cross_out, ckeys, cvalues)
            parts[c] = swap(part)
        if layer == 0:
            for c in range(CHUNKS):
                h_cur[c], part = dense_call(c, h_cur[c], parts[c], norm_scale, dense_gate, dense_up, dense_down)
                parts[c] = swap(part)
    h_all = jnp.concatenate([add_parts(h_cur[c], *parts[c]) for c in range(CHUNKS)])
    normed = rms_norm(h_all, norm_scale[1, 2])
    delta = switch_layer(normed, expert_idx, router, exp_gate, exp_up, exp_down)
    h_all = (h_all.astype(F32) + delta).astype(BF16)
    back = (0, 4, 1, 2, 3)
    return h_all, jnp.transpose(outs[0], back), jnp.transpose(outs[1], back)


def solution(mesh):
    batch = ('dp', 'ep')
    row_spec = P(batch, None)
    vec_spec = P(batch)
    cache_spec = P(None, batch, 'tp', None, None)
    col_spec = P(None, None, 'tp')
    out_rows = P(None, 'tp', None)
    in_specs = (row_spec, vec_spec, row_spec, vec_spec, cache_spec, cache_spec, cache_spec, cache_spec, P('tp', None), P(), col_spec, col_spec, col_spec, out_rows, col_spec, out_rows, P(None, 'tp'), P(None, 'tp'), P('tp', None), P(), P('ep', None, 'tp'), P('ep', None, 'tp'), P('ep', 'tp', None))
    out_specs = (row_spec, cache_spec, cache_spec)
    return jax.shard_map(decode_body, mesh=mesh, in_specs=in_specs, out_specs=out_specs, check_vma=False)
```

time: 461 us -> 193 us (0.42); the launches traced: 453 us -> 192 us
  other arithmetic: 169 us -> 3.41 us
  Pallas kernels: 0 us -> 82 us
  waiting for transfers between devices: 99.1 us -> 18 us
  local copies, waits for them, and re-layouts: 91.6 us -> 21.8 us
  matrix products: 59.3 us -> 26.1 us
  between operations: 15 us -> 1.01 us
  blocking collectives: 14.4 us -> 28.1 us
  starting transfers between devices: 4.44 us -> 11.6 us
    psum x6 -> x0, waiting for transfers between devices: 99 us -> none  [the longest x2 40.8 us: decode_body(): h_cur = add_residual(h_cur, lax.psum(attn_part.astype(jnp.bfloat16), 'tp'))]
    pallas_call x0 -> x10, Pallas kernels: none -> 82 us  [the longest x4 57 us: self_call(): pl.pallas_call(functools.partial(self_kernel, layer, residual), grid=(hea...]
    gather x1 -> x0, local copies, waits for them, and re-layouts: 54.9 us -> none  [self_attention(): bias = jnp.take(rel_bias, jnp.maximum(distance, 0), axis=1)]
    dot_general x6 -> x0, other arithmetic: 37.7 us -> none  [the longest x2 18.1 us: self_attention(): jnp.einsum('thl,thld->thd', attn_prob, values, preferred_element_type=jnp...]
    select_n x1 -> x0, other arithmetic: 33.3 us -> none  [self_attention(): values = jnp.where(at_slot, value_new[:, :, None, :], values)]
    dot_general x19 -> x5, matrix products: 59.3 us -> 26.1 us  [the longest x1 16.4 us: switch_layer(): jnp.einsum('ecf,efd->ecd', product, exp_down, preferred_element_type=F32)]
    another operation x3 -> x2, other arithmetic: 33.8 us -> 1.32 us  [the longest x1 33.2 us: decode_body(): return (h_cur, jnp.stack(keys_list), jnp.stack(values_list))]
    div x4 -> x0, other arithmetic: 27.4 us -> none  [the longest x2 25.7 us: self_attention(): attn_prob = jax.nn.softmax(scores, axis=-1).astype(jnp.bfloat16)]
  transfers between devices with their start and end apart: 7 -> 11, of which waited for: 5 -> 4; matrix products, arithmetic and copies ran while one was open for 16% -> 2% of each run, Pallas kernels for 0% -> 35%
where the time goes in v1:
time: 193 us; the launch traced here: 192 us
  Pallas kernels  82 us (42%)
  blocking collectives  28.1 us (15%)
  matrix products  26.1 us (14%)
  local copies, waits for them, and re-layouts  21.8 us (11%)
  waiting for transfers between devices  18 us (9%)
  starting transfers between devices  11.6 us (6%)
  other arithmetic  3.41 us (2%)
    pallas_call x4, Pallas kernels, self_call(): pl.pallas_call(functools.partial(self_kernel, layer, residual), grid=(hea...  57 us
    pallas_call x4, Pallas kernels, cross_call(): pl.pallas_call(cross_kernel, grid=(heads // per,), in_specs=[row_spec, fi...  20 us
    unnamed x61, local copies, waits for them, and re-layouts  17.7 us
    dot_general x1, matrix products, switch_layer(): jnp.einsum('ecf,efd->ecd', product, exp_down, preferred_element_type=F32)  16.4 us
    all_to_all x1, blocking collectives, switch_layer(): received = lax.all_to_all(buffers, 'ep', 0, 1, tiled=True)  14 us
    all_to_all x1, blocking collectives, switch_layer(): returned = lax.all_to_all(expert_out, 'ep', 1, 0, tiled=True)  14 us
    ppermute x10, starting transfers between devices, swap(): return (part, lax.ppermute(part, 'tp', SWAP))  11.6 us
    ppermute x1, waiting for transfers between devices, switch_layer(): peer = lax.ppermute(combined, 'tp', SWAP)  9.57 us
  transfers between devices with their start and end apart: 11, of which 4 were waited for; matrix products, arithmetic and copies ran while one was open for 2% of the time, Pallas kernels for 35%

profile of v1, /device:TPU:0, one launch (start us, length us, event | category | flops | bytes accessed | tf_op | source)
XLA Modules:
  0.0 191.9 jit_solution(907501367321430489)
XLA Ops:
  0.6 0.8 copy.60.refs_2_.scale_ref.refs_4_
  1.4 0.7 pad.4.refs_3_.refs_5_
  2.1 1.3 copy-done.5
  3.4 1.3 copy-done.7
  4.6 1.3 copy-done.9
  5.9 1.3 copy-done.11
  7.2 1.0 copy-done.19
  8.2 0.7 copy-done.22
  8.9 14.1 %self0_0.1 = (bf16[128,768]{1,0:T(8,128)(2,1)S(1)}, bf16[2,6,64,64,256]{4,3,2,1,0:T(8,128)(2,1)}, bf16[2,6,64,64,256]{4,3,2,1,0:T(8,128)(2,1)}) custom-call(bf16[256,768]{1,0:T(8,128)(2,1)S(1)} %copy-done.19, s32[1,256]{1,0:T(1,128)S(1)} %bitcast.59, f32[2,3,768]{2,1,0:T(4,128)S(1)} %copy.60.refs_2_.scale_ref.refs_4_, f32[8,128]{1,0:T(8,128)S(1)} %pad.4.refs_3_.refs_5_, ...), custom_call_target="tpu_custom_call" | custom-call | flops 1258291200 | bytes 25165824 | tf_op jit(solution)/shard_map/self0_0/pallas_call | solution.py:131
  23.0 3.4 %collective-permute-start = (bf16[128,768]{1,0:T(8,128)(2,1)S(1)}, bf16[128,768]{1,0:T(8,128)(2,1)}, u32[]{:S(2)}, u32[]{:S(2)}) collective-permute-start(bf16[128,768]{1,0:T(8,128)(2,1)S(1)} %get-tuple-element.29.own_ref), channel_id=1, source_target_pairs={{0,4},{4,0},{1,5},{5,1},{2,6},{6,2},{3,7},{7,3}} | collective-permute-start | bytes 589832 | tf_op jit(solution)/shard_map/ppermute | solution.py:271
  26.4 14.3 %self0_1.1 = (bf16[128,768]{1,0:T(8,128)(2,1)S(1)}, bf16[2,6,64,64,256]{4,3,2,1,0:T(8,128)(2,1)}, bf16[2,6,64,64,256]{4,3,2,1,0:T(8,128)(2,1)}) custom-call(bf16[256,768]{1,0:T(8,128)(2,1)S(1)} %copy-done.19, s32[1,256]{1,0:T(1,128)S(1)} %bitcast.60, ...), custom_call_target="tpu_custom_call", output_to_operand_aliasing={{1}: (10, {}), {2}: (11, {})} | custom-call | flops 1258291200 | bytes 25165824 | tf_op jit(solution)/shard_map/self0_1/pallas_call | solution.py:131
  40.7 0.6 fusion.27
  41.3 1.3 reduce-window.6
  42.6 0.2 slice_reduce_fusion
  42.8 4.6 %copy-done.1 = bf16[2,256,6,32,64]{1,4,3,2,0:T(8,128)(2,1)S(1)} copy-done((bf16[2,256,6,32,64]{1,4,3,2,0:T(8,128)(2,1)S(1)}, bf16[2,256,6,32,64]{1,4,3,2,0:T(8,128)(2,1)}, u32[]{:S(2)}) %copy-start.1) | copy-done | bytes 12582936
  47.4 5.6 %cross0_0.1 = (bf16[128,768]{1,0:T(8,128)(2,1)S(1)}, bf16[128,768]{1,0:T(8,128)(2,1)S(1)}) custom-call(bf16[256,768]{1,0:T(8,128)(2,1)S(1)} %copy-done.20, bf16[128,768]{1,0:T(8,128)(2,1)S(1)} %get-tuple-element.29.own_ref, bf16[128,768]{1,0:T(8,128)(2,1)} %collective-permute-done.peer_ref, s32[32,256]{1,0:T(8,128)S(1)} %bitcast.55, ...), custom_call_target="tpu_custom_call" | custom-call | flops 629145600 | bytes 6291456 | tf_op jit(solution)/shard_map/cross0_0/pallas_call | solution.py:199
  53.0 2.0 %collective-permute-start.1 = (bf16[128,768]{1,0:T(8,128)(2,1)S(1)}, bf16[128,768]{1,0:T(8,128)(2,1)S(1)}, u32[]{:S(2)}, u32[]{:S(2)}) collective-permute-start(bf16[128,768]{1,0:T(8,128)(2,1)S(1)} %get-tuple-element.31.own_ref), channel_id=1, source_target_pairs={{0,4},{4,0},{1,5},{5,1},{2,6},{6,2},{3,7},{7,3}} | collective-permute-start | bytes 589832 | tf_op jit(solution)/shard_map/ppermute | solution.py:271
  55.1 4.9 %cross0_1.1 = (bf16[128,768]{1,0:T(8,128)(2,1)S(1)}, bf16[128,768]{1,0:T(8,128)(2,1)S(1)}) custom-call(bf16[256,768]{1,0:T(8,128)(2,1)S(1)} %copy-done.20, bf16[128,768]{1,0:T(8,128)(2,1)S(1)} %get-tuple-element.42.own_ref, bf16[128,768]{1,0:T(8,128)(2,1)S(1)} %collective-permute-done.5.peer_ref, s32[32,256]{1,0:T(8,128)S(1)} %bitcast.56, ...), custom_call_target="tpu_custom_call" | custom-call | flops 629145600 | bytes 6291456 | tf_op jit(solution)/shard_map/cross0_1/pallas_call | solution.py:199
  60.1 2.5 %dense_0.1 = (bf16[128,768]{1,0:T(8,128)(2,1)S(1)}, bf16[128,768]{1,0:T(8,128)(2,1)S(1)}) custom-call(bf16[128,768]{1,0:T(8,128)(2,1)S(1)} %get-tuple-element.30.h_ref, bf16[128,768]{1,0:T(8,128)(2,1)S(1)} %get-tuple-element.31.own_ref, bf16[128,768]{1,0:T(8,128)(2,1)S(1)} %collective-permute-done.1.peer_ref, ...), custom_call_target="tpu_custom_call" | custom-call | flops 905969664 | bytes 7077888 | tf_op jit(solution)/shard_map/dense_0/pallas_call | solution.py:235
  62.6 2.0 %collective-permute-start.2 = (bf16[128,768]{1,0:T(8,128)(2,1)S(1)}, bf16[128,768]{1,0:T(8,128)(2,1)S(1)}, u32[]{:S(2)}, u32[]{:S(2)}) collective-permute-start(bf16[128,768]{1,0:T(8,128)(2,1)S(1)} %get-tuple-element.33.refs_1_), channel_id=1, source_target_pairs={{0,4},{4,0},{1,5},{5,1},{2,6},{6,2},{3,7},{7,3}} | collective-permute-start | bytes 589832 | tf_op jit(solution)/shard_map/ppermute | solution.py:271
  64.6 0.1 fusion.25
  64.7 2.7 %collective-permute-done.6.peer_ref = bf16[128,768]{1,0:T(8,128)(2,1)S(1)} collective-permute-done((bf16[128,768]{1,0:T(8,128)(2,1)S(1)}, bf16[128,768]{1,0:T(8,128)(2,1)S(1)}, u32[]{:S(2)}, u32[]{:S(2)}) %collective-permute-start.6) | collective-permute-done | bytes 196640 | tf_op jit(solution)/shard_map/ppermute | solution.py:271
  67.5 1.7 copy-done.14
  69.1 1.7 copy-done.16
  70.8 1.7 copy-done.18
  72.5 2.5 %dense_1.1 = (bf16[128,768]{1,0:T(8,128)(2,1)S(1)}, bf16[128,768]{1,0:T(8,128)(2,1)S(1)}) custom-call(bf16[128,768]{1,0:T(8,128)(2,1)S(1)} %get-tuple-element.43.h_ref, bf16[128,768]{1,0:T(8,128)(2,1)S(1)} %get-tuple-element.44.own_ref, bf16[128,768]{1,0:T(8,128)(2,1)S(1)} %collective-permute-done.6.peer_ref, ...), custom_call_target="tpu_custom_call" | custom-call | flops 905969664 | bytes 7077888 | tf_op jit(solution)/shard_map/dense_1/pallas_call | solution.py:235
  75.1 14.2 %self1_0.1 = (bf16[128,768]{1,0:T(8,128)(2,1)S(1)}, bf16[128,768]{1,0:T(8,128)(2,1)S(1)}, bf16[2,6,64,64,256]{4,3,2,1,0:T(8,128)(2,1)}, bf16[2,6,64,64,256]{4,3,2,1,0:T(8,128)(2,1)}) custom-call(bf16[128,768]{1,0:T(8,128)(2,1)S(1)} %get-tuple-element.32.refs_0_, ...), custom_call_target="tpu_custom_call", output_to_operand_aliasing={{2}: (12, {}), {3}: (13, {})} | custom-call | flops 1258291200 | bytes 25165824 | tf_op jit(solution)/shard_map/self1_0/pallas_call | solution.py:131
  89.3 2.0 %collective-permute-start.3 = (bf16[128,768]{1,0:T(8,128)(2,1)S(1)}, bf16[128,768]{1,0:T(8,128)(2,1)S(1)}, u32[]{:S(2)}, u32[]{:S(2)}) collective-permute-start(bf16[128,768]{1,0:T(8,128)(2,1)S(1)} %get-tuple-element.39.own_ref), channel_id=1, source_target_pairs={{0,4},{4,0},{1,5},{5,1},{2,6},{6,2},{3,7},{7,3}} | collective-permute-start | bytes 589832 | tf_op jit(solution)/shard_map/ppermute | solution.py:271
  91.3 14.4 %self1_1.1 = (bf16[128,768]{1,0:T(8,128)(2,1)S(1)}, bf16[128,768]{1,0:T(8,128)(2,1)S(1)}, bf16[2,6,64,64,256]{4,3,2,1,0:T(8,128)(2,1)}, bf16[2,6,64,64,256]{4,3,2,1,0:T(8,128)(2,1)}) custom-call(bf16[128,768]{1,0:T(8,128)(2,1)S(1)} %get-tuple-element.45.refs_0_, ...), custom_call_target="tpu_custom_call", output_to_operand_aliasing={{2}: (12, {}), {3}: (13, {})} | custom-call | flops 1258291200 | bytes 25165824 | tf_op jit(solution)/shard_map/self1_1/pallas_call | solution.py:131
  105.7 4.7 %cross1_0.1 = (bf16[128,768]{1,0:T(8,128)(2,1)S(1)}, bf16[128,768]{1,0:T(8,128)(2,1)S(1)}) custom-call(bf16[128,768]{1,0:T(8,128)(2,1)S(1)} %get-tuple-element.38.h_ref, bf16[128,768]{1,0:T(8,128)(2,1)S(1)} %get-tuple-element.39.own_ref, bf16[128,768]{1,0:T(8,128)(2,1)S(1)} %collective-permute-done.3.peer_ref, s32[32,256]{1,0:T(8,128)S(1)} %bitcast.57, ...), custom_call_target="tpu_custom_call" | custom-call | flops 629145600 | bytes 6291456 | tf_op jit(solution)/shard_map/cross1_0/pallas_call | solution.py:199
  110.5 2.0 %collective-permute-start.4 = (bf16[128,768]{1,0:T(8,128)(2,1)S(1)}, bf16[128,768]{1,0:T(8,128)(2,1)S(1)}, u32[]{:S(2)}, u32[]{:S(2)}) collective-permute-start(bf16[128,768]{1,0:T(8,128)(2,1)S(1)} %get-tuple-element.41), channel_id=1, source_target_pairs={{0,4},{4,0},{1,5},{5,1},{2,6},{6,2},{3,7},{7,3}} | collective-permute-start | bytes 589832 | tf_op jit(solution)/shard_map/ppermute | solution.py:271
  112.6 0.7 slice_reduce_fusion.1
  113.3 0.1 collective-permute-done.8.peer_ref
  113.4 4.7 %cross1_1.1 = (bf16[128,768]{1,0:T(8,128)(2,1)S(1)}, bf16[128,768]{1,0:T(8,128)(2,1)S(1)}) custom-call(bf16[128,768]{1,0:T(8,128)(2,1)S(1)} %get-tuple-element.49.h_ref, bf16[128,768]{1,0:T(8,128)(2,1)S(1)} %get-tuple-element.50.own_ref, bf16[128,768]{1,0:T(8,128)(2,1)S(1)} %collective-permute-done.8.peer_ref, s32[32,256]{1,0:T(8,128)S(1)} %bitcast.58, ...), custom_call_target="tpu_custom_call" | custom-call | flops 629145600 | bytes 6291456 | tf_op jit(solution)/shard_map/cross1_1/pallas_call | solution.py:199
  118.2 5.6 %collective-permute-done.9 = bf16[128,768]{1,0:T(8,128)(2,1)S(1)} collective-permute-done((bf16[128,768]{1,0:T(8,128)(2,1)S(1)}, bf16[128,768]{1,0:T(8,128)(2,1)S(1)}, u32[]{:S(2)}, u32[]{:S(2)}) %collective-permute-start.9) | collective-permute-done | bytes 196640 | tf_op jit(solution)/shard_map/ppermute | solution.py:271
  123.9 0.2 fusion.15
  124.1 0.6 convolution_convert_fusion
  124.7 14.0 %all_to_all.36 = bf16[32,16,768]{2,1,0:T(8,128)(2,1)S(1)} all-to-all(bf16[32,16,768]{2,1,0:T(8,128)(2,1)S(1)} %convolution_convert_fusion), channel_id=1, replica_groups=mesh['dp'=1,'tp'=2,'ep'=4] {'ep'}, dimensions={0} | all-to-all | bytes 1572864 | tf_op jit(solution)/shard_map/all_to_all | solution.py:259
  138.7 1.0 copy.72
  139.6 8.4 %fusion.38 = f32[8,64,1536]{2,1,0:T(8,128)S(1)} fusion(bf16[8,64,768]{2,1,0:T(8,128)(2,1)} %bitcast.11, bf16[8,768,1536]{2,1,0:T(8,128)(2,1)} %param.43), kind=kOutput, calls=%fused_computation.59 | convolution fusion | flops 1207959552 | bytes 22806528 | tf_op jit(solution)/shard_map/ecd,edf->ecf/dot_general | solution.py:260
  148.0 16.4 %fusion.13 = bf16[8,64,768]{2,1,0:T(8,128)(2,1)} fusion(bf16[8,1536,768]{2,1,0:T(8,128)(2,1)} %param.45, bf16[8,64,768]{2,1,0:T(8,128)(2,1)} %bitcast.11, bf16[8,768,1536]{2,1,0:T(8,128)(2,1)} %param.44, f32[8,64,1536]{2,1,0:T(8,128)S(1)} %fusion.38), kind=kOutput, calls=%fused_computation.16 | convolution fusion | flops 2424176640 | bytes 42467328 | tf_op jit(solution)/shard_map/ecf,efd->ecd/dot_general | solution.py:263
  164.4 1.6 copy.73
  166.0 14.0 %all_to_all.37 = bf16[8,64,768]{2,0,1:T(8,128)(2,1)S(1)} all-to-all(bf16[8,64,768]{2,0,1:T(8,128)(2,1)S(1)} %copy.73), channel_id=1, replica_groups=mesh['dp'=1,'tp'=2,'ep'=4] {'ep'}, dimensions={1} | all-to-all | bytes 1572864 | tf_op jit(solution)/shard_map/all_to_all | solution.py:264
  180.0 0.4 fusion.14
  180.5 0.5 copy-done.25
  181.0 0.3 fusion.37
  181.4 9.6 %collective-permute-done.10 = bf16[256,768]{1,0:T(8,128)(2,1)S(1)} collective-permute-done((bf16[256,768]{1,0:T(8,128)(2,1)S(1)}, bf16[256,768]{1,0:T(8,128)(2,1)S(1)}, u32[]{:S(2)}, u32[]{:S(2)}) %collective-permute-start.10) | collective-permute-done | bytes 393248 | tf_op jit(solution)/shard_map/ppermute | solution.py:266
  191.0 0.9 fusion.18
  (73 shorter events, 0.7 us)
Async XLA Ops:
  0.6 179.9 %copy-start = (f32[768,32]{0,1:T(8,128)S(1)}, f32[768,32]{0,1:T(8,128)}, u32[]{:S(2)}) copy-start(f32[768,32]{0,1:T(8,128)} %param.42) | copy-start | bytes 294916
  2.1 1.3 copy-start.5
  3.4 1.3 copy-start.7
  4.6 1.3 copy-start.9
  5.9 1.3 copy-start.11
  7.2 1.0 copy-start.19
  8.2 0.7 copy-start.22
  23.0 19.8 %collective-permute-start = (bf16[128,768]{1,0:T(8,128)(2,1)S(1)}, bf16[128,768]{1,0:T(8,128)(2,1)}, u32[]{:S(2)}, u32[]{:S(2)}) collective-permute-start(bf16[128,768]{1,0:T(8,128)(2,1)S(1)} %get-tuple-element.29.own_ref), channel_id=1, source_target_pairs={{0,4},{4,0},{1,5},{5,1},{2,6},{6,2},{3,7},{7,3}} | collective-permute-start | bytes 589832 | tf_op jit(solution)/shard_map/ppermute | solution.py:271
  26.3 14.3 %copy-start.28 = (s32[256]{0:T(256)S(1)}, s32[256]{0:T(256)}, u32[]{:S(2)}) copy-start(s32[256]{0:T(256)} %param.26) | copy-start | bytes 3076
  26.3 16.5 %copy-start.3 = (bf16[2,768,384]{2,1,0:T(8,128)(2,1)S(1)}, bf16[2,768,384]{2,1,0:T(8,128)(2,1)}, u32[]{:S(2)}) copy-start(bf16[2,768,384]{2,1,0:T(8,128)(2,1)} %wq_ref.7) | copy-start | bytes 3538948
  26.3 16.5 %copy-start.4 = (bf16[2,384,768]{2,1,0:T(8,128)(2,1)S(1)}, bf16[2,384,768]{2,1,0:T(8,128)(2,1)}, u32[]{:S(2)}) copy-start(bf16[2,384,768]{2,1,0:T(8,128)(2,1)} %wo_ref.7) | copy-start | bytes 3538948
  26.3 16.5 %copy-start.20 = (bf16[256,768]{1,0:T(8,128)(2,1)S(1)}, bf16[256,768]{1,0:T(8,128)(2,1)}, u32[]{:S(2)}) copy-start(bf16[256,768]{1,0:T(8,128)(2,1)} %h_ref.3) | copy-start | bytes 1179652
  26.3 16.5 %copy-start.21 = (s32[256,32]{0,1:T(8,128)S(1)}, s32[256,32]{0,1:T(8,128)}, u32[]{:S(2)}) copy-start(s32[256,32]{0,1:T(8,128)} %param.25) | copy-start | bytes 98308
  40.6 14.4 %collective-permute-start.5 = (bf16[128,768]{1,0:T(8,128)(2,1)S(1)}, bf16[128,768]{1,0:T(8,128)(2,1)S(1)}, u32[]{:S(2)}, u32[]{:S(2)}) collective-permute-start(bf16[128,768]{1,0:T(8,128)(2,1)S(1)} %get-tuple-element.42.own_ref), channel_id=1, source_target_pairs={{0,4},{4,0},{1,5},{5,1},{2,6},{6,2},{3,7},{7,3}} | collective-permute-start | bytes 589832 | tf_op jit(solution)/shard_map/ppermute | solution.py:271
  42.8 10.2 %copy-start.29 = (s32[32,3]{0,1:T(4,128)}, s32[32,3]{0,1:T(4,128)S(1)}, u32[]{:S(2)}) copy-start(s32[32,3]{0,1:T(4,128)S(1)} %reduce-window.9) | copy-start | bytes 1156
  42.8 4.6 %copy-start.1 = (bf16[2,256,6,32,64]{1,4,3,2,0:T(8,128)(2,1)S(1)}, bf16[2,256,6,32,64]{1,4,3,2,0:T(8,128)(2,1)}, u32[]{:S(2)}) copy-start(bf16[2,256,6,32,64]{1,4,3,2,0:T(8,128)(2,1)} %param.29) | copy-start | bytes 37748740
  47.4 7.7 %copy-start.2 = (bf16[2,256,6,32,64]{1,4,3,2,0:T(8,128)(2,1)S(1)}, bf16[2,256,6,32,64]{1,4,3,2,0:T(8,128)(2,1)}, u32[]{:S(2)}) copy-start(bf16[2,256,6,32,64]{1,4,3,2,0:T(8,128)(2,1)} %param.29) | copy-start | bytes 37748740
  53.0 7.1 %collective-permute-start.1 = (bf16[128,768]{1,0:T(8,128)(2,1)S(1)}, bf16[128,768]{1,0:T(8,128)(2,1)S(1)}, u32[]{:S(2)}, u32[]{:S(2)}) collective-permute-start(bf16[128,768]{1,0:T(8,128)(2,1)S(1)} %get-tuple-element.31.own_ref), channel_id=1, source_target_pairs={{0,4},{4,0},{1,5},{5,1},{2,6},{6,2},{3,7},{7,3}} | collective-permute-start | bytes 589832 | tf_op jit(solution)/shard_map/ppermute | solution.py:271
  55.0 57.5 %copy-start.26 = (s32[256,32]{0,1:T(8,128)}, s32[256,32]{0,1:T(8,128)S(1)}, u32[]{:S(2)}) copy-start(s32[256,32]{0,1:T(8,128)S(1)} %fusion.26) | copy-start | bytes 98308
  55.0 5.0 %copy-start.13 = (bf16[768,1536]{1,0:T(8,128)(2,1)S(1)}, bf16[768,1536]{1,0:T(8,128)(2,1)}, u32[]{:S(2)}) copy-start(bf16[768,1536]{1,0:T(8,128)(2,1)} %wg_ref.3) | copy-start | bytes 7077892
  55.1 5.0 %copy-start.15 = (bf16[768,1536]{1,0:T(8,128)(2,1)S(1)}, bf16[768,1536]{1,0:T(8,128)(2,1)}, u32[]{:S(2)}) copy-start(bf16[768,1536]{1,0:T(8,128)(2,1)} %wu_ref.3) | copy-start | bytes 7077892
  55.1 5.0 %copy-start.17 = (bf16[1536,768]{1,0:T(8,128)(2,1)S(1)}, bf16[1536,768]{1,0:T(8,128)(2,1)}, u32[]{:S(2)}) copy-start(bf16[1536,768]{1,0:T(8,128)(2,1)} %wd_ref.3) | copy-start | bytes 7077892
  60.0 7.4 %collective-permute-start.6 = (bf16[128,768]{1,0:T(8,128)(2,1)S(1)}, bf16[128,768]{1,0:T(8,128)(2,1)S(1)}, u32[]{:S(2)}, u32[]{:S(2)}) collective-permute-start(bf16[128,768]{1,0:T(8,128)(2,1)S(1)} %get-tuple-element.44.own_ref), channel_id=1, source_target_pairs={{0,4},{4,0},{1,5},{5,1},{2,6},{6,2},{3,7},{7,3}} | collective-permute-start | bytes 589832 | tf_op jit(solution)/shard_map/ppermute | solution.py:271
  60.1 4.5 %slice-start = ((s32[32,3]{0,1:T(4,128)}), s32[32,2]{0,1:T(2,128)S(1)}, s32[]{:S(2)}) async-start(s32[32,3]{0,1:T(4,128)} %copy-done.29), calls=%async_computation.2 | async-start | bytes 2048 | tf_op jit(solution)/shard_map/slice.2
  62.6 12.4 %collective-permute-start.2 = (bf16[128,768]{1,0:T(8,128)(2,1)S(1)}, bf16[128,768]{1,0:T(8,128)(2,1)S(1)}, u32[]{:S(2)}, u32[]{:S(2)}) collective-permute-start(bf16[128,768]{1,0:T(8,128)(2,1)S(1)} %get-tuple-element.33.refs_1_), channel_id=1, source_target_pairs={{0,4},{4,0},{1,5},{5,1},{2,6},{6,2},{3,7},{7,3}} | collective-permute-start | bytes 589832 | tf_op jit(solution)/shard_map/ppermute | solution.py:271
  67.5 1.7 copy-start.14
  69.1 1.7 copy-start.16
  70.8 1.7 copy-start.18
  72.4 2.6 %copy-start.6 = (bf16[2,768,384]{2,1,0:T(8,128)(2,1)S(1)}, bf16[2,768,384]{2,1,0:T(8,128)(2,1)}, u32[]{:S(2)}) copy-start(bf16[2,768,384]{2,1,0:T(8,128)(2,1)} %refs_6_.7) | copy-start | bytes 3538948
  72.5 2.6 %copy-start.8 = (bf16[2,768,384]{2,1,0:T(8,128)(2,1)S(1)}, bf16[2,768,384]{2,1,0:T(8,128)(2,1)}, u32[]{:S(2)}) copy-start(bf16[2,768,384]{2,1,0:T(8,128)(2,1)} %refs_7_.7) | copy-start | bytes 3538948
  72.5 2.6 %copy-start.10 = (bf16[2,768,384]{2,1,0:T(8,128)(2,1)S(1)}, bf16[2,768,384]{2,1,0:T(8,128)(2,1)}, u32[]{:S(2)}) copy-start(bf16[2,768,384]{2,1,0:T(8,128)(2,1)} %refs_8_.3) | copy-start | bytes 3538948
  72.5 2.6 %copy-start.12 = (bf16[2,384,768]{2,1,0:T(8,128)(2,1)S(1)}, bf16[2,384,768]{2,1,0:T(8,128)(2,1)}, u32[]{:S(2)}) copy-start(bf16[2,384,768]{2,1,0:T(8,128)(2,1)} %refs_9_.3) | copy-start | bytes 3538948
  72.5 2.6 %copy-start.23 = (s32[256]{0:T(256)S(1)}, s32[256]{0:T(256)}, u32[]{:S(2)}) copy-start(s32[256]{0:T(256)} %param.24) | copy-start | bytes 3076
  75.0 16.3 %collective-permute-start.7 = (bf16[128,768]{1,0:T(8,128)(2,1)S(1)}, bf16[128,768]{1,0:T(8,128)(2,1)S(1)}, u32[]{:S(2)}, u32[]{:S(2)}) collective-permute-start(bf16[128,768]{1,0:T(8,128)(2,1)S(1)} %get-tuple-element.46.refs_1_), channel_id=1, source_target_pairs={{0,4},{4,0},{1,5},{5,1},{2,6},{6,2},{3,7},{7,3}} | collective-permute-start | bytes 589832 | tf_op jit(solution)/shard_map/ppermute | solution.py:271
  89.3 16.4 %collective-permute-start.3 = (bf16[128,768]{1,0:T(8,128)(2,1)S(1)}, bf16[128,768]{1,0:T(8,128)(2,1)S(1)}, u32[]{:S(2)}, u32[]{:S(2)}) collective-permute-start(bf16[128,768]{1,0:T(8,128)(2,1)S(1)} %get-tuple-element.39.own_ref), channel_id=1, source_target_pairs={{0,4},{4,0},{1,5},{5,1},{2,6},{6,2},{3,7},{7,3}} | collective-permute-start | bytes 589832 | tf_op jit(solution)/shard_map/ppermute | solution.py:271
  105.7 7.7 %collective-permute-start.8 = (bf16[128,768]{1,0:T(8,128)(2,1)S(1)}, bf16[128,768]{1,0:T(8,128)(2,1)S(1)}, u32[]{:S(2)}, u32[]{:S(2)}) collective-permute-start(bf16[128,768]{1,0:T(8,128)(2,1)S(1)} %get-tuple-element.50.own_ref), channel_id=1, source_target_pairs={{0,4},{4,0},{1,5},{5,1},{2,6},{6,2},{3,7},{7,3}} | collective-permute-start | bytes 589832 | tf_op jit(solution)/shard_map/ppermute | solution.py:271
  110.5 7.7 %collective-permute-start.4 = (bf16[128,768]{1,0:T(8,128)(2,1)S(1)}, bf16[128,768]{1,0:T(8,128)(2,1)S(1)}, u32[]{:S(2)}, u32[]{:S(2)}) collective-permute-start(bf16[128,768]{1,0:T(8,128)(2,1)S(1)} %get-tuple-element.41), channel_id=1, source_target_pairs={{0,4},{4,0},{1,5},{5,1},{2,6},{6,2},{3,7},{7,3}} | collective-permute-start | bytes 589832 | tf_op jit(solution)/shard_map/ppermute | solution.py:271
  118.1 5.7 %collective-permute-start.9 = (bf16[128,768]{1,0:T(8,128)(2,1)S(1)}, bf16[128,768]{1,0:T(8,128)(2,1)S(1)}, u32[]{:S(2)}, u32[]{:S(2)}) collective-permute-start(bf16[128,768]{1,0:T(8,128)(2,1)S(1)} %get-tuple-element.52), channel_id=1, source_target_pairs={{0,4},{4,0},{1,5},{5,1},{2,6},{6,2},{3,7},{7,3}} | collective-permute-start | bytes 589832 | tf_op jit(solution)/shard_map/ppermute | solution.py:271
  123.9 15.8 %copy-start.24 = (bf16[128,768]{1,0:T(8,128)(2,1)}, bf16[128,768]{1,0:T(8,128)(2,1)S(1)}, u32[]{:S(2)}) copy-start(bf16[128,768]{1,0:T(8,128)(2,1)S(1)} %add_convert_fusion) | copy-start | bytes 589828
  164.4 15.6 %copy-start.27 = (s32[256,32]{0,1:T(8,128)S(1)}, s32[256,32]{0,1:T(8,128)}, u32[]{:S(2)}) copy-start(s32[256,32]{0,1:T(8,128)} %copy-done.26) | copy-start | bytes 98308
  180.0 0.9 copy-start.25
  180.4 10.5 %collective-permute-start.10 = (bf16[256,768]{1,0:T(8,128)(2,1)S(1)}, bf16[256,768]{1,0:T(8,128)(2,1)S(1)}, u32[]{:S(2)}, u32[]{:S(2)}) collective-permute-start(bf16[256,768]{1,0:T(8,128)(2,1)S(1)} %fusion.14), channel_id=1, source_target_pairs={{0,4},{4,0},{1,5},{5,1},{2,6},{6,2},{3,7},{7,3}} | collective-permute-start | bytes 1179656 | tf_op jit(solution)/shard_map/ppermute | solution.py:266

commit v2 on v0

v2 whole, which is shorter than its diff:
```python
import functools

import jax
import jax.numpy as jnp
from jax import lax
from jax.experimental import pallas as pl
from jax.experimental.pallas import tpu as pltpu
from jax.sharding import PartitionSpec as P

EPS = 1e-6
NEG_BIG = -1e9
F32 = jnp.float32
BF16 = jnp.bfloat16
CHUNKS = 2
VMEM_SPEC = pl.BlockSpec(memory_space=pltpu.VMEM)
HBM_SPEC = pl.BlockSpec(memory_space=pltpu.HBM)
SWAP = [(0, 1), (1, 0)]


def rms_norm(h_cur, scale):
    h_float = h_cur.astype(F32)
    inv_rms = lax.rsqrt(jnp.mean(h_float * h_float, axis=-1, keepdims=True) + EPS)
    return (h_float * inv_rms * scale).astype(BF16)


def project(normed, weight):
    return jnp.dot(normed, weight, preferred_element_type=F32)


def add_parts(h_cur, own, peer):
    total = (own.astype(F32) + peer.astype(F32)).astype(BF16)
    return (h_cur.astype(F32) + total.astype(F32)).astype(BF16)


def softmax_rows(scores):
    top = jnp.max(scores, axis=0, keepdims=True)
    weight = jnp.exp(scores - top)
    return weight / jnp.sum(weight, axis=0, keepdims=True)


def self_kernel(layer, chunk, residual, aliased, *refs):
    refs = list(refs)
    h_ref = refs.pop(0)
    if residual:
        own_ref, peer_ref = refs.pop(0), refs.pop(0)
    pos_hbm, scale_hbm, bias_hbm, wq_hbm, wk_hbm, wv_hbm, wo_hbm, k_hbm, v_hbm = refs[:9]
    refs = refs[9 + 2 * aliased:]
    if residual:
        h_out = refs.pop(0)
    part_ref, ko_hbm, vo_hbm, h_scr, pos_scr, scale_scr, bias_scr, line_scr, wq_scr, wk_scr, wv_scr, wo_scr, kbuf, vbuf, q_t, k_t, v_t, ctx_t, prob, posb, hot, small_sem, w_sem, k_sem, v_sem, ko_sem, vo_sem = refs
    heads, slots, head_dim, tc = kbuf.shape
    lanes = pl.ds(chunk * tc, tc)

    small = [
        pltpu.make_async_copy(pos_hbm.at[:, lanes], pos_scr, small_sem.at[0]),
        pltpu.make_async_copy(scale_hbm.at[0], scale_scr, small_sem.at[1]),
        pltpu.make_async_copy(bias_hbm, bias_scr, small_sem.at[2]),
    ]
    sliced = h_ref.shape[0] != tc
    if sliced:
        small.append(pltpu.make_async_copy(h_ref.at[lanes, :], h_scr, small_sem.at[3]))
    for copy in small:
        copy.start()
    weights = [pltpu.make_async_copy(hbm.at[layer], scr, w_sem.at[i]) for i, (hbm, scr) in enumerate(((wq_hbm, wq_scr), (wk_hbm, wk_scr), (wv_hbm, wv_scr), (wo_hbm, wo_scr)))]
    for copy in weights[:3]:
        copy.start()

    def fetch_k(head):
        return pltpu.make_async_copy(k_hbm.at[layer, head, :, :, lanes], kbuf.at[head], k_sem.at[head])

    def fetch_v(head):
        return pltpu.make_async_copy(v_hbm.at[layer, head, :, :, lanes], vbuf.at[head], v_sem.at[head])

    def store_k(head):
        return pltpu.make_async_copy(kbuf.at[head], ko_hbm.at[layer, head, :, :, lanes], ko_sem.at[head])

    def store_v(head):
        return pltpu.make_async_copy(vbuf.at[head], vo_hbm.at[layer, head, :, :, lanes], vo_sem.at[head])

    for head in range(heads):
        fetch_k(head).start()
        fetch_v(head).start()
    weights[3].start()
    for copy in small:
        copy.wait()
    if residual:
        h_cur = add_parts(h_ref[...], own_ref[...], peer_ref[...])
        h_out[...] = h_cur
    else:
        h_cur = h_scr[...] if sliced else h_ref[...]
    x = rms_norm(h_cur, scale_scr[layer:layer + 1, :])
    pos = pos_scr[...]
    posb[...] = jnp.broadcast_to(pos.astype(F32), posb.shape).astype(BF16)
    hot[...] = (lax.broadcasted_iota(jnp.int32, hot.shape, 0) == pos).astype(F32)
    line_scr[...] = jnp.zeros_like(line_scr)
    line_scr[0:heads, 0:slots] = bias_scr[...]
    weights[0].wait()
    q_t[...] = jnp.transpose(project(x, wq_scr[...])).astype(BF16).astype(F32)
    weights[1].wait()
    k_t[...] = jnp.transpose(project(x, wk_scr[...])).astype(BF16)
    weights[2].wait()
    v_t[...] = jnp.transpose(project(x, wv_scr[...])).astype(BF16)
    posv = posb[...]

    @pl.loop(0, heads)
    def _(head):
        rows = pl.ds(pl.multiple_of(head * head_dim, head_dim), head_dim)
        q = q_t[rows, :]
        k_new = k_t[rows, :]
        fetch_k(head).wait()
        for s8 in range(0, slots, 8):
            out_rows = []
            for s in range(s8, s8 + 8):
                cur = jnp.where(posv == jnp.asarray(s, BF16), k_new, kbuf[head, s])
                kbuf[head, s] = cur
                out_rows.append(jnp.sum(cur.astype(F32) * q, axis=0, keepdims=True))
            prob[s8:s8 + 8, :] = jnp.concatenate(out_rows, axis=0)
        store_k(head).start()
        line = jnp.broadcast_to(line_scr[pl.ds(head, 1), :], (slots, 128))
        table = pltpu.roll(line, 0, 1, stride=1, stride_axis=0)
        bias = jnp.dot(table, hot[...], precision=lax.Precision.HIGHEST, preferred_element_type=F32)
        slot_id = lax.broadcasted_iota(jnp.int32, bias.shape, 0)
        scores = jnp.where(slot_id <= pos_scr[...], prob[...] + bias, NEG_BIG)
        prob[...] = softmax_rows(scores).astype(BF16).astype(F32)
        v_new = v_t[rows, :]
        fetch_v(head).wait()
        acc = jnp.zeros(q.shape, F32)
        for s in range(slots):
            cur = jnp.where(posv == jnp.asarray(s, BF16), v_new, vbuf[head, s])
            vbuf[head, s] = cur
            acc = acc + prob[s:s + 1, :] * cur.astype(F32)
        store_v(head).start()
        ctx_t[rows, :] = acc

    weights[3].wait()
    ctx = jnp.transpose(ctx_t[...]).astype(BF16)
    part_ref[...] = project(ctx, wo_scr[...]).astype(BF16)
    for head in range(heads):
        store_k(head).wait()
        store_v(head).wait()


def self_call(layer, chunk, h_cur, parts, pos, scale, bias, wq, wk, wv, wo, keys, values, outs):
    heads, slots, head_dim, tokens = keys.shape[1:]
    tc = tokens // CHUNKS
    dim, width = wq.shape[1:]
    residual = parts is not None
    aliased = outs is not None
    in_specs = [VMEM_SPEC] * 3 if residual else [VMEM_SPEC if h_cur.shape[0] == tc else HBM_SPEC]
    in_specs += [HBM_SPEC] * 9
    args = [h_cur] + (list(parts) if residual else []) + [pos, scale, bias, wq, wk, wv, wo, keys, values]
    rows = jax.ShapeDtypeStruct((tc, dim), BF16)
    out_shape = [rows] * (1 + residual) + [jax.ShapeDtypeStruct(keys.shape, BF16)] * 2
    out_specs = [VMEM_SPEC] * (1 + residual) + [HBM_SPEC] * 2
    aliases = {}
    if aliased:
        aliases = {len(args): 1 + residual, len(args) + 1: 2 + residual}
        args += list(outs)
        in_specs += [HBM_SPEC] * 2
    size = heads * slots * head_dim * tc
    return pl.pallas_call(
        functools.partial(self_kernel, layer, chunk, residual, aliased),
        in_specs=in_specs,
        out_specs=out_specs,
        out_shape=out_shape,
        input_output_aliases=aliases,
        scratch_shapes=[
            pltpu.VMEM((tc, dim), BF16),
            pltpu.VMEM((1, tc), jnp.int32),
            pltpu.VMEM(scale.shape[1:], F32),
            pltpu.VMEM(bias.shape, F32),
            pltpu.VMEM((8, 128), F32),
            pltpu.VMEM((dim, width), BF16),
            pltpu.VMEM((dim, width), BF16),
            pltpu.VMEM((dim, width), BF16),
            pltpu.VMEM((width, dim), BF16),
            pltpu.VMEM((heads, slots, head_dim, tc), BF16),
            pltpu.VMEM((heads, slots, head_dim, tc), BF16),
            pltpu.VMEM((width, tc), F32),
            pltpu.VMEM((width, tc), BF16),
            pltpu.VMEM((width, tc), BF16),
            pltpu.VMEM((width, tc), F32),
            pltpu.VMEM((slots, tc), F32),
            pltpu.VMEM((head_dim, tc), BF16),
            pltpu.VMEM((128, tc), F32),
            pltpu.SemaphoreType.DMA((4,)),
            pltpu.SemaphoreType.DMA((4,)),
            pltpu.SemaphoreType.DMA((heads,)),
            pltpu.SemaphoreType.DMA((heads,)),
            pltpu.SemaphoreType.DMA((heads,)),
            pltpu.SemaphoreType.DMA((heads,)),
        ],
        compiler_params=pltpu.CompilerParams(vmem_limit_bytes=48 << 20),
        cost_estimate=pl.CostEstimate(flops=size * 400, bytes_accessed=size * 8, transcendentals=0),
        name=f"self{layer}_{chunk}",
    )(*args)


def tp_peer():
    return (lax.axis_index('dp'), 1 - lax.axis_index('tp'), lax.axis_index('ep'))


def remote(src, dst, sems, device):
    return pltpu.make_async_remote_copy(src_ref=src, dst_ref=dst, send_sem=sems[0], recv_sem=sems[1], device_id=device, device_id_type=pl.DeviceIdType.MESH)


def greet(devices):
    barrier = pltpu.get_barrier_semaphore()
    for device in devices:
        pl.semaphore_signal(barrier, inc=1, device_id=device, device_id_type=pl.DeviceIdType.MESH)
    pl.semaphore_wait(barrier, len(devices))


def cross_part(x, keys, values, mask_t, wq, wo, q_t, ctx_t, prob, before_attention, out_ref):
    heads, slots, head_dim, _ = keys.shape
    q_t[...] = jnp.transpose(project(x, wq[...])).astype(BF16).astype(F32)
    before_attention()

    @pl.loop(0, heads)
    def _(head):
        rows = pl.ds(pl.multiple_of(head * head_dim, head_dim), head_dim)
        q = q_t[rows, :]
        for s8 in range(0, slots, 8):
            out_rows = []
            for s in range(s8, s8 + 8):
                out_rows.append(jnp.sum(keys[head, s].astype(F32) * q, axis=0, keepdims=True))
            prob[s8:s8 + 8, :] = jnp.concatenate(out_rows, axis=0)
        scores = jnp.where(mask_t > 0, prob[...], NEG_BIG)
        prob[...] = softmax_rows(scores).astype(BF16).astype(F32)
        acc = jnp.zeros(q.shape, F32)
        for s in range(slots):
            acc = acc + prob[s:s + 1, :] * values[head, s].astype(F32)
        ctx_t[rows, :] = acc

    ctx = jnp.transpose(ctx_t[...]).astype(BF16)
    out_ref[...] = project(ctx, wo[...]).astype(BF16)


def cross_scratch(heads, slots, head_dim, tokens, dim):
    tc = tokens // 2
    width = heads * head_dim
    return dict(
        scale_scr=pltpu.VMEM((3, 2, dim), F32),
        mask_scr=pltpu.VMEM((slots, tokens), jnp.int32),
        wq_scr=pltpu.VMEM((dim, width), BF16),
        wo_scr=pltpu.VMEM((width, dim), BF16),
        kbuf=pltpu.VMEM((2, heads, slots, head_dim, tc), BF16),
        vbuf=pltpu.VMEM((2, heads, slots, head_dim, tc), BF16),
        q_t=pltpu.VMEM((width, tc), F32),
        ctx_t=pltpu.VMEM((width, tc), F32),
        prob=pltpu.VMEM((slots, tc), F32),
        sbuf=pltpu.VMEM((3, tc, dim), BF16),
        rbuf=pltpu.VMEM((4, tc, dim), BF16),
        send_sem=pltpu.SemaphoreType.DMA((4,)),
        recv_sem=pltpu.SemaphoreType.DMA((4,)),
        c_sem=pltpu.SemaphoreType.DMA((8,)),
    )


class Cross:
    def __init__(self, layer, r, t, count):
        self.layer, self.r, self.t = layer, r, t
        tc = t.sbuf.shape[1]
        self.loads = [
            pltpu.make_async_copy(r.scale, t.scale_scr, t.c_sem.at[0]),
            pltpu.make_async_copy(r.mask, t.mask_scr, t.c_sem.at[1]),
            pltpu.make_async_copy(r.wq.at[layer], t.wq_scr, t.c_sem.at[2]),
            pltpu.make_async_copy(r.wo.at[layer], t.wo_scr, t.c_sem.at[3]),
        ]
        self.kv = []
        for c in range(2):
            lanes = pl.ds(c * tc, tc)
            self.kv.append([
                pltpu.make_async_copy(r.keys.at[layer, :, :, :, lanes], t.kbuf.at[c], t.c_sem.at[4 + 2 * c]),
                pltpu.make_async_copy(r.values.at[layer, :, :, :, lanes], t.vbuf.at[c], t.c_sem.at[5 + 2 * c]),
            ])
        peer = tp_peer()
        sources = [r.p_b] + [t.sbuf.at[i] for i in range(3)]
        self.swaps = [remote(sources[i], t.rbuf.at[i], (t.send_sem.at[i], t.recv_sem.at[i]), peer) for i in range(count)]
        self.tc = tc

    def start_loads(self):
        for copy in self.loads + self.kv[0] + self.kv[1]:
            copy.start()

    def run(self):
        t, r = self.t, self.r
        self.swaps[0].start()
        for copy in self.loads:
            copy.wait()
        streams = []
        for c in range(2):
            if c == 0:
                h_cur = add_parts(r.h_a[...], r.p_a[...], r.peer_a[...])
            else:
                self.swaps[0].wait_recv()
                h_cur = add_parts(r.h_b[...], r.p_b[...], t.rbuf[0])
            streams.append(h_cur)
            x = rms_norm(h_cur, t.scale_scr[1, self.layer:self.layer + 1, :])

            def ready():
                for copy in self.kv[c]:
                    copy.wait()

            cross_part(x, t.kbuf.at[c], t.vbuf.at[c], t.mask_scr[:, c * self.tc:(c + 1) * self.tc], t.wq_scr, t.wo_scr, t.q_t, t.ctx_t, t.prob, ready, t.sbuf.at[c])
            self.swaps[1 + c].start()
        return streams


class Refs:
    def __init__(self, names, refs):
        self.__dict__.update(zip(names, refs, strict=True))


CROSS_IN = ('h_a', 'h_b', 'p_a', 'peer_a', 'p_b', 'mask', 'scale', 'wq', 'wo', 'keys', 'values')


def dense_part(x, wg, wu, wd, acc, out_ref, tile=512):
    acc[...] = jnp.zeros_like(acc)

    @pl.loop(0, wg.shape[1] // tile)
    def _(i):
        cols = pl.ds(pl.multiple_of(i * tile, tile), tile)
        product = (jax.nn.gelu(project(x, wg[:, cols])) * project(x, wu[:, cols])).astype(BF16)
        acc[...] += project(product, wd[cols, :])

    out_ref[...] = acc[...].astype(BF16)


def block_a_kernel(names, *refs):
    r = t = Refs(names, refs)
    cross = Cross(0, r, t, 4)
    cross.start_loads()
    dense = [pltpu.make_async_copy(src, dst, t.d_sem.at[i]) for i, (src, dst) in enumerate(((r.wg, t.wg_scr), (r.wu, t.wu_scr), (r.wd, t.wd_scr)))]
    for copy in dense:
        copy.start()
    greet([tp_peer()])
    h_a, h_b = cross.run()
    r.h2_a[...] = h_a
    r.h2_b[...] = h_b
    for copy in dense:
        copy.wait()
    scale = t.scale_scr[2, 0:1, :]
    cross.swaps[1].wait_recv()
    h_a = add_parts(r.h2_a[...], t.sbuf[0], t.rbuf[1])
    r.h2_a[...] = h_a
    dense_part(rms_norm(h_a, scale), t.wg_scr, t.wu_scr, t.wd_scr, t.acc, t.sbuf.at[2])
    cross.swaps[3].start()
    cross.swaps[2].wait_recv()
    h_b = add_parts(r.h2_b[...], t.sbuf[1], t.rbuf[2])
    r.h2_b[...] = h_b
    dense_part(rms_norm(h_b, scale), t.wg_scr, t.wu_scr, t.wd_scr, t.acc, r.pd_b)
    cross.swaps[3].wait_recv()
    r.h2_a[...] = add_parts(r.h2_a[...], t.sbuf[2], t.rbuf[3])
    for copy in cross.swaps:
        copy.wait_send()


def block_a_call(h_a, h_b, p_a, peer_a, p_b, mask, scale, wq, wo, keys, values, wg, wu, wd):
    _, heads, slots, head_dim, tokens = keys.shape
    dim, ff = wg.shape
    tc = tokens // 2
    scratch = cross_scratch(heads, slots, head_dim, tokens, dim)
    scratch.update(
        wg_scr=pltpu.VMEM((dim, ff), BF16),
        wu_scr=pltpu.VMEM((dim, ff), BF16),
        wd_scr=pltpu.VMEM((ff, dim), BF16),
        acc=pltpu.VMEM((tc, dim), F32),
        d_sem=pltpu.SemaphoreType.DMA((3,)),
    )
    names = CROSS_IN + ('wg', 'wu', 'wd', 'h2_a', 'h2_b', 'pd_b') + tuple(scratch)
    rows = jax.ShapeDtypeStruct((tc, dim), BF16)
    return pl.pallas_call(
        functools.partial(block_a_kernel, names),
        in_specs=[VMEM_SPEC] * 5 + [HBM_SPEC] * 9,
        out_specs=[VMEM_SPEC] * 3,
        out_shape=[rows] * 3,
        scratch_shapes=list(scratch.values()),
        compiler_params=pltpu.CompilerParams(vmem_limit_bytes=56 << 20, collective_id=0, has_side_effects=True),
        cost_estimate=pl.CostEstimate(flops=20_000_000_000, bytes_accessed=20 << 20, transcendentals=0),
        name="block_a",
    )(h_a, h_b, p_a, peer_a, p_b, mask, scale, wq, wo, keys, values, wg, wu, wd)


def block_b_kernel(names, *refs):
    r = t = Refs(names, refs)
    dp, tp, me = lax.axis_index('dp'), lax.axis_index('tp'), lax.axis_index('ep')
    group = lax.axis_size('ep')
    local, cap_rows, dim = t.xin.shape
    capacity = cap_rows // group
    tokens = t.x_scr.shape[0]
    ring = t.wg_ring.shape[0]
    tc = tokens // 2
    others = [(dp, tp, lax.rem(me + k, group)) for k in range(1, group)]

    def fetch(i):
        slot = lax.rem(i, ring)
        return [pltpu.make_async_copy(src.at[i], dst.at[slot], t.e_sem.at[n, slot]) for n, (src, dst) in enumerate(((r.wg, t.wg_ring), (r.wu, t.wu_ring), (r.wd, t.wd_ring)))]

    cross = Cross(1, r, t, 3)
    cross.start_loads()
    side = [pltpu.make_async_copy(r.router, t.router_scr, t.s_sem.at[0]), pltpu.make_async_copy(r.idx, t.idx_scr, t.s_sem.at[1])]
    for copy in side:
        copy.start()
    for i in range(ring):
        for copy in fetch(i):
            copy.start()
    greet([tp_peer()] + others)
    h_a, h_b = cross.run()
    t.h_scr[0:tc, :] = h_a
    t.h_scr[tc:, :] = h_b

    for copy in side:
        copy.wait()
    lane_idx = jnp.broadcast_to(t.idx_scr[...].astype(F32), (tokens, tokens))
    row_idx = jnp.transpose(lane_idx)
    same = lane_idx == row_idx
    row_no = lax.broadcasted_iota(jnp.int32, same.shape, 0)
    lane_no = lax.broadcasted_iota(jnp.int32, same.shape, 1)
    lane_slot = jnp.sum(jnp.where(same & (row_no < lane_no), 1.0, 0.0), axis=0, keepdims=True)
    row_slot = jnp.sum(jnp.where(same & (lane_no < row_no), 1.0, 0.0), axis=1, keepdims=True)
    total = group * local * capacity
    lane_dest = jnp.where(lane_slot < capacity, lane_idx[0:1, :] * capacity + lane_slot, -1.0)
    row_dest = jnp.where(row_slot < capacity, row_idx[:, 0:1] * capacity + row_slot, -1.0)
    t.pick[...] = (lax.broadcasted_iota(jnp.int32, (total, tokens), 0).astype(F32) == lane_dest).astype(BF16)
    t.place[...] = (lax.broadcasted_iota(jnp.int32, (tokens, total), 1).astype(F32) == row_dest).astype(BF16)
    expert_hot = lax.broadcasted_iota(jnp.int32, (tokens, group * local), 1).astype(F32) == row_idx[:, 0:1]

    for c in range(2):
        rows = slice(c * tc, (c + 1) * tc)
        cross.swaps[1 + c].wait_recv()
        h_cur = add_parts(t.h_scr[rows, :], t.sbuf[c], t.rbuf[1 + c])
        t.h_scr[rows, :] = h_cur
        t.x_scr[rows, :] = rms_norm(h_cur, t.scale_scr[2, 1:2, :])
    t.disp[...] = project(t.pick[...], t.x_scr[...]).astype(BF16)

    def span(owner, i):
        return pl.ds(pl.multiple_of((owner * local + i) * capacity, capacity), capacity)

    def mine(owner):
        return pl.ds(pl.multiple_of(owner * capacity, capacity), capacity)

    def send_rows(i, k):
        dst = lax.rem(me + k, group)
        return remote(t.disp.at[span(dst, i), :], t.xin.at[i, mine(me), :], (t.ds_sem.at[k - 1, i], t.dr_sem.at[k - 1, i]), (dp, tp, dst))

    def send_back(i, k):
        dst = lax.rem(me + k, group)
        return remote(t.yout.at[i, mine(dst), :], t.ret.at[span(me, i), :], (t.bs_sem.at[k - 1, i], t.br_sem.at[k - 1, i]), (dp, tp, dst))

    @pl.loop(0, local)
    def _(i):
        for k in range(1, group):
            send_rows(i, k).start()
        t.xin[i, mine(me), :] = t.disp[span(me, i), :]

    logits = jnp.dot(t.x_scr[...].astype(F32), t.router_scr[...].T, precision=lax.Precision.HIGHEST, preferred_element_type=F32)
    top = jnp.max(logits, axis=-1, keepdims=True)
    weight = jnp.exp(logits - top)
    weight = weight / jnp.sum(weight, axis=-1, keepdims=True)
    t.gate[...] = jnp.broadcast_to(jnp.sum(jnp.where(expert_hot, weight, 0.0), axis=-1, keepdims=True), t.gate.shape)

    @pl.loop(0, local)
    def _(i):
        slot = lax.rem(i, ring)
        for k in range(1, group):
            send_rows(i, k).wait_recv()
        copies = fetch(i)
        x = t.xin[i]
        copies[0].wait()
        gate_in = jax.nn.gelu(project(x, t.wg_ring[slot]))
        copies[1].wait()
        product = (gate_in * project(x, t.wu_ring[slot])).astype(BF16)
        copies[2].wait()
        t.yout[i] = project(product, t.wd_ring[slot]).astype(BF16)
        for k in range(1, group):
            send_back(i, k).start()
        t.ret[span(me, i), :] = t.yout[i, mine(me), :]

        @pl.when(i + ring < local)
        def _():
            for copy in fetch(i + ring):
                copy.start()

    @pl.loop(0, local)
    def _(i):
        for k in range(1, group):
            send_back(i, k).wait_recv()

    pieces = t.comb.shape[0]
    size = tokens // pieces
    last = [remote(t.comb.at[p], t.comb_peer.at[p], (t.fs_sem.at[p], t.fr_sem.at[p]), tp_peer()) for p in range(pieces)]
    for p in range(pieces):
        t.comb[p] = project(t.place[p * size:(p + 1) * size, :], t.ret[...]).astype(BF16)
        last[p].start()
    for p in range(pieces):
        rows = slice(p * size, (p + 1) * size)
        last[p].wait_recv()
        both = (t.comb[p].astype(F32) + t.comb_peer[p].astype(F32))
        gate = t.gate[rows, 0:1]
        r.out[rows, :] = (t.h_scr[rows, :].astype(F32) + gate * both).astype(BF16)
    for copy in cross.swaps + last:
        copy.wait_send()

    @pl.loop(0, local)
    def _(i):
        for k in range(1, group):
            send_rows(i, k).wait_send()
            send_back(i, k).wait_send()


def block_b_call(h_a, h_b, p_a, peer_a, p_b, mask, scale, wq, wo, keys, values, router, idx, wg, wu, wd, group):
    _, heads, slots, head_dim, tokens = keys.shape
    local, dim, ff = wg.shape
    experts = router.shape[0]
    capacity = (2 * tokens + experts - 1) // experts
    ring = 5
    pieces = 4
    scratch = cross_scratch(heads, slots, head_dim, tokens, dim)
    hops = (group - 1, local)
    scratch.update(
        wg_ring=pltpu.VMEM((ring, dim, ff), BF16),
        wu_ring=pltpu.VMEM((ring, dim, ff), BF16),
        wd_ring=pltpu.VMEM((ring, ff, dim), BF16),
        router_scr=pltpu.VMEM(router.shape, F32),
        idx_scr=pltpu.VMEM((1, tokens), jnp.int32),
        h_scr=pltpu.VMEM((tokens, dim), BF16),
        x_scr=pltpu.VMEM((tokens, dim), BF16),
        pick=pltpu.VMEM((experts * capacity, tokens), BF16),
        place=pltpu.VMEM((tokens, experts * capacity), BF16),
        gate=pltpu.VMEM((tokens, 128), F32),
        disp=pltpu.VMEM((experts * capacity, dim), BF16),
        xin=pltpu.VMEM((local, group * capacity, dim), BF16),
        yout=pltpu.VMEM((local, group * capacity, dim), BF16),
        ret=pltpu.VMEM((experts * capacity, dim), BF16),
        comb=pltpu.VMEM((pieces, tokens // pieces, dim), BF16),
        comb_peer=pltpu.VMEM((pieces, tokens // pieces, dim), BF16),
        e_sem=pltpu.SemaphoreType.DMA((3, ring)),
        s_sem=pltpu.SemaphoreType.DMA((2,)),
        ds_sem=pltpu.SemaphoreType.DMA(hops),
        dr_sem=pltpu.SemaphoreType.DMA(hops),
        bs_sem=pltpu.SemaphoreType.DMA(hops),
        br_sem=pltpu.SemaphoreType.DMA(hops),
        fs_sem=pltpu.SemaphoreType.DMA((pieces,)),
        fr_sem=pltpu.SemaphoreType.DMA((pieces,)),
    )
    names = CROSS_IN + ('router', 'idx', 'wg', 'wu', 'wd', 'out') + tuple(scratch)
    return pl.pallas_call(
        functools.partial(block_b_kernel, names),
        in_specs=[VMEM_SPEC] * 5 + [HBM_SPEC] * 11,
        out_specs=VMEM_SPEC,
        out_shape=jax.ShapeDtypeStruct((tokens, dim), BF16),
        scratch_shapes=list(scratch.values()),
        compiler_params=pltpu.CompilerParams(vmem_limit_bytes=63 << 20, collective_id=1, has_side_effects=True),
        cost_estimate=pl.CostEstimate(flops=40_000_000_000, bytes_accessed=70 << 20, transcendentals=0),
        name="block_b",
    )(h_a, h_b, p_a, peer_a, p_b, mask, scale, wq, wo, keys, values, router, idx, wg, wu, wd)


def swap(part):
    return part, lax.ppermute(part, 'tp', SWAP)


def decode_body(hidden, write_pos, enc_mask, expert_idx, self_keys, self_values, cross_keys, cross_values, rel_bias, norm_scale, w_query, w_key, w_value, w_out, w_cross_query, w_cross_out, dense_gate, dense_up, dense_down, router, exp_gate, exp_up, exp_down):
    order = (0, 2, 3, 4, 1)
    keys, values = jnp.transpose(self_keys, order), jnp.transpose(self_values, order)
    ckeys, cvalues = jnp.transpose(cross_keys, order), jnp.transpose(cross_values, order)
    pos = write_pos.reshape(1, -1)
    mask = enc_mask.T
    scale = jnp.transpose(norm_scale, (1, 0, 2))
    shared = (pos, scale, rel_bias, w_query, w_key, w_value, w_out, keys, values)
    cross = (mask, scale, w_cross_query, w_cross_out, ckeys, cvalues)
    p_a, *outs = self_call(0, 0, hidden, None, *shared, None)
    pair_a = swap(p_a)
    p_b, *outs = self_call(0, 1, hidden, None, *shared, outs)
    h_a, h_b = hidden[:hidden.shape[0] // 2], hidden[hidden.shape[0] // 2:]
    h_a, h_b, pd_b = block_a_call(h_a, h_b, *pair_a, p_b, *cross, dense_gate, dense_up, dense_down)
    pair_b = swap(pd_b)
    p_a, *outs = self_call(1, 0, h_a, None, *shared, outs)
    pair_a = swap(p_a)
    h_b, p_b, *outs = self_call(1, 1, h_b, pair_b, *shared, outs)
    h_all = block_b_call(h_a, h_b, *pair_a, p_b, *cross, router.T, expert_idx.reshape(1, -1), exp_gate, exp_up, exp_down, lax.axis_size('ep'))
    back = (0, 4, 1, 2, 3)
    return h_all, jnp.transpose(outs[0], back), jnp.transpose(outs[1], back)


def solution(mesh):
    batch = ('dp', 'ep')
    row_spec = P(batch, None)
    vec_spec = P(batch)
    cache_spec = P(None, batch, 'tp', None, None)
    col_spec = P(None, None, 'tp')
    out_rows = P(None, 'tp', None)
    in_specs = (row_spec, vec_spec, row_spec, vec_spec, cache_spec, cache_spec, cache_spec, cache_spec, P('tp', None), P(), col_spec, col_spec, col_spec, out_rows, col_spec, out_rows, P(None, 'tp'), P(None, 'tp'), P('tp', None), P(), P('ep', None, 'tp'), P('ep', None, 'tp'), P('ep', 'tp', None))
    out_specs = (row_spec, cache_spec, cache_spec)
    return jax.shard_map(decode_body, mesh=mesh, in_specs=in_specs, out_specs=out_specs, check_vma=False)
```

time: 461 us -> 140 us (0.30); the launches traced: 453 us -> 139 us
  other arithmetic: 169 us -> 0 us
  Pallas kernels: 0 us -> 119 us
  waiting for transfers between devices: 99.1 us -> 0.01 us
  local copies, waits for them, and re-layouts: 91.6 us -> 14.4 us
  matrix products: 59.3 us -> 0 us
  blocking collectives: 14.4 us -> 0 us
  between operations: 15 us -> 0.82 us
    pallas_call x0 -> x6, Pallas kernels: none -> 119 us  [the longest x1 57.4 us: block_b_call(): pl.pallas_call(functools.partial(block_b_kernel, names), in_specs=[VMEM_S...]
    psum x6 -> x0, waiting for transfers between devices: 99 us -> none  [the longest x2 40.8 us: decode_body(): h_cur = add_residual(h_cur, lax.psum(attn_part.astype(jnp.bfloat16), 'tp'))]
    dot_general x19 -> x0, matrix products: 59.3 us -> none  [the longest x14 27.3 us: project(): return jnp.dot(normed, weight, preferred_element_type=jnp.float32)]
    gather x1 -> x0, local copies, waits for them, and re-layouts: 54.9 us -> none  [self_attention(): bias = jnp.take(rel_bias, jnp.maximum(distance, 0), axis=1)]
    dot_general x6 -> x0, other arithmetic: 37.7 us -> none  [the longest x2 18.1 us: self_attention(): jnp.einsum('thl,thld->thd', attn_prob, values, preferred_element_type=jnp...]
    another operation x3 -> x0, other arithmetic: 33.8 us -> none  [the longest x1 33.2 us: decode_body(): return (h_cur, jnp.stack(keys_list), jnp.stack(values_list))]
    select_n x1 -> x0, other arithmetic: 33.3 us -> none  [self_attention(): values = jnp.where(at_slot, value_new[:, :, None, :], values)]
    div x4 -> x0, other arithmetic: 27.4 us -> none  [the longest x2 25.7 us: self_attention(): attn_prob = jax.nn.softmax(scores, axis=-1).astype(jnp.bfloat16)]
  transfers between devices with their start and end apart: 7 -> 3, of which waited for: 5 -> 0; matrix products, arithmetic and copies ran while one was open for 16% -> 1% of each run, Pallas kernels for 0% -> 21%
where the time goes in v2:
time: 140 us; the launch traced here: 139 us
  Pallas kernels  119 us (85%)
  local copies, waits for them, and re-layouts  14.4 us (10%)
  starting transfers between devices  5.46 us (4%)
    pallas_call x1, Pallas kernels, block_b_call(): pl.pallas_call(functools.partial(block_b_kernel, names), in_specs=[VMEM_S...  57.4 us
    pallas_call x4, Pallas kernels, self_call(): pl.pallas_call(functools.partial(self_kernel, layer, chunk, residual, ali...  39.7 us
    pallas_call x1, Pallas kernels, block_a_call(): pl.pallas_call(functools.partial(block_a_kernel, names), in_specs=[VMEM_S...  21.6 us
    unnamed x51, local copies, waits for them, and re-layouts  13.6 us
    ppermute x3, starting transfers between devices, swap(): return (part, lax.ppermute(part, 'tp', SWAP))  5.46 us
  transfers between devices with their start and end apart: 3, of which 0 were waited for; matrix products, arithmetic and copies ran while one was open for 1% of the time, Pallas kernels for 21%

profile of v2, /device:TPU:0, one launch (start us, length us, event | category | flops | bytes accessed | tf_op | source)
XLA Modules:
  0.0 139.3 jit_solution(11797540866333864100)
XLA Ops:
  0.6 0.0 copy-start
  0.6 1.3 copy-done
  1.9 1.3 copy-done.2
  3.2 1.3 copy-done.4
  4.4 1.3 copy-done.6
  5.7 1.0 copy-done.8
  6.7 0.7 copy-done.9
  7.4 0.7 copy-done.14
  8.1 0.7 copy-done.16
  8.8 10.0 %self0_0.1 = (bf16[128,768]{1,0:T(8,128)(2,1)S(1)}, bf16[2,6,64,64,256]{4,3,2,1,0:T(8,128)(2,1)}, bf16[2,6,64,64,256]{4,3,2,1,0:T(8,128)(2,1)}) custom-call(bf16[256,768]{1,0:T(8,128)(2,1)S(1)} %copy-done.8, s32[1,256]{1,0:T(1,128)S(1)} %bitcast.17, f32[3,2,768]{2,1,0:T(2,128)S(1)} %bitcast.13, f32[6,64]{1,0:T(8,128)S(1)} %copy-done.14, ...), custom_call_target="tpu_custom_call" | custom-call | flops 1258291200 | bytes 25165824 | tf_op jit(solution)/shard_map/self0_0/pallas_call | solution.py:161
  18.8 0.0 copy-start.19
  18.9 3.4 %collective-permute-start = (bf16[128,768]{1,0:T(8,128)(2,1)S(1)}, bf16[128,768]{1,0:T(8,128)(2,1)S(1)}, u32[]{:S(2)}, u32[]{:S(2)}) collective-permute-start(bf16[128,768]{1,0:T(8,128)(2,1)S(1)} %get-tuple-element.19.refs_2_), channel_id=1, source_target_pairs={{0,4},{4,0},{1,5},{5,1},{2,6},{6,2},{3,7},{7,3}} | collective-permute-start | bytes 589832 | tf_op jit(solution)/shard_map/ppermute | solution.py:561
  22.2 10.0 %self0_1.1 = (bf16[128,768]{1,0:T(8,128)(2,1)S(1)}, bf16[2,6,64,64,256]{4,3,2,1,0:T(8,128)(2,1)}, bf16[2,6,64,64,256]{4,3,2,1,0:T(8,128)(2,1)}) custom-call(bf16[256,768]{1,0:T(8,128)(2,1)S(1)} %copy-done.8, s32[1,256]{1,0:T(1,128)S(1)} %bitcast.18, f32[3,2,768]{2,1,0:T(2,128)S(1)} %bitcast.14, ...), custom_call_target="tpu_custom_call", output_to_operand_aliasing={{1}: (10, {}), {2}: (11, {})} | custom-call | flops 1258291200 | bytes 25165824 | tf_op jit(solution)/shard_map/self0_1/pallas_call | solution.py:161
  32.3 0.0 copy-done.19
  32.3 0.0 copy-start.20
  32.3 0.8 fusion
  33.1 0.0 collective-permute-done.refs_3_
  33.1 0.0 copy-done.20
  33.1 0.7 copy-done.24
  33.8 0.0 copy-start.10
  33.8 0.0 copy-start.15
  33.8 0.0 copy-start.17
  33.8 21.6 %block_a.1 = (bf16[128,768]{1,0:T(8,128)(2,1)}, bf16[128,768]{1,0:T(8,128)(2,1)}, bf16[128,768]{1,0:T(8,128)(2,1)}) custom-call(bf16[128,768]{1,0:T(8,128)(2,1)} %get-tuple-element.36.refs_0_, bf16[128,768]{1,0:T(8,128)(2,1)} %get-tuple-element.35.refs_1_, bf16[128,768]{1,0:T(8,128)(2,1)} %copy-done.19, bf16[128,768]{1,0:T(8,128)(2,1)} %copy-done.24, ...), custom_call_target="tpu_custom_call" | custom-call | flops 20000000000 | bytes 20971520 | tf_op jit(solution)/shard_map/block_a/pallas_call | solution.py:373
  55.4 1.6 %collective-permute-start.1 = (bf16[128,768]{1,0:T(8,128)(2,1)}, bf16[128,768]{1,0:T(8,128)(2,1)S(1)}, u32[]{:S(2)}, u32[]{:S(2)}) collective-permute-start(bf16[128,768]{1,0:T(8,128)(2,1)} %get-tuple-element.25.refs_1_), channel_id=1, source_target_pairs={{0,4},{4,0},{1,5},{5,1},{2,6},{6,2},{3,7},{7,3}} | collective-permute-start | bytes 589832 | tf_op jit(solution)/shard_map/ppermute | solution.py:561
  57.0 0.0 copy-done.1
  57.0 0.0 copy-done.3
  57.0 0.0 copy-done.5
  57.0 0.0 copy-done.7
  57.0 0.0 copy-done.10
  57.0 0.0 copy-done.15
  57.0 0.0 copy-done.17
  57.0 0.0 copy-start.11
  57.0 0.9 copy-done.11
  57.9 9.8 %self1_0.1 = (bf16[128,768]{1,0:T(8,128)(2,1)S(1)}, bf16[2,6,64,64,256]{4,3,2,1,0:T(8,128)(2,1)}, bf16[2,6,64,64,256]{4,3,2,1,0:T(8,128)(2,1)}) custom-call(bf16[128,768]{1,0:T(8,128)(2,1)S(1)} %copy-done.11, s32[1,256]{1,0:T(1,128)S(1)} %bitcast.19, f32[3,2,768]{2,1,0:T(2,128)S(1)} %bitcast.15, ...), custom_call_target="tpu_custom_call", output_to_operand_aliasing={{1}: (10, {}), {2}: (11, {})} | custom-call | flops 1258291200 | bytes 25165824 | tf_op jit(solution)/shard_map/self1_0/pallas_call | solution.py:161
  67.7 0.0 copy-start.18
  67.8 0.5 collective-permute-start.2
  68.2 0.0 collective-permute-done.1.refs_2_
  68.3 0.0 copy-done.12
  68.3 0.0 copy-done.13
  68.3 9.8 %self1_1.1 = (bf16[128,768]{1,0:T(8,128)(2,1)S(1)}, bf16[128,768]{1,0:T(8,128)(2,1)S(1)}, bf16[2,6,64,64,256]{4,3,2,1,0:T(8,128)(2,1)}, bf16[2,6,64,64,256]{4,3,2,1,0:T(8,128)(2,1)}) custom-call(bf16[128,768]{1,0:T(8,128)(2,1)S(1)} %copy-done.12, bf16[128,768]{1,0:T(8,128)(2,1)S(1)} %copy-done.13, ...), custom_call_target="tpu_custom_call", output_to_operand_aliasing={{2}: (12, {}), {3}: (13, {})} | custom-call | flops 1258291200 | bytes 25165824 | tf_op jit(solution)/shard_map/self1_1/pallas_call | solution.py:161
  78.1 0.0 copy-done.18
  78.1 0.0 copy-start.21
  78.1 0.7 copy-done.21
  78.8 0.7 copy-done.22
  79.5 0.0 collective-permute-done.2.refs_3_
  79.5 0.7 copy-done.23
  80.2 57.4 %block_b.1 = bf16[256,768]{1,0:T(8,128)(2,1)} custom-call(bf16[128,768]{1,0:T(8,128)(2,1)} %get-tuple-element.23.refs_0_, bf16[128,768]{1,0:T(8,128)(2,1)} %copy-done.21, bf16[128,768]{1,0:T(8,128)(2,1)} %copy-done.18, bf16[128,768]{1,0:T(8,128)(2,1)} %copy-done.23, bf16[128,768]{1,0:T(8,128)(2,1)} %copy-done.22, s32[32,256]{1,0:T(8,128)} %bitcast.37, ...), custom_call_target="tpu_custom_call" | custom-call | flops 40000000000 | bytes 73400320 | tf_op jit(solution)/shard_map/block_b/pallas_call | solution.py:548
  137.5 1.8 %copy.39 = bf16[256,768]{1,0:T(8,128)(2,1)} copy(bf16[256,768]{1,0:T(8,128)(2,1)} %block_b.1) | data formatting | bytes 786432
  (16 shorter events, 0.0 us)
Async XLA Ops:
  0.6 1.3 copy-start
  1.9 1.3 copy-start.2
  3.2 1.3 copy-start.4
  4.4 1.3 copy-start.6
  5.7 1.0 copy-start.8
  6.7 0.7 copy-start.9
  7.4 0.7 copy-start.14
  8.1 0.7 copy-start.16
  18.8 13.4 %copy-start.19 = (bf16[128,768]{1,0:T(8,128)(2,1)}, bf16[128,768]{1,0:T(8,128)(2,1)S(1)}, u32[]{:S(2)}) copy-start(bf16[128,768]{1,0:T(8,128)(2,1)S(1)} %get-tuple-element.19.refs_2_) | copy-start | bytes 589828
  18.9 14.3 %collective-permute-start = (bf16[128,768]{1,0:T(8,128)(2,1)S(1)}, bf16[128,768]{1,0:T(8,128)(2,1)S(1)}, u32[]{:S(2)}, u32[]{:S(2)}) collective-permute-start(bf16[128,768]{1,0:T(8,128)(2,1)S(1)} %get-tuple-element.19.refs_2_), channel_id=1, source_target_pairs={{0,4},{4,0},{1,5},{5,1},{2,6},{6,2},{3,7},{7,3}} | collective-permute-start | bytes 589832 | tf_op jit(solution)/shard_map/ppermute | solution.py:561
  32.3 0.8 copy-start.20
  33.1 0.7 copy-start.24
  33.8 23.2 %copy-start.1 = (bf16[2,768,384]{2,1,0:T(8,128)(2,1)S(1)}, bf16[2,768,384]{2,1,0:T(8,128)(2,1)}, u32[]{:S(2)}) copy-start(bf16[2,768,384]{2,1,0:T(8,128)(2,1)} %refs_6_.7) | copy-start | bytes 3538948
  33.8 23.2 %copy-start.3 = (bf16[2,768,384]{2,1,0:T(8,128)(2,1)S(1)}, bf16[2,768,384]{2,1,0:T(8,128)(2,1)}, u32[]{:S(2)}) copy-start(bf16[2,768,384]{2,1,0:T(8,128)(2,1)} %refs_7_.10) | copy-start | bytes 3538948
  33.8 23.2 %copy-start.5 = (bf16[2,768,384]{2,1,0:T(8,128)(2,1)S(1)}, bf16[2,768,384]{2,1,0:T(8,128)(2,1)}, u32[]{:S(2)}) copy-start(bf16[2,768,384]{2,1,0:T(8,128)(2,1)} %refs_8_.4) | copy-start | bytes 3538948
  33.8 23.2 %copy-start.7 = (bf16[2,384,768]{2,1,0:T(8,128)(2,1)S(1)}, bf16[2,384,768]{2,1,0:T(8,128)(2,1)}, u32[]{:S(2)}) copy-start(bf16[2,384,768]{2,1,0:T(8,128)(2,1)} %refs_9_.1) | copy-start | bytes 3538948
  33.8 23.2 %copy-start.10 = (f32[2,3,768]{2,0,1:T(2,128)S(1)}, f32[2,3,768]{2,0,1:T(2,128)}, u32[]{:S(2)}) copy-start(f32[2,3,768]{2,0,1:T(2,128)} %param.32) | copy-start | bytes 55300
  33.8 23.2 %copy-start.15 = (f32[6,64]{1,0:T(8,128)S(1)}, f32[6,64]{1,0:T(8,128)}, u32[]{:S(2)}) copy-start(f32[6,64]{1,0:T(8,128)} %refs_5_.7) | copy-start | bytes 4612
  33.8 23.2 %copy-start.17 = (s32[256]{0:T(256)S(1)}, s32[256]{0:T(256)}, u32[]{:S(2)}) copy-start(s32[256]{0:T(256)} %param.24) | copy-start | bytes 3076
  55.4 12.9 %collective-permute-start.1 = (bf16[128,768]{1,0:T(8,128)(2,1)}, bf16[128,768]{1,0:T(8,128)(2,1)S(1)}, u32[]{:S(2)}, u32[]{:S(2)}) collective-permute-start(bf16[128,768]{1,0:T(8,128)(2,1)} %get-tuple-element.25.refs_1_), channel_id=1, source_target_pairs={{0,4},{4,0},{1,5},{5,1},{2,6},{6,2},{3,7},{7,3}} | collective-permute-start | bytes 589832 | tf_op jit(solution)/shard_map/ppermute | solution.py:561
  57.0 0.9 copy-start.11
  57.9 10.3 %copy-start.12 = (bf16[128,768]{1,0:T(8,128)(2,1)S(1)}, bf16[128,768]{1,0:T(8,128)(2,1)}, u32[]{:S(2)}) copy-start(bf16[128,768]{1,0:T(8,128)(2,1)} %get-tuple-element.24.refs_0_) | copy-start | bytes 589828
  57.9 10.3 %copy-start.13 = (bf16[128,768]{1,0:T(8,128)(2,1)S(1)}, bf16[128,768]{1,0:T(8,128)(2,1)}, u32[]{:S(2)}) copy-start(bf16[128,768]{1,0:T(8,128)(2,1)} %get-tuple-element.25.refs_1_) | copy-start | bytes 589828
  67.7 10.4 %copy-start.18 = (bf16[128,768]{1,0:T(8,128)(2,1)}, bf16[128,768]{1,0:T(8,128)(2,1)S(1)}, u32[]{:S(2)}) copy-start(bf16[128,768]{1,0:T(8,128)(2,1)S(1)} %get-tuple-element.31.refs_2_) | copy-start | bytes 589828
  67.8 11.7 %collective-permute-start.2 = (bf16[128,768]{1,0:T(8,128)(2,1)S(1)}, bf16[128,768]{1,0:T(8,128)(2,1)S(1)}, u32[]{:S(2)}, u32[]{:S(2)}) collective-permute-start(bf16[128,768]{1,0:T(8,128)(2,1)S(1)} %get-tuple-element.31.refs_2_), channel_id=1, source_target_pairs={{0,4},{4,0},{1,5},{5,1},{2,6},{6,2},{3,7},{7,3}} | collective-permute-start | bytes 589832 | tf_op jit(solution)/shard_map/ppermute | solution.py:561
  78.1 0.7 copy-start.21
  78.8 0.7 copy-start.22
  79.5 0.7 copy-start.23

commit v3 on v2

--- a/solution.py
+++ b/solution.py
@@ -77,10 +77,8 @@
     def store_v(head):
         return pltpu.make_async_copy(vbuf.at[head], vo_hbm.at[layer, head, :, :, lanes], vo_sem.at[head])
 
-    for head in range(heads):
-        fetch_k(head).start()
-        fetch_v(head).start()
-    weights[3].start()
+    fetch_k(0).start()
+    fetch_v(0).start()
     for copy in small:
         copy.wait()
     if residual:
@@ -94,11 +92,14 @@
     hot[...] = (lax.broadcasted_iota(jnp.int32, hot.shape, 0) == pos).astype(F32)
     line_scr[...] = jnp.zeros_like(line_scr)
     line_scr[0:heads, 0:slots] = bias_scr[...]
-    weights[0].wait()
+    for copy in weights[:3]:
+        copy.wait()
+    for head in range(1, heads):
+        fetch_k(head).start()
+        fetch_v(head).start()
+    weights[3].start()
     q_t[...] = jnp.transpose(project(x, wq_scr[...])).astype(BF16).astype(F32)
-    weights[1].wait()
     k_t[...] = jnp.transpose(project(x, wk_scr[...])).astype(BF16)
-    weights[2].wait()
     v_t[...] = jnp.transpose(project(x, wv_scr[...])).astype(BF16)
     posv = posb[...]
 
@@ -280,14 +281,16 @@
         self.tc = tc
 
     def start_loads(self):
-        for copy in self.loads + self.kv[0] + self.kv[1]:
+        for copy in self.loads[:4] + self.kv[0]:
             copy.start()
 
-    def run(self):
+    def run(self, later):
         t, r = self.t, self.r
         self.swaps[0].start()
         for copy in self.loads:
             copy.wait()
+        for copy in self.kv[1]:
+            copy.start()
         streams = []
         for c in range(2):
             if c == 0:
@@ -301,6 +304,9 @@
             def ready():
                 for copy in self.kv[c]:
                     copy.wait()
+                if c == 0:
+                    for copy in later:
+                        copy.start()
 
             cross_part(x, t.kbuf.at[c], t.vbuf.at[c], t.mask_scr[:, c * self.tc:(c + 1) * self.tc], t.wq_scr, t.wo_scr, t.q_t, t.ctx_t, t.prob, ready, t.sbuf.at[c])
             self.swaps[1 + c].start()
@@ -329,13 +335,16 @@
 
 def block_a_kernel(names, *refs):
     r = t = Refs(names, refs)
+    stream = pltpu.make_async_copy(r.hidden, t.h_scr, t.d_sem.at[3])
+    stream.start()
+    tc = t.acc.shape[0]
+    r.h_a, r.h_b = t.h_scr.at[0:tc, :], t.h_scr.at[tc:, :]
     cross = Cross(0, r, t, 4)
+    cross.loads.append(stream)
     cross.start_loads()
     dense = [pltpu.make_async_copy(src, dst, t.d_sem.at[i]) for i, (src, dst) in enumerate(((r.wg, t.wg_scr), (r.wu, t.wu_scr), (r.wd, t.wd_scr)))]
-    for copy in dense:
-        copy.start()
     greet([tp_peer()])
-    h_a, h_b = cross.run()
+    h_a, h_b = cross.run(dense)
     r.h2_a[...] = h_a
     r.h2_b[...] = h_b
     for copy in dense:
@@ -356,7 +365,7 @@
         copy.wait_send()
 
 
-def block_a_call(h_a, h_b, p_a, peer_a, p_b, mask, scale, wq, wo, keys, values, wg, wu, wd):
+def block_a_call(hidden, p_a, peer_a, p_b, mask, scale, wq, wo, keys, values, wg, wu, wd):
     _, heads, slots, head_dim, tokens = keys.shape
     dim, ff = wg.shape
     tc = tokens // 2
@@ -366,20 +375,21 @@
         wu_scr=pltpu.VMEM((dim, ff), BF16),
         wd_scr=pltpu.VMEM((ff, dim), BF16),
         acc=pltpu.VMEM((tc, dim), F32),
-        d_sem=pltpu.SemaphoreType.DMA((3,)),
+        h_scr=pltpu.VMEM((tokens, dim), BF16),
+        d_sem=pltpu.SemaphoreType.DMA((4,)),
     )
-    names = CROSS_IN + ('wg', 'wu', 'wd', 'h2_a', 'h2_b', 'pd_b') + tuple(scratch)
+    names = ('hidden',) + CROSS_IN[2:] + ('wg', 'wu', 'wd', 'h2_a', 'h2_b', 'pd_b') + tuple(scratch)
     rows = jax.ShapeDtypeStruct((tc, dim), BF16)
     return pl.pallas_call(
         functools.partial(block_a_kernel, names),
-        in_specs=[VMEM_SPEC] * 5 + [HBM_SPEC] * 9,
+        in_specs=[HBM_SPEC] + [VMEM_SPEC] * 3 + [HBM_SPEC] * 9,
         out_specs=[VMEM_SPEC] * 3,
         out_shape=[rows] * 3,
         scratch_shapes=list(scratch.values()),
-        compiler_params=pltpu.CompilerParams(vmem_limit_bytes=56 << 20, collective_id=0, has_side_effects=True),
+        compiler_params=pltpu.CompilerParams(vmem_limit_bytes=48 << 20, collective_id=0, has_side_effects=True),
         cost_estimate=pl.CostEstimate(flops=20_000_000_000, bytes_accessed=20 << 20, transcendentals=0),
         name="block_a",
-    )(h_a, h_b, p_a, peer_a, p_b, mask, scale, wq, wo, keys, values, wg, wu, wd)
+    )(hidden, p_a, peer_a, p_b, mask, scale, wq, wo, keys, values, wg, wu, wd)
 
 
 def block_b_kernel(names, *refs):
@@ -388,10 +398,16 @@
     group = lax.axis_size('ep')
     local, cap_rows, dim = t.xin.shape
     capacity = cap_rows // group
-    tokens = t.x_scr.shape[0]
+    tokens = t.h_scr.shape[0]
     ring = t.wg_ring.shape[0]
     tc = tokens // 2
+    half = dim // 2
+    lag = 3
+    rows_local = local * capacity
+    near = (dp, tp, me + 1 - 2 * lax.rem(me, 2))
+    across = (dp, tp, lax.rem(me + 2, group))
     others = [(dp, tp, lax.rem(me + k, group)) for k in range(1, group)]
+    owners = (me, near[2], across[2], lax.rem(near[2] + 2, group))
 
     def fetch(i):
         slot = lax.rem(i, ring)
@@ -402,16 +418,56 @@
     side = [pltpu.make_async_copy(r.router, t.router_scr, t.s_sem.at[0]), pltpu.make_async_copy(r.idx, t.idx_scr, t.s_sem.at[1])]
     for copy in side:
         copy.start()
+    greet([tp_peer()] + others)
+    early = []
     for i in range(ring):
-        for copy in fetch(i):
-            copy.start()
-    greet([tp_peer()] + others)
-    h_a, h_b = cross.run()
+        early += fetch(i)
+
+    h_a, h_b = cross.run(early)
     t.h_scr[0:tc, :] = h_a
     t.h_scr[tc:, :] = h_b
-
-    for copy in side:
-        copy.wait()
+    def spread(c):
+        rows = pl.ds(c * tc, tc)
+        mine = t.x_scr.at[0, rows, :]
+        return [
+            remote(mine, t.x_scr.at[2, rows, :], (t.xs_sem.at[c, 0], t.xr_sem.at[c, 0]), across),
+            remote(mine, t.x_scr.at[1, rows, :], (t.xs_sem.at[c, 1], t.xr_sem.at[c, 1]), near),
+            remote(t.x_scr.at[2, rows, :], t.x_scr.at[3, rows, :], (t.xs_sem.at[c, 2], t.xr_sem.at[c, 2]), near),
+        ]
+
+    def span(owner, i):
+        return pl.ds(pl.multiple_of((owner * local + i) * capacity, capacity), capacity)
+
+    def mine(owner):
+        return pl.ds(pl.multiple_of(owner * capacity, capacity), capacity)
+
+    def send_back(i, k):
+        dst = lax.rem(me + k, group)
+        return remote(t.ysum.at[i, mine(dst), :], t.ret.at[span(me, i), :], (t.bs_sem.at[k - 1, i], t.br_sem.at[k - 1, i]), (dp, tp, dst))
+
+    def fold(i):
+        return remote(t.yout.at[i], t.yin.at[i], (t.os_sem.at[i], t.or_sem.at[i]), tp_peer())
+
+    def give_back(i):
+        fold(i).wait_recv()
+        t.ysum[i] = (t.ysum[i].astype(F32) + t.yin[i].astype(F32)).astype(BF16)
+        for k in range(1, group):
+            send_back(i, k).start()
+        t.ret[span(me, i), :] = t.ysum[i, mine(me), :]
+
+    def finish(c):
+        rows = slice(c * tc, (c + 1) * tc)
+        cross.swaps[1 + c].wait_recv()
+        h_cur = add_parts(t.h_scr[rows, :], t.sbuf[c], t.rbuf[1 + c])
+        t.h_scr[rows, :] = h_cur
+        t.x_scr[0, rows, :] = rms_norm(h_cur, t.scale_scr[2, 1:2, :])
+        hops = spread(c)
+        hops[0].start()
+        hops[1].start()
+        return hops
+
+    first = finish(0)
+    side[1].wait()
     lane_idx = jnp.broadcast_to(t.idx_scr[...].astype(F32), (tokens, tokens))
     row_idx = jnp.transpose(lane_idx)
     same = lane_idx == row_idx
@@ -419,52 +475,43 @@
     lane_no = lax.broadcasted_iota(jnp.int32, same.shape, 1)
     lane_slot = jnp.sum(jnp.where(same & (row_no < lane_no), 1.0, 0.0), axis=0, keepdims=True)
     row_slot = jnp.sum(jnp.where(same & (lane_no < row_no), 1.0, 0.0), axis=1, keepdims=True)
-    total = group * local * capacity
+    total = group * rows_local
     lane_dest = jnp.where(lane_slot < capacity, lane_idx[0:1, :] * capacity + lane_slot, -1.0)
     row_dest = jnp.where(row_slot < capacity, row_idx[:, 0:1] * capacity + row_slot, -1.0)
-    t.pick[...] = (lax.broadcasted_iota(jnp.int32, (total, tokens), 0).astype(F32) == lane_dest).astype(BF16)
+    t.dest[0] = jnp.broadcast_to(lane_dest, t.dest.shape[1:])
+    dest_sends = [remote(t.dest.at[0], t.dest.at[k], (t.is_sem.at[k - 1], t.ir_sem.at[k - 1]), (dp, tp, owners[k])) for k in range(1, group)]
+    for copy in dest_sends:
+        copy.start()
     t.place[...] = (lax.broadcasted_iota(jnp.int32, (tokens, total), 1).astype(F32) == row_dest).astype(BF16)
-    expert_hot = lax.broadcasted_iota(jnp.int32, (tokens, group * local), 1).astype(F32) == row_idx[:, 0:1]
-
-    for c in range(2):
-        rows = slice(c * tc, (c + 1) * tc)
-        cross.swaps[1 + c].wait_recv()
-        h_cur = add_parts(t.h_scr[rows, :], t.sbuf[c], t.rbuf[1 + c])
-        t.h_scr[rows, :] = h_cur
-        t.x_scr[rows, :] = rms_norm(h_cur, t.scale_scr[2, 1:2, :])
-    t.disp[...] = project(t.pick[...], t.x_scr[...]).astype(BF16)
-
-    def span(owner, i):
-        return pl.ds(pl.multiple_of((owner * local + i) * capacity, capacity), capacity)
-
-    def mine(owner):
-        return pl.ds(pl.multiple_of(owner * capacity, capacity), capacity)
-
-    def send_rows(i, k):
-        dst = lax.rem(me + k, group)
-        return remote(t.disp.at[span(dst, i), :], t.xin.at[i, mine(me), :], (t.ds_sem.at[k - 1, i], t.dr_sem.at[k - 1, i]), (dp, tp, dst))
-
-    def send_back(i, k):
-        dst = lax.rem(me + k, group)
-        return remote(t.yout.at[i, mine(dst), :], t.ret.at[span(me, i), :], (t.bs_sem.at[k - 1, i], t.br_sem.at[k - 1, i]), (dp, tp, dst))
-
-    @pl.loop(0, local)
-    def _(i):
-        for k in range(1, group):
-            send_rows(i, k).start()
-        t.xin[i, mine(me), :] = t.disp[span(me, i), :]
-
-    logits = jnp.dot(t.x_scr[...].astype(F32), t.router_scr[...].T, precision=lax.Precision.HIGHEST, preferred_element_type=F32)
+    t.hot[...] = jnp.where(lax.broadcasted_iota(jnp.int32, t.hot.shape, 1).astype(F32) == row_idx[:, 0:1], 1.0, 0.0)
+
+    second = finish(1)
+    first[0].wait_recv()
+    first[2].start()
+    first_row = (me * rows_local).astype(F32)
+    for k in range(group):
+        if k:
+            dest_sends[k - 1].wait_recv()
+        wanted = lax.broadcasted_iota(jnp.int32, (rows_local, tokens), 0).astype(F32) + first_row
+        t.pick[k] = (wanted == t.dest[k, 0:1, :]).astype(BF16)
+    side[0].wait()
+    logits = jnp.dot(t.x_scr[0].astype(F32), t.router_scr[...].T, precision=lax.Precision.HIGHEST, preferred_element_type=F32)
     top = jnp.max(logits, axis=-1, keepdims=True)
     weight = jnp.exp(logits - top)
     weight = weight / jnp.sum(weight, axis=-1, keepdims=True)
-    t.gate[...] = jnp.broadcast_to(jnp.sum(jnp.where(expert_hot, weight, 0.0), axis=-1, keepdims=True), t.gate.shape)
+    t.gate[...] = jnp.broadcast_to(jnp.sum(t.hot[...] * weight, axis=-1, keepdims=True), t.gate.shape)
+    second[0].wait_recv()
+    second[2].start()
+    for copy in first[1:] + second[1:]:
+        copy.wait_recv()
+    for k in range(group):
+        block = project(t.pick[k], t.x_scr[k]).astype(BF16)
+        for i in range(local):
+            t.xin[i, mine(owners[k]), :] = block[i * capacity:(i + 1) * capacity, :]
 
     @pl.loop(0, local)
     def _(i):
         slot = lax.rem(i, ring)
-        for k in range(1, group):
-            send_rows(i, k).wait_recv()
         copies = fetch(i)
         x = t.xin[i]
         copies[0].wait()
@@ -472,15 +519,24 @@
         copies[1].wait()
         product = (gate_in * project(x, t.wu_ring[slot])).astype(BF16)
         copies[2].wait()
-        t.yout[i] = project(product, t.wd_ring[slot]).astype(BF16)
-        for k in range(1, group):
-            send_back(i, k).start()
-        t.ret[span(me, i), :] = t.yout[i, mine(me), :]
+        result = project(product, t.wd_ring[slot]).astype(BF16)
+        low, high = result[:, :half], result[:, half:]
+        t.ysum[i] = jnp.where(tp == 0, low, high)
+        t.yout[i] = jnp.where(tp == 0, high, low)
+        fold(i).start()
+
+        @pl.when(i >= lag)
+        def _():
+            give_back(i - lag)
 
         @pl.when(i + ring < local)
         def _():
             for copy in fetch(i + ring):
                 copy.start()
+
+    @pl.loop(local - lag, local)
+    def _(i):
+        give_back(i)
 
     @pl.loop(0, local)
     def _(i):
@@ -496,16 +552,18 @@
     for p in range(pieces):
         rows = slice(p * size, (p + 1) * size)
         last[p].wait_recv()
-        both = (t.comb[p].astype(F32) + t.comb_peer[p].astype(F32))
+        own, peer = t.comb[p].astype(F32), t.comb_peer[p].astype(F32)
         gate = t.gate[rows, 0:1]
-        r.out[rows, :] = (t.h_scr[rows, :].astype(F32) + gate * both).astype(BF16)
-    for copy in cross.swaps + last:
+        for side_no, both in enumerate((jnp.where(tp == 0, own, peer), jnp.where(tp == 0, peer, own))):
+            cols = slice(side_no * half, (side_no + 1) * half)
+            r.out[rows, cols] = (t.h_scr[rows, cols].astype(F32) + gate * both).astype(BF16)
+    for copy in cross.swaps + last + dest_sends + first + second:
         copy.wait_send()
 
     @pl.loop(0, local)
     def _(i):
+        fold(i).wait_send()
         for k in range(1, group):
-            send_rows(i, k).wait_send()
             send_back(i, k).wait_send()
 
 
@@ -525,22 +583,29 @@
         router_scr=pltpu.VMEM(router.shape, F32),
         idx_scr=pltpu.VMEM((1, tokens), jnp.int32),
         h_scr=pltpu.VMEM((tokens, dim), BF16),
-        x_scr=pltpu.VMEM((tokens, dim), BF16),
-        pick=pltpu.VMEM((experts * capacity, tokens), BF16),
+        x_scr=pltpu.VMEM((group, tokens, dim), BF16),
+        dest=pltpu.VMEM((group, 8, tokens), F32),
+        hot=pltpu.VMEM((tokens, experts), F32),
+        pick=pltpu.VMEM((group, local * capacity, tokens), BF16),
         place=pltpu.VMEM((tokens, experts * capacity), BF16),
         gate=pltpu.VMEM((tokens, 128), F32),
-        disp=pltpu.VMEM((experts * capacity, dim), BF16),
         xin=pltpu.VMEM((local, group * capacity, dim), BF16),
-        yout=pltpu.VMEM((local, group * capacity, dim), BF16),
-        ret=pltpu.VMEM((experts * capacity, dim), BF16),
-        comb=pltpu.VMEM((pieces, tokens // pieces, dim), BF16),
-        comb_peer=pltpu.VMEM((pieces, tokens // pieces, dim), BF16),
+        yout=pltpu.VMEM((local, group * capacity, dim // 2), BF16),
+        yin=pltpu.VMEM((local, group * capacity, dim // 2), BF16),
+        ysum=pltpu.VMEM((local, group * capacity, dim // 2), BF16),
+        ret=pltpu.VMEM((experts * capacity, dim // 2), BF16),
+        comb=pltpu.VMEM((pieces, tokens // pieces, dim // 2), BF16),
+        comb_peer=pltpu.VMEM((pieces, tokens // pieces, dim // 2), BF16),
         e_sem=pltpu.SemaphoreType.DMA((3, ring)),
         s_sem=pltpu.SemaphoreType.DMA((2,)),
-        ds_sem=pltpu.SemaphoreType.DMA(hops),
-        dr_sem=pltpu.SemaphoreType.DMA(hops),
+        is_sem=pltpu.SemaphoreType.DMA((group - 1,)),
+        ir_sem=pltpu.SemaphoreType.DMA((group - 1,)),
+        xs_sem=pltpu.SemaphoreType.DMA((2, 3)),
+        xr_sem=pltpu.SemaphoreType.DMA((2, 3)),
         bs_sem=pltpu.SemaphoreType.DMA(hops),
         br_sem=pltpu.SemaphoreType.DMA(hops),
+        os_sem=pltpu.SemaphoreType.DMA((local,)),
+        or_sem=pltpu.SemaphoreType.DMA((local,)),
         fs_sem=pltpu.SemaphoreType.DMA((pieces,)),
         fr_sem=pltpu.SemaphoreType.DMA((pieces,)),
     )
@@ -551,7 +616,7 @@
         out_specs=VMEM_SPEC,
         out_shape=jax.ShapeDtypeStruct((tokens, dim), BF16),
         scratch_shapes=list(scratch.values()),
-        compiler_params=pltpu.CompilerParams(vmem_limit_bytes=63 << 20, collective_id=1, has_side_effects=True),
+        compiler_params=pltpu.CompilerParams(vmem_limit_bytes=62 << 20, collective_id=1, has_side_effects=True),
         cost_estimate=pl.CostEstimate(flops=40_000_000_000, bytes_accessed=70 << 20, transcendentals=0),
         name="block_b",
     )(h_a, h_b, p_a, peer_a, p_b, mask, scale, wq, wo, keys, values, router, idx, wg, wu, wd)
@@ -568,18 +633,25 @@
     pos = write_pos.reshape(1, -1)
     mask = enc_mask.T
     scale = jnp.transpose(norm_scale, (1, 0, 2))
+    def hbm(*arrays):
+        return [pltpu.with_memory_space_constraint(array, pltpu.HBM) for array in arrays]
+
+    hidden, pos, scale, rel_bias, mask = hbm(hidden, pos, scale, rel_bias, mask)
+    w_query, w_key, w_value, w_out, w_cross_query, w_cross_out = hbm(w_query, w_key, w_value, w_out, w_cross_query, w_cross_out)
+    keys, values, ckeys, cvalues = hbm(keys, values, ckeys, cvalues)
+    dense_gate, dense_up, dense_down, exp_gate, exp_up, exp_down = hbm(dense_gate, dense_up, dense_down, exp_gate, exp_up, exp_down)
+    router_t, idx = hbm(router.T, expert_idx.reshape(1, -1))
     shared = (pos, scale, rel_bias, w_query, w_key, w_value, w_out, keys, values)
     cross = (mask, scale, w_cross_query, w_cross_out, ckeys, cvalues)
     p_a, *outs = self_call(0, 0, hidden, None, *shared, None)
     pair_a = swap(p_a)
     p_b, *outs = self_call(0, 1, hidden, None, *shared, outs)
-    h_a, h_b = hidden[:hidden.shape[0] // 2], hidden[hidden.shape[0] // 2:]
-    h_a, h_b, pd_b = block_a_call(h_a, h_b, *pair_a, p_b, *cross, dense_gate, dense_up, dense_down)
+    h_a, h_b, pd_b = block_a_call(hidden, *pair_a, p_b, *cross, dense_gate, dense_up, dense_down)
     pair_b = swap(pd_b)
     p_a, *outs = self_call(1, 0, h_a, None, *shared, outs)
     pair_a = swap(p_a)
     h_b, p_b, *outs = self_call(1, 1, h_b, pair_b, *shared, outs)
-    h_all = block_b_call(h_a, h_b, *pair_a, p_b, *cross, router.T, expert_idx.reshape(1, -1), exp_gate, exp_up, exp_down, lax.axis_size('ep'))
+    h_all = block_b_call(h_a, h_b, *pair_a, p_b, *cross, router_t, idx, exp_gate, exp_up, exp_down, lax.axis_size('ep'))
     back = (0, 4, 1, 2, 3)
     return h_all, jnp.transpose(outs[0], back), jnp.transpose(outs[1], back)
 

time: 140 us -> 125 us (0.89)
  local copies, waits for them, and re-layouts: 14.4 us -> 3.8 us
  Pallas kernels: 119 us -> 114 us
    unnamed x51 -> x11, local copies, waits for them, and re-layouts: 13.6 us -> 3.8 us
    pallas_call x1, Pallas kernels: 57.4 us -> 53.2 us  [block_b_call(): pl.pallas_call(functools.partial(block_b_kernel, names), in_specs=[VMEM_S...]
    pallas_call x1, Pallas kernels: 21.6 us -> 19.3 us  [block_a_call(): pl.pallas_call(functools.partial(block_a_kernel, names), in_specs=[HBM_SP...]
    pallas_call x4, Pallas kernels: 39.7 us -> 41.9 us  [self_call(): pl.pallas_call(functools.partial(self_kernel, layer, chunk, residual, ali...]
  transfers between devices with their start and end apart: 3 -> 3, of which waited for: 0 -> 0; matrix products, arithmetic and copies ran while one was open for 1% -> 0% of each run, Pallas kernels for 21% -> 25%
where the time goes in v3:
time: 125 us; the launch traced here: 124 us
  Pallas kernels  114 us (91%)
  starting transfers between devices  5.46 us (4%)
  local copies, waits for them, and re-layouts  3.8 us (3%)
    pallas_call x1, Pallas kernels, block_b_call(): pl.pallas_call(functools.partial(block_b_kernel, names), in_specs=[VMEM_S...  53.2 us
    pallas_call x4, Pallas kernels, self_call(): pl.pallas_call(functools.partial(self_kernel, layer, chunk, residual, ali...  41.9 us
    pallas_call x1, Pallas kernels, block_a_call(): pl.pallas_call(functools.partial(block_a_kernel, names), in_specs=[HBM_SP...  19.3 us
    ppermute x3, starting transfers between devices, swap(): return (part, lax.ppermute(part, 'tp', SWAP))  5.46 us
    unnamed x11, local copies, waits for them, and re-layouts  3.8 us
  transfers between devices with their start and end apart: 3, of which 0 were waited for; matrix products, arithmetic and copies ran while one was open for 0% of the time, Pallas kernels for 25%

profile of v3, /device:TPU:0, one launch (start us, length us, event | category | flops | bytes accessed | tf_op | source)
XLA Modules:
  0.0 124.4 jit_solution(17876156586844659016)
XLA Ops:
  0.6 10.5 %self0_0.1 = (bf16[128,768]{1,0:T(8,128)(2,1)S(1)}, bf16[2,6,64,64,256]{4,3,2,1,0:T(8,128)(2,1)}, bf16[2,6,64,64,256]{4,3,2,1,0:T(8,128)(2,1)}) custom-call(bf16[256,768]{1,0:T(8,128)(2,1)} %refs_0_.5, s32[1,256]{1,0:T(1,128)} %bitcast.27, f32[3,2,768]{2,1,0:T(2,128)} %bitcast.21, f32[6,64]{1,0:T(8,128)} %refs_5_.7, bf16[2,768,384]{2,1,0:T(8,128)(2,1)} %refs_6_.9, ...), custom_call_target="tpu_custom_call" | custom-call | flops 1258291200 | bytes 25165824 | tf_op jit(solution)/shard_map/self0_0/pallas_call | solution.py:162
  11.1 3.4 %collective-permute-start = (bf16[128,768]{1,0:T(8,128)(2,1)S(1)}, bf16[128,768]{1,0:T(8,128)(2,1)S(1)}, u32[]{:S(2)}, u32[]{:S(2)}) collective-permute-start(bf16[128,768]{1,0:T(8,128)(2,1)S(1)} %get-tuple-element.19.refs_1_), channel_id=1, source_target_pairs={{0,4},{4,0},{1,5},{5,1},{2,6},{6,2},{3,7},{7,3}} | collective-permute-start | bytes 589832 | tf_op jit(solution)/shard_map/ppermute | solution.py:626
  14.5 10.5 %self0_1.1 = (bf16[128,768]{1,0:T(8,128)(2,1)S(1)}, bf16[2,6,64,64,256]{4,3,2,1,0:T(8,128)(2,1)}, bf16[2,6,64,64,256]{4,3,2,1,0:T(8,128)(2,1)}) custom-call(bf16[256,768]{1,0:T(8,128)(2,1)} %refs_0_.5, s32[1,256]{1,0:T(1,128)} %bitcast.28, f32[3,2,768]{2,1,0:T(2,128)} %bitcast.22, f32[6,64]{1,0:T(8,128)} %refs_5_.7, ...), custom_call_target="tpu_custom_call", output_to_operand_aliasing={{1}: (10, {}), {2}: (11, {})} | custom-call | flops 1258291200 | bytes 25165824 | tf_op jit(solution)/shard_map/self0_1/pallas_call | solution.py:162
  25.0 0.0 collective-permute-done.refs_2_
  25.0 19.3 %block_a.1 = (bf16[128,768]{1,0:T(8,128)(2,1)S(1)}, bf16[128,768]{1,0:T(8,128)(2,1)S(1)}, bf16[128,768]{1,0:T(8,128)(2,1)S(1)}) custom-call(bf16[256,768]{1,0:T(8,128)(2,1)} %refs_0_.5, bf16[128,768]{1,0:T(8,128)(2,1)S(1)} %get-tuple-element.19.refs_1_, bf16[128,768]{1,0:T(8,128)(2,1)S(1)} %collective-permute-done.refs_2_, ...), custom_call_target="tpu_custom_call" | custom-call | flops 20000000000 | bytes 20971520 | tf_op jit(solution)/shard_map/block_a/pallas_call | solution.py:383
  44.4 0.0 copy-start
  44.4 1.4 %collective-permute-start.1 = (bf16[128,768]{1,0:T(8,128)(2,1)S(1)}, bf16[128,768]{1,0:T(8,128)(2,1)S(1)}, u32[]{:S(2)}, u32[]{:S(2)}) collective-permute-start(bf16[128,768]{1,0:T(8,128)(2,1)S(1)} %get-tuple-element.25.refs_1_), channel_id=1, source_target_pairs={{0,4},{4,0},{1,5},{5,1},{2,6},{6,2},{3,7},{7,3}} | collective-permute-start | bytes 589832 | tf_op jit(solution)/shard_map/ppermute | solution.py:626
  45.7 10.4 %self1_0.1 = (bf16[128,768]{1,0:T(8,128)(2,1)S(1)}, bf16[2,6,64,64,256]{4,3,2,1,0:T(8,128)(2,1)}, bf16[2,6,64,64,256]{4,3,2,1,0:T(8,128)(2,1)}) custom-call(bf16[128,768]{1,0:T(8,128)(2,1)S(1)} %get-tuple-element.23.refs_0_, s32[1,256]{1,0:T(1,128)} %bitcast.29, f32[3,2,768]{2,1,0:T(2,128)} %bitcast.24, ...), custom_call_target="tpu_custom_call", output_to_operand_aliasing={{1}: (10, {}), {2}: (11, {})} | custom-call | flops 1258291200 | bytes 25165824 | tf_op jit(solution)/shard_map/self1_0/pallas_call | solution.py:162
  56.2 0.0 copy-done
  56.2 0.0 copy-start.1
  56.2 0.7 collective-permute-start.2
  56.9 0.0 collective-permute-done.1.refs_2_
  56.9 10.4 %self1_1.1 = (bf16[128,768]{1,0:T(8,128)(2,1)S(1)}, bf16[128,768]{1,0:T(8,128)(2,1)S(1)}, bf16[2,6,64,64,256]{4,3,2,1,0:T(8,128)(2,1)}, bf16[2,6,64,64,256]{4,3,2,1,0:T(8,128)(2,1)}) custom-call(bf16[128,768]{1,0:T(8,128)(2,1)S(1)} %get-tuple-element.24.refs_0_, ...), custom_call_target="tpu_custom_call", output_to_operand_aliasing={{2}: (12, {}), {3}: (13, {})} | custom-call | flops 1258291200 | bytes 25165824 | tf_op jit(solution)/shard_map/self1_1/pallas_call | solution.py:162
  67.3 0.0 copy-done.1
  67.4 0.0 copy-start.2
  67.4 0.7 copy-done.2
  68.0 0.0 copy-start.3
  68.0 0.7 copy-done.3
  68.7 0.0 collective-permute-done.2.refs_3_
  68.7 0.0 copy-start.4
  68.7 0.7 copy-done.4
  69.4 53.2 %block_b.1 = bf16[256,768]{1,0:T(8,128)(2,1)} custom-call(bf16[128,768]{1,0:T(8,128)(2,1)} %copy-done, bf16[128,768]{1,0:T(8,128)(2,1)} %copy-done.2, bf16[128,768]{1,0:T(8,128)(2,1)} %copy-done.1, bf16[128,768]{1,0:T(8,128)(2,1)} %copy-done.4, bf16[128,768]{1,0:T(8,128)(2,1)} %copy-done.3, s32[32,256]{1,0:T(8,128)} %bitcast.37, f32[3,2,768]{2,1,0:T(2,128)} %bitcast.26, ...), custom_call_target="tpu_custom_call" | custom-call | flops 40000000000 | bytes 73400320 | tf_op jit(solution)/shard_map/block_b/pallas_call | solution.py:613
  122.6 1.8 %copy.39 = bf16[256,768]{1,0:T(8,128)(2,1)} copy(bf16[256,768]{1,0:T(8,128)(2,1)} %block_b.1) | data formatting | bytes 786432
Async XLA Ops:
  11.1 13.9 %collective-permute-start = (bf16[128,768]{1,0:T(8,128)(2,1)S(1)}, bf16[128,768]{1,0:T(8,128)(2,1)S(1)}, u32[]{:S(2)}, u32[]{:S(2)}) collective-permute-start(bf16[128,768]{1,0:T(8,128)(2,1)S(1)} %get-tuple-element.19.refs_1_), channel_id=1, source_target_pairs={{0,4},{4,0},{1,5},{5,1},{2,6},{6,2},{3,7},{7,3}} | collective-permute-start | bytes 589832 | tf_op jit(solution)/shard_map/ppermute | solution.py:626
  44.4 11.8 %copy-start = (bf16[128,768]{1,0:T(8,128)(2,1)}, bf16[128,768]{1,0:T(8,128)(2,1)S(1)}, u32[]{:S(2)}) copy-start(bf16[128,768]{1,0:T(8,128)(2,1)S(1)} %get-tuple-element.23.refs_0_) | copy-start | bytes 589828
  44.4 12.5 %collective-permute-start.1 = (bf16[128,768]{1,0:T(8,128)(2,1)S(1)}, bf16[128,768]{1,0:T(8,128)(2,1)S(1)}, u32[]{:S(2)}, u32[]{:S(2)}) collective-permute-start(bf16[128,768]{1,0:T(8,128)(2,1)S(1)} %get-tuple-element.25.refs_1_), channel_id=1, source_target_pairs={{0,4},{4,0},{1,5},{5,1},{2,6},{6,2},{3,7},{7,3}} | collective-permute-start | bytes 589832 | tf_op jit(solution)/shard_map/ppermute | solution.py:626
  56.2 11.2 %copy-start.1 = (bf16[128,768]{1,0:T(8,128)(2,1)}, bf16[128,768]{1,0:T(8,128)(2,1)S(1)}, u32[]{:S(2)}) copy-start(bf16[128,768]{1,0:T(8,128)(2,1)S(1)} %get-tuple-element.31.refs_2_) | copy-start | bytes 589828
  56.2 12.5 %collective-permute-start.2 = (bf16[128,768]{1,0:T(8,128)(2,1)S(1)}, bf16[128,768]{1,0:T(8,128)(2,1)S(1)}, u32[]{:S(2)}, u32[]{:S(2)}) collective-permute-start(bf16[128,768]{1,0:T(8,128)(2,1)S(1)} %get-tuple-element.31.refs_2_), channel_id=1, source_target_pairs={{0,4},{4,0},{1,5},{5,1},{2,6},{6,2},{3,7},{7,3}} | collective-permute-start | bytes 589832 | tf_op jit(solution)/shard_map/ppermute | solution.py:626
  67.4 0.7 copy-start.2
  68.0 0.7 copy-start.3
  68.7 0.7 copy-start.4

commit v4 on v3

--- a/solution.py
+++ b/solution.py
@@ -12,6 +12,8 @@
 F32 = jnp.float32
 BF16 = jnp.bfloat16
 CHUNKS = 2
+SELF_LIMIT = 18 << 20
+B_LIMIT = 62 << 20
 VMEM_SPEC = pl.BlockSpec(memory_space=pltpu.VMEM)
 HBM_SPEC = pl.BlockSpec(memory_space=pltpu.HBM)
 SWAP = [(0, 1), (1, 0)]
@@ -38,160 +40,219 @@
     return weight / jnp.sum(weight, axis=0, keepdims=True)
 
 
-def self_kernel(layer, chunk, residual, aliased, *refs):
-    refs = list(refs)
-    h_ref = refs.pop(0)
-    if residual:
-        own_ref, peer_ref = refs.pop(0), refs.pop(0)
-    pos_hbm, scale_hbm, bias_hbm, wq_hbm, wk_hbm, wv_hbm, wo_hbm, k_hbm, v_hbm = refs[:9]
-    refs = refs[9 + 2 * aliased:]
-    if residual:
-        h_out = refs.pop(0)
-    part_ref, ko_hbm, vo_hbm, h_scr, pos_scr, scale_scr, bias_scr, line_scr, wq_scr, wk_scr, wv_scr, wo_scr, kbuf, vbuf, q_t, k_t, v_t, ctx_t, prob, posb, hot, small_sem, w_sem, k_sem, v_sem, ko_sem, vo_sem = refs
-    heads, slots, head_dim, tc = kbuf.shape
+class Refs:
+    def __init__(self, names, refs):
+        self.__dict__.update(zip(names, refs, strict=True))
+
+
+WEIGHTS = ('wq', 'wk', 'wv', 'wo')
+
+
+def self_kernel(layer, chunk, ahead_first, names, *refs):
+    t = Refs(names, refs)
+    ready = hasattr(t, 'k_ready')
+    heads, slots, head_dim, tc = t.kbuf.shape
     lanes = pl.ds(chunk * tc, tc)
-
     small = [
-        pltpu.make_async_copy(pos_hbm.at[:, lanes], pos_scr, small_sem.at[0]),
-        pltpu.make_async_copy(scale_hbm.at[0], scale_scr, small_sem.at[1]),
-        pltpu.make_async_copy(bias_hbm, bias_scr, small_sem.at[2]),
+        pltpu.make_async_copy(t.pos.at[:, lanes], t.pos_scr, t.small_sem.at[0]),
+        pltpu.make_async_copy(t.scale.at[0], t.scale_scr, t.small_sem.at[1]),
+        pltpu.make_async_copy(t.bias, t.bias_scr, t.small_sem.at[2]),
     ]
-    sliced = h_ref.shape[0] != tc
-    if sliced:
-        small.append(pltpu.make_async_copy(h_ref.at[lanes, :], h_scr, small_sem.at[3]))
+    if hasattr(t, 'h_scr'):
+        small.append(pltpu.make_async_copy(t.h.at[lanes, :], t.h_scr, t.small_sem.at[3]))
     for copy in small:
         copy.start()
-    weights = [pltpu.make_async_copy(hbm.at[layer], scr, w_sem.at[i]) for i, (hbm, scr) in enumerate(((wq_hbm, wq_scr), (wk_hbm, wk_scr), (wv_hbm, wv_scr), (wo_hbm, wo_scr)))]
+    weights = []
+    if hasattr(t, 'wq_hbm'):
+        weights = [pltpu.make_async_copy(getattr(t, name + '_hbm').at[layer], getattr(t, name), t.w_sem.at[i]) for i, name in enumerate(WEIGHTS)]
     for copy in weights[:3]:
         copy.start()
 
-    def fetch_k(head):
-        return pltpu.make_async_copy(k_hbm.at[layer, head, :, :, lanes], kbuf.at[head], k_sem.at[head])
-
-    def fetch_v(head):
-        return pltpu.make_async_copy(v_hbm.at[layer, head, :, :, lanes], vbuf.at[head], v_sem.at[head])
+    def fetch(head):
+        if ready:
+            return []
+        return [
+            pltpu.make_async_copy(t.keys.at[layer, head, :, :, lanes], t.kbuf.at[head], t.k_sem.at[head]),
+            pltpu.make_async_copy(t.values.at[layer, head, :, :, lanes], t.vbuf.at[head], t.v_sem.at[head]),
+        ]
 
     def store_k(head):
-        return pltpu.make_async_copy(kbuf.at[head], ko_hbm.at[layer, head, :, :, lanes], ko_sem.at[head])
+        return pltpu.make_async_copy(t.kbuf.at[head], t.ko.at[layer, head, :, :, lanes], t.ko_sem.at[head])
 
     def store_v(head):
-        return pltpu.make_async_copy(vbuf.at[head], vo_hbm.at[layer, head, :, :, lanes], vo_sem.at[head])
-
-    fetch_k(0).start()
-    fetch_v(0).start()
+        return pltpu.make_async_copy(t.vbuf.at[head], t.vo.at[layer, head, :, :, lanes], t.vo_sem.at[head])
+
+    results = []
+    for copy in fetch(0):
+        copy.start()
     for copy in small:
         copy.wait()
-    if residual:
-        h_cur = add_parts(h_ref[...], own_ref[...], peer_ref[...])
-        h_out[...] = h_cur
-    else:
-        h_cur = h_scr[...] if sliced else h_ref[...]
-    x = rms_norm(h_cur, scale_scr[layer:layer + 1, :])
-    pos = pos_scr[...]
-    posb[...] = jnp.broadcast_to(pos.astype(F32), posb.shape).astype(BF16)
-    hot[...] = (lax.broadcasted_iota(jnp.int32, hot.shape, 0) == pos).astype(F32)
-    line_scr[...] = jnp.zeros_like(line_scr)
-    line_scr[0:heads, 0:slots] = bias_scr[...]
+    h_cur = t.h_scr[...] if hasattr(t, 'h_scr') else t.h[...]
+    if hasattr(t, 'own'):
+        h_cur = add_parts(h_cur, t.own[...], t.peer[...])
+        t.h_out_scr[...] = h_cur
+        results.append(pltpu.make_async_copy(t.h_out_scr, t.h_out, t.o_sem.at[1]))
+        results[0].start()
+    x = rms_norm(h_cur, t.scale_scr[layer:layer + 1, :])
+    pos = t.pos_scr[...]
+    t.posb[...] = jnp.broadcast_to(pos.astype(F32), t.posb.shape).astype(BF16)
+    t.hot[...] = (lax.broadcasted_iota(jnp.int32, t.hot.shape, 0) == pos).astype(F32)
+    t.line_scr[...] = jnp.zeros_like(t.line_scr)
+    t.line_scr[0:heads, 0:slots] = t.bias_scr[...]
     for copy in weights[:3]:
         copy.wait()
     for head in range(1, heads):
-        fetch_k(head).start()
-        fetch_v(head).start()
-    weights[3].start()
-    q_t[...] = jnp.transpose(project(x, wq_scr[...])).astype(BF16).astype(F32)
-    k_t[...] = jnp.transpose(project(x, wk_scr[...])).astype(BF16)
-    v_t[...] = jnp.transpose(project(x, wv_scr[...])).astype(BF16)
-    posv = posb[...]
+        for copy in fetch(head):
+            copy.start()
+    ahead = []
+    if hasattr(t, 'next_k'):
+        for c in range(t.k_ahead.shape[0]):
+            cols = pl.ds((c + ahead_first) * tc, tc)
+            ahead.append(pltpu.make_async_copy(t.next_k.at[1, :, :, :, cols], t.k_ahead.at[c], t.a_sem.at[2 * c]))
+            ahead.append(pltpu.make_async_copy(t.next_v.at[1, :, :, :, cols], t.v_ahead.at[c], t.a_sem.at[2 * c + 1]))
+    for copy in weights[3:] + ahead:
+        copy.start()
+    t.q_t[...] = jnp.transpose(project(x, t.wq[...])).astype(BF16).astype(F32)
+    t.k_t[...] = jnp.transpose(project(x, t.wk[...])).astype(BF16)
+    t.v_t[...] = jnp.transpose(project(x, t.wv[...])).astype(BF16)
+    posv = t.posb[...]
+    k_src, v_src = (t.k_ready.at[0], t.v_ready.at[0]) if ready else (t.kbuf, t.vbuf)
 
     @pl.loop(0, heads)
     def _(head):
         rows = pl.ds(pl.multiple_of(head * head_dim, head_dim), head_dim)
-        q = q_t[rows, :]
-        k_new = k_t[rows, :]
-        fetch_k(head).wait()
+        q = t.q_t[rows, :]
+        k_new = t.k_t[rows, :]
+        arrive = fetch(head)
+        for copy in arrive[:1]:
+            copy.wait()
         for s8 in range(0, slots, 8):
             out_rows = []
             for s in range(s8, s8 + 8):
-                cur = jnp.where(posv == jnp.asarray(s, BF16), k_new, kbuf[head, s])
-                kbuf[head, s] = cur
+                cur = jnp.where(posv == jnp.asarray(s, BF16), k_new, k_src[head, s])
+                t.kbuf[head, s] = cur
                 out_rows.append(jnp.sum(cur.astype(F32) * q, axis=0, keepdims=True))
-            prob[s8:s8 + 8, :] = jnp.concatenate(out_rows, axis=0)
+            t.prob[s8:s8 + 8, :] = jnp.concatenate(out_rows, axis=0)
         store_k(head).start()
-        line = jnp.broadcast_to(line_scr[pl.ds(head, 1), :], (slots, 128))
+        line = jnp.broadcast_to(t.line_scr[pl.ds(head, 1), :], (slots, 128))
         table = pltpu.roll(line, 0, 1, stride=1, stride_axis=0)
-        bias = jnp.dot(table, hot[...], precision=lax.Precision.HIGHEST, preferred_element_type=F32)
+        bias = jnp.dot(table, t.hot[...], precision=lax.Precision.HIGHEST, preferred_element_type=F32)
         slot_id = lax.broadcasted_iota(jnp.int32, bias.shape, 0)
-        scores = jnp.where(slot_id <= pos_scr[...], prob[...] + bias, NEG_BIG)
-        prob[...] = softmax_rows(scores).astype(BF16).astype(F32)
-        v_new = v_t[rows, :]
-        fetch_v(head).wait()
+        scores = jnp.where(slot_id <= t.pos_scr[...], t.prob[...] + bias, NEG_BIG)
+        t.prob[...] = softmax_rows(scores).astype(BF16).astype(F32)
+        v_new = t.v_t[rows, :]
+        for copy in arrive[1:]:
+            copy.wait()
         acc = jnp.zeros(q.shape, F32)
         for s in range(slots):
-            cur = jnp.where(posv == jnp.asarray(s, BF16), v_new, vbuf[head, s])
-            vbuf[head, s] = cur
-            acc = acc + prob[s:s + 1, :] * cur.astype(F32)
+            cur = jnp.where(posv == jnp.asarray(s, BF16), v_new, v_src[head, s])
+            t.vbuf[head, s] = cur
+            acc = acc + t.prob[s:s + 1, :] * cur.astype(F32)
         store_v(head).start()
-        ctx_t[rows, :] = acc
-
-    weights[3].wait()
-    ctx = jnp.transpose(ctx_t[...]).astype(BF16)
-    part_ref[...] = project(ctx, wo_scr[...]).astype(BF16)
+        t.ctx_t[rows, :] = acc
+
+    for copy in weights[3:]:
+        copy.wait()
+    ctx = jnp.transpose(t.ctx_t[...]).astype(BF16)
+    t.part_scr[...] = project(ctx, t.wo[...]).astype(BF16)
+    results.append(pltpu.make_async_copy(t.part_scr, t.part, t.o_sem.at[0]))
+    results[-1].start()
     for head in range(heads):
         store_k(head).wait()
         store_v(head).wait()
-
-
-def self_call(layer, chunk, h_cur, parts, pos, scale, bias, wq, wk, wv, wo, keys, values, outs):
+    for copy in ahead + results:
+        copy.wait()
+
+
+def weight_shapes(dim, width):
+    return [(dim, width)] * 3 + [(width, dim)]
+
+
+def self_call(layer, chunk, h_cur, pos, scale, bias, keys, values, outs=None, parts=None, weights=None, held=None, ready=None, ahead=None, ahead_first=0):
     heads, slots, head_dim, tokens = keys.shape[1:]
     tc = tokens // CHUNKS
-    dim, width = wq.shape[1:]
-    residual = parts is not None
-    aliased = outs is not None
-    in_specs = [VMEM_SPEC] * 3 if residual else [VMEM_SPEC if h_cur.shape[0] == tc else HBM_SPEC]
-    in_specs += [HBM_SPEC] * 9
-    args = [h_cur] + (list(parts) if residual else []) + [pos, scale, bias, wq, wk, wv, wo, keys, values]
-    rows = jax.ShapeDtypeStruct((tc, dim), BF16)
-    out_shape = [rows] * (1 + residual) + [jax.ShapeDtypeStruct(keys.shape, BF16)] * 2
-    out_specs = [VMEM_SPEC] * (1 + residual) + [HBM_SPEC] * 2
-    aliases = {}
-    if aliased:
-        aliases = {len(args): 1 + residual, len(args) + 1: 2 + residual}
-        args += list(outs)
-        in_specs += [HBM_SPEC] * 2
+    dim = h_cur.shape[1]
+    width = heads * head_dim
+    args, specs, aliases, names, out_shape, out_names, out_specs = [], [], {}, [], [], [], []
+
+    def take(spec, pairs):
+        for name, array in pairs:
+            names.append(name)
+            args.append(array)
+            specs.append(spec)
+
+    def give(name, shape):
+        out_names.append(name)
+        out_shape.append(pltpu.VMEM(shape, BF16))
+        out_specs.append(VMEM_SPEC)
+
+    def result(name):
+        out_names.append(name)
+        out_shape.append(pltpu.HBM((tc, dim), BF16))
+        out_specs.append(HBM_SPEC)
+
+    take(HBM_SPEC if h_cur.shape[0] != tc else VMEM_SPEC, [('h', h_cur)])
+    if parts is not None:
+        take(VMEM_SPEC, zip(('own', 'peer'), parts))
+        result('h_out')
+    result('part')
+    take(HBM_SPEC, (('pos', pos), ('scale', scale), ('bias', bias)))
+    if weights is not None:
+        take(HBM_SPEC, zip([name + '_hbm' for name in WEIGHTS], weights))
+        for name, shape in zip(WEIGHTS, weight_shapes(dim, width)):
+            give(name, shape)
+    else:
+        take(VMEM_SPEC, zip(WEIGHTS, held))
+    if ready is None:
+        take(HBM_SPEC, (('keys', keys), ('values', values)))
+    else:
+        take(VMEM_SPEC, zip(('k_ready', 'v_ready'), ready))
+    if ahead is not None:
+        take(HBM_SPEC, zip(('next_k', 'next_v'), ahead))
+        shape = (CHUNKS - ahead_first, heads, ahead[0].shape[2], head_dim, tc)
+        give('k_ahead', shape)
+        give('v_ahead', shape)
+    count = len(out_shape)
+    if outs is not None:
+        aliases = {len(args): count, len(args) + 1: count + 1}
+        take(HBM_SPEC, zip(('old_k', 'old_v'), outs))
+    out_shape += [jax.ShapeDtypeStruct(keys.shape, BF16)] * 2
+    scratch = dict(
+        pos_scr=pltpu.VMEM((1, tc), jnp.int32),
+        scale_scr=pltpu.VMEM(scale.shape[1:], F32),
+        bias_scr=pltpu.VMEM(bias.shape, F32),
+        line_scr=pltpu.VMEM((8, 128), F32),
+        kbuf=pltpu.VMEM((heads, slots, head_dim, tc), BF16),
+        vbuf=pltpu.VMEM((heads, slots, head_dim, tc), BF16),
+        q_t=pltpu.VMEM((width, tc), F32),
+        k_t=pltpu.VMEM((width, tc), BF16),
+        v_t=pltpu.VMEM((width, tc), BF16),
+        ctx_t=pltpu.VMEM((width, tc), F32),
+        prob=pltpu.VMEM((slots, tc), F32),
+        posb=pltpu.VMEM((head_dim, tc), BF16),
+        hot=pltpu.VMEM((128, tc), F32),
+        part_scr=pltpu.VMEM((tc, dim), BF16),
+        h_out_scr=pltpu.VMEM((tc, dim), BF16),
+        o_sem=pltpu.SemaphoreType.DMA((2,)),
+        small_sem=pltpu.SemaphoreType.DMA((4,)),
+        w_sem=pltpu.SemaphoreType.DMA((4,)),
+        a_sem=pltpu.SemaphoreType.DMA((4,)),
+        k_sem=pltpu.SemaphoreType.DMA((heads,)),
+        v_sem=pltpu.SemaphoreType.DMA((heads,)),
+        ko_sem=pltpu.SemaphoreType.DMA((heads,)),
+        vo_sem=pltpu.SemaphoreType.DMA((heads,)),
+    )
+    if h_cur.shape[0] != tc:
+        scratch.update(h_scr=pltpu.VMEM((tc, dim), BF16))
     size = heads * slots * head_dim * tc
     return pl.pallas_call(
-        functools.partial(self_kernel, layer, chunk, residual, aliased),
-        in_specs=in_specs,
-        out_specs=out_specs,
+        functools.partial(self_kernel, layer, chunk, ahead_first, tuple(names + out_names + ['ko', 'vo'] + list(scratch))),
+        in_specs=specs,
+        out_specs=out_specs + [HBM_SPEC] * 2,
         out_shape=out_shape,
         input_output_aliases=aliases,
-        scratch_shapes=[
-            pltpu.VMEM((tc, dim), BF16),
-            pltpu.VMEM((1, tc), jnp.int32),
-            pltpu.VMEM(scale.shape[1:], F32),
-            pltpu.VMEM(bias.shape, F32),
-            pltpu.VMEM((8, 128), F32),
-            pltpu.VMEM((dim, width), BF16),
-            pltpu.VMEM((dim, width), BF16),
-            pltpu.VMEM((dim, width), BF16),
-            pltpu.VMEM((width, dim), BF16),
-            pltpu.VMEM((heads, slots, head_dim, tc), BF16),
-            pltpu.VMEM((heads, slots, head_dim, tc), BF16),
-            pltpu.VMEM((width, tc), F32),
-            pltpu.VMEM((width, tc), BF16),
-            pltpu.VMEM((width, tc), BF16),
-            pltpu.VMEM((width, tc), F32),
-            pltpu.VMEM((slots, tc), F32),
-            pltpu.VMEM((head_dim, tc), BF16),
-            pltpu.VMEM((128, tc), F32),
-            pltpu.SemaphoreType.DMA((4,)),
-            pltpu.SemaphoreType.DMA((4,)),
-            pltpu.SemaphoreType.DMA((heads,)),
-            pltpu.SemaphoreType.DMA((heads,)),
-            pltpu.SemaphoreType.DMA((heads,)),
-            pltpu.SemaphoreType.DMA((heads,)),
-        ],
-        compiler_params=pltpu.CompilerParams(vmem_limit_bytes=48 << 20),
+        scratch_shapes=list(scratch.values()),
+        compiler_params=pltpu.CompilerParams(vmem_limit_bytes=SELF_LIMIT),
         cost_estimate=pl.CostEstimate(flops=size * 400, bytes_accessed=size * 8, transcendentals=0),
         name=f"self{layer}_{chunk}",
     )(*args)
@@ -212,10 +273,10 @@
     pl.semaphore_wait(barrier, len(devices))
 
 
-def cross_part(x, keys, values, mask_t, wq, wo, q_t, ctx_t, prob, before_attention, out_ref):
+def cross_part(x, keys, values, mask_t, wq, wo, q_t, ctx_t, prob, after_query, out_ref):
     heads, slots, head_dim, _ = keys.shape
     q_t[...] = jnp.transpose(project(x, wq[...])).astype(BF16).astype(F32)
-    before_attention()
+    after_query()
 
     @pl.loop(0, heads)
     def _(head):
@@ -237,16 +298,21 @@
     out_ref[...] = project(ctx, wo[...]).astype(BF16)
 
 
-def cross_scratch(heads, slots, head_dim, tokens, dim):
+def cross_scratch(heads, slots, head_dim, tokens, dim, caches, staged):
     tc = tokens // 2
     width = heads * head_dim
+    kept = {}
+    if caches:
+        kept = {name: pltpu.VMEM((2, heads, slots, head_dim, tc), BF16) for name in ('kbuf', 'vbuf')}
+        kept['kv_sem'] = pltpu.SemaphoreType.DMA((2, 2))
     return dict(
+        **kept,
+        staged=pltpu.VMEM((staged, tc, dim), BF16),
+        st_sem=pltpu.SemaphoreType.DMA((staged,)),
         scale_scr=pltpu.VMEM((3, 2, dim), F32),
         mask_scr=pltpu.VMEM((slots, tokens), jnp.int32),
         wq_scr=pltpu.VMEM((dim, width), BF16),
         wo_scr=pltpu.VMEM((width, dim), BF16),
-        kbuf=pltpu.VMEM((2, heads, slots, head_dim, tc), BF16),
-        vbuf=pltpu.VMEM((2, heads, slots, head_dim, tc), BF16),
         q_t=pltpu.VMEM((width, tc), F32),
         ctx_t=pltpu.VMEM((width, tc), F32),
         prob=pltpu.VMEM((slots, tc), F32),
@@ -254,13 +320,18 @@
         rbuf=pltpu.VMEM((4, tc, dim), BF16),
         send_sem=pltpu.SemaphoreType.DMA((4,)),
         recv_sem=pltpu.SemaphoreType.DMA((4,)),
-        c_sem=pltpu.SemaphoreType.DMA((8,)),
+        c_sem=pltpu.SemaphoreType.DMA((4,)),
     )
 
 
 class Cross:
-    def __init__(self, layer, r, t, count):
+    def __init__(self, layer, r, t, count, staged):
         self.layer, self.r, self.t = layer, r, t
+        self.rows = []
+        self.send_row = staged.index('p_b')
+        for i, name in enumerate(staged):
+            self.rows.append(pltpu.make_async_copy(getattr(r, name), t.staged.at[i], t.st_sem.at[i]))
+            setattr(r, name, t.staged.at[i])
         tc = t.sbuf.shape[1]
         self.loads = [
             pltpu.make_async_copy(r.scale, t.scale_scr, t.c_sem.at[0]),
@@ -268,29 +339,38 @@
             pltpu.make_async_copy(r.wq.at[layer], t.wq_scr, t.c_sem.at[2]),
             pltpu.make_async_copy(r.wo.at[layer], t.wo_scr, t.c_sem.at[3]),
         ]
-        self.kv = []
-        for c in range(2):
-            lanes = pl.ds(c * tc, tc)
-            self.kv.append([
-                pltpu.make_async_copy(r.keys.at[layer, :, :, :, lanes], t.kbuf.at[c], t.c_sem.at[4 + 2 * c]),
-                pltpu.make_async_copy(r.values.at[layer, :, :, :, lanes], t.vbuf.at[c], t.c_sem.at[5 + 2 * c]),
-            ])
+        self.caches = t.kbuf, t.vbuf
         peer = tp_peer()
         sources = [r.p_b] + [t.sbuf.at[i] for i in range(3)]
         self.swaps = [remote(sources[i], t.rbuf.at[i], (t.send_sem.at[i], t.recv_sem.at[i]), peer) for i in range(count)]
         self.tc = tc
 
+    def kv(self, c):
+        r, t, where = self.r, self.t, (self.layer, slice(None), slice(None), slice(None), pl.ds(c * self.tc, self.tc))
+        return [
+            pltpu.make_async_copy(r.keys.at[where], t.kbuf.at[c], t.kv_sem.at[c, 0]),
+            pltpu.make_async_copy(r.values.at[where], t.vbuf.at[c], t.kv_sem.at[c, 1]),
+        ]
+
+    def start_kv(self, c):
+        for copy in self.kv(c):
+            copy.start()
+
     def start_loads(self):
-        for copy in self.loads[:4] + self.kv[0]:
+        for copy in self.rows + self.loads[:4]:
             copy.start()
+        self.start_kv(0)
 
     def run(self, later):
         t, r = self.t, self.r
+        for copy in self.rows[self.send_row:self.send_row + 1]:
+            copy.wait()
         self.swaps[0].start()
+        for copy in self.rows[:self.send_row] + self.rows[self.send_row + 1:]:
+            copy.wait()
         for copy in self.loads:
             copy.wait()
-        for copy in self.kv[1]:
-            copy.start()
+        self.start_kv(1)
         streams = []
         for c in range(2):
             if c == 0:
@@ -301,21 +381,16 @@
             streams.append(h_cur)
             x = rms_norm(h_cur, t.scale_scr[1, self.layer:self.layer + 1, :])
 
-            def ready():
-                for copy in self.kv[c]:
+            def after_query():
+                for copy in self.kv(c):
                     copy.wait()
                 if c == 0:
                     for copy in later:
                         copy.start()
 
-            cross_part(x, t.kbuf.at[c], t.vbuf.at[c], t.mask_scr[:, c * self.tc:(c + 1) * self.tc], t.wq_scr, t.wo_scr, t.q_t, t.ctx_t, t.prob, ready, t.sbuf.at[c])
+            cross_part(x, self.caches[0].at[c], self.caches[1].at[c], t.mask_scr[:, c * self.tc:(c + 1) * self.tc], t.wq_scr, t.wo_scr, t.q_t, t.ctx_t, t.prob, after_query, t.sbuf.at[c])
             self.swaps[1 + c].start()
         return streams
-
-
-class Refs:
-    def __init__(self, names, refs):
-        self.__dict__.update(zip(names, refs, strict=True))
 
 
 CROSS_IN = ('h_a', 'h_b', 'p_a', 'peer_a', 'p_b', 'mask', 'scale', 'wq', 'wo', 'keys', 'values')
@@ -339,9 +414,14 @@
     stream.start()
     tc = t.acc.shape[0]
     r.h_a, r.h_b = t.h_scr.at[0:tc, :], t.h_scr.at[tc:, :]
-    cross = Cross(0, r, t, 4)
+    cross = Cross(0, r, t, 4, ('p_a', 'peer_a', 'p_b'))
     cross.loads.append(stream)
     cross.start_loads()
+    ahead = [pltpu.make_async_copy(getattr(r, name + '_next').at[1], getattr(r, name + '_out'), t.n_sem.at[i]) for i, name in enumerate(WEIGHTS)]
+    for c, (k_out, v_out) in enumerate(((r.k_a.at[0], r.v_a.at[0]), (r.k_b.at[0], r.v_b.at[0]))):
+        lanes = pl.ds(c * tc, tc)
+        ahead.append(pltpu.make_async_copy(r.next_k.at[1, :, :, :, lanes], k_out, t.n_sem.at[4 + 2 * c]))
+        ahead.append(pltpu.make_async_copy(r.next_v.at[1, :, :, :, lanes], v_out, t.n_sem.at[5 + 2 * c]))
     dense = [pltpu.make_async_copy(src, dst, t.d_sem.at[i]) for i, (src, dst) in enumerate(((r.wg, t.wg_scr), (r.wu, t.wu_scr), (r.wd, t.wd_scr)))]
     greet([tp_peer()])
     h_a, h_b = cross.run(dense)
@@ -349,6 +429,8 @@
     r.h2_b[...] = h_b
     for copy in dense:
         copy.wait()
+    for copy in ahead:
+        copy.start()
     scale = t.scale_scr[2, 0:1, :]
     cross.swaps[1].wait_recv()
     h_a = add_parts(r.h2_a[...], t.sbuf[0], t.rbuf[1])
@@ -363,13 +445,15 @@
     r.h2_a[...] = add_parts(r.h2_a[...], t.sbuf[2], t.rbuf[3])
     for copy in cross.swaps:
         copy.wait_send()
-
-
-def block_a_call(hidden, p_a, peer_a, p_b, mask, scale, wq, wo, keys, values, wg, wu, wd):
+    for copy in ahead:
+        copy.wait()
+
+
+def block_a_call(hidden, p_a, peer_a, p_b, mask, scale, wq, wo, keys, values, wg, wu, wd, next_weights, self_keys, self_values):
     _, heads, slots, head_dim, tokens = keys.shape
     dim, ff = wg.shape
     tc = tokens // 2
-    scratch = cross_scratch(heads, slots, head_dim, tokens, dim)
+    scratch = cross_scratch(heads, slots, head_dim, tokens, dim, True, 3)
     scratch.update(
         wg_scr=pltpu.VMEM((dim, ff), BF16),
         wu_scr=pltpu.VMEM((dim, ff), BF16),
@@ -377,19 +461,21 @@
         acc=pltpu.VMEM((tc, dim), F32),
         h_scr=pltpu.VMEM((tokens, dim), BF16),
         d_sem=pltpu.SemaphoreType.DMA((4,)),
+        n_sem=pltpu.SemaphoreType.DMA((8,)),
     )
-    names = ('hidden',) + CROSS_IN[2:] + ('wg', 'wu', 'wd', 'h2_a', 'h2_b', 'pd_b') + tuple(scratch)
-    rows = jax.ShapeDtypeStruct((tc, dim), BF16)
+    names = ('hidden',) + CROSS_IN[2:] + ('wg', 'wu', 'wd') + tuple(name + '_next' for name in WEIGHTS) + ('next_k', 'next_v', 'h2_a', 'h2_b', 'pd_b') + tuple(name + '_out' for name in WEIGHTS) + ('k_a', 'v_a', 'k_b', 'v_b') + tuple(scratch)
+    cache = (1,) + self_keys.shape[1:4] + (tc,)
+    shapes = [(tc, dim)] * 3 + weight_shapes(dim, heads * head_dim) + [cache] * 4
     return pl.pallas_call(
         functools.partial(block_a_kernel, names),
-        in_specs=[HBM_SPEC] + [VMEM_SPEC] * 3 + [HBM_SPEC] * 9,
-        out_specs=[VMEM_SPEC] * 3,
-        out_shape=[rows] * 3,
+        in_specs=[HBM_SPEC] * 19,
+        out_specs=[VMEM_SPEC] * 11,
+        out_shape=[pltpu.VMEM(shape, BF16) for shape in shapes],
         scratch_shapes=list(scratch.values()),
-        compiler_params=pltpu.CompilerParams(vmem_limit_bytes=48 << 20, collective_id=0, has_side_effects=True),
+        compiler_params=pltpu.CompilerParams(vmem_limit_bytes=30 << 20, collective_id=0, has_side_effects=True),
         cost_estimate=pl.CostEstimate(flops=20_000_000_000, bytes_accessed=20 << 20, transcendentals=0),
         name="block_a",
-    )(hidden, p_a, peer_a, p_b, mask, scale, wq, wo, keys, values, wg, wu, wd)
+    )(hidden, p_a, peer_a, p_b, mask, scale, wq, wo, keys, values, wg, wu, wd, *next_weights, self_keys, self_values)
 
 
 def block_b_kernel(names, *refs):
@@ -413,7 +499,7 @@
         slot = lax.rem(i, ring)
         return [pltpu.make_async_copy(src.at[i], dst.at[slot], t.e_sem.at[n, slot]) for n, (src, dst) in enumerate(((r.wg, t.wg_ring), (r.wu, t.wu_ring), (r.wd, t.wd_ring)))]
 
-    cross = Cross(1, r, t, 3)
+    cross = Cross(1, r, t, 3, ('p_b', 'p_a', 'peer_a', 'h_a', 'h_b'))
     cross.start_loads()
     side = [pltpu.make_async_copy(r.router, t.router_scr, t.s_sem.at[0]), pltpu.make_async_copy(r.idx, t.idx_scr, t.s_sem.at[1])]
     for copy in side:
@@ -574,7 +660,7 @@
     capacity = (2 * tokens + experts - 1) // experts
     ring = 5
     pieces = 4
-    scratch = cross_scratch(heads, slots, head_dim, tokens, dim)
+    scratch = cross_scratch(heads, slots, head_dim, tokens, dim, True, 5)
     hops = (group - 1, local)
     scratch.update(
         wg_ring=pltpu.VMEM((ring, dim, ff), BF16),
@@ -612,11 +698,11 @@
     names = CROSS_IN + ('router', 'idx', 'wg', 'wu', 'wd', 'out') + tuple(scratch)
     return pl.pallas_call(
         functools.partial(block_b_kernel, names),
-        in_specs=[VMEM_SPEC] * 5 + [HBM_SPEC] * 11,
+        in_specs=[HBM_SPEC] * 16,
         out_specs=VMEM_SPEC,
         out_shape=jax.ShapeDtypeStruct((tokens, dim), BF16),
         scratch_shapes=list(scratch.values()),
-        compiler_params=pltpu.CompilerParams(vmem_limit_bytes=62 << 20, collective_id=1, has_side_effects=True),
+        compiler_params=pltpu.CompilerParams(vmem_limit_bytes=B_LIMIT, collective_id=1, has_side_effects=True),
         cost_estimate=pl.CostEstimate(flops=40_000_000_000, bytes_accessed=70 << 20, transcendentals=0),
         name="block_b",
     )(h_a, h_b, p_a, peer_a, p_b, mask, scale, wq, wo, keys, values, router, idx, wg, wu, wd)
@@ -641,16 +727,19 @@
     keys, values, ckeys, cvalues = hbm(keys, values, ckeys, cvalues)
     dense_gate, dense_up, dense_down, exp_gate, exp_up, exp_down = hbm(dense_gate, dense_up, dense_down, exp_gate, exp_up, exp_down)
     router_t, idx = hbm(router.T, expert_idx.reshape(1, -1))
-    shared = (pos, scale, rel_bias, w_query, w_key, w_value, w_out, keys, values)
+    shared = (pos, scale, rel_bias, keys, values)
+    weights = (w_query, w_key, w_value, w_out)
     cross = (mask, scale, w_cross_query, w_cross_out, ckeys, cvalues)
-    p_a, *outs = self_call(0, 0, hidden, None, *shared, None)
+    p_a, *rest = self_call(0, 0, hidden, *shared, weights=weights)
+    held, outs = rest[:4], rest[4:]
     pair_a = swap(p_a)
-    p_b, *outs = self_call(0, 1, hidden, None, *shared, outs)
-    h_a, h_b, pd_b = block_a_call(hidden, *pair_a, p_b, *cross, dense_gate, dense_up, dense_down)
+    p_b, *outs = self_call(0, 1, hidden, *shared, outs=outs, held=held)
+    h_a, h_b, pd_b, *rest = block_a_call(hidden, *pair_a, p_b, *cross, dense_gate, dense_up, dense_down, weights, keys, values)
+    held, ready_a, ready_b = rest[:4], rest[4:6], rest[6:]
     pair_b = swap(pd_b)
-    p_a, *outs = self_call(1, 0, h_a, None, *shared, outs)
+    p_a, *outs = self_call(1, 0, h_a, *shared, outs=outs, held=held, ready=ready_a)
     pair_a = swap(p_a)
-    h_b, p_b, *outs = self_call(1, 1, h_b, pair_b, *shared, outs)
+    h_b, p_b, *outs = self_call(1, 1, h_b, *shared, outs=outs, parts=pair_b, held=held, ready=ready_b)
     h_all = block_b_call(h_a, h_b, *pair_a, p_b, *cross, router_t, idx, exp_gate, exp_up, exp_down, lax.axis_size('ep'))
     back = (0, 4, 1, 2, 3)
     return h_all, jnp.transpose(outs[0], back), jnp.transpose(outs[1], back)

time: 125 us -> 121 us (0.968)
  Pallas kernels: 114 us -> 112 us
    pallas_call x5, Pallas kernels: 95.1 us -> 90.8 us  [the longest x1 52 us: block_b_call(): pl.pallas_call(functools.partial(block_b_kernel, names), in_specs=[HBM_SP...]
    pallas_call x1, Pallas kernels: 19.3 us -> 20.8 us  [block_a_call(): pl.pallas_call(functools.partial(block_a_kernel, names), in_specs=[HBM_SP...]
    unnamed x11 -> x7, local copies, waits for them, and re-layouts: 3.8 us -> 3.11 us
  transfers between devices with their start and end apart: 3 -> 3, of which waited for: 0 -> 0; matrix products, arithmetic and copies ran while one was open for 0% -> 0% of each run, Pallas kernels for 25% -> 23%
where the time goes in v4:
time: 121 us
  Pallas kernels  112 us (93%)
  starting transfers between devices  5.46 us (5%)
  local copies, waits for them, and re-layouts  3.11 us (3%)
    pallas_call x1, Pallas kernels, block_b_call(): pl.pallas_call(functools.partial(block_b_kernel, names), in_specs=[HBM_SP...  52 us
    pallas_call x4, Pallas kernels, self_call(): pl.pallas_call(functools.partial(self_kernel, layer, chunk, ahead_first,...  38.8 us
    pallas_call x1, Pallas kernels, block_a_call(): pl.pallas_call(functools.partial(block_a_kernel, names), in_specs=[HBM_SP...  20.8 us
    ppermute x3, starting transfers between devices, swap(): return (part, lax.ppermute(part, 'tp', SWAP))  5.46 us
    unnamed x7, local copies, waits for them, and re-layouts  3.11 us
  transfers between devices with their start and end apart: 3, of which 0 were waited for; matrix products, arithmetic and copies ran while one was open for 0% of the time, Pallas kernels for 23%

profile of v4, /device:TPU:0, one launch (start us, length us, event | category | flops | bytes accessed | tf_op | source)
XLA Modules:
  0.0 120.9 jit_solution(14929164746964526512)
XLA Ops:
  0.6 10.8 %self0_0.1 = (bf16[128,768]{1,0:T(8,128)(2,1)}, bf16[768,384]{1,0:T(8,128)(2,1)S(1)}, bf16[768,384]{1,0:T(8,128)(2,1)S(1)}, bf16[768,384]{1,0:T(8,128)(2,1)S(1)}...) custom-call(bf16[256,768]{1,0:T(8,128)(2,1)} %refs_0_.5, ...), custom_call_target="tpu_custom_call" | custom-call | flops 1258291200 | bytes 25165824 | tf_op jit(solution)/shard_map/self0_0/pallas_call | solution.py:248
  11.5 3.4 %collective-permute-start = (bf16[128,768]{1,0:T(8,128)(2,1)}, bf16[128,768]{1,0:T(8,128)(2,1)S(1)}, u32[]{:S(2)}, u32[]{:S(2)}) collective-permute-start(bf16[128,768]{1,0:T(8,128)(2,1)} %get-tuple-element.31.refs_1_), channel_id=1, source_target_pairs={{0,4},{4,0},{1,5},{5,1},{2,6},{6,2},{3,7},{7,3}} | collective-permute-start | bytes 589832 | tf_op jit(solution)/shard_map/ppermute | solution.py:712
  14.9 10.3 %self0_1.1 = (bf16[128,768]{1,0:T(8,128)(2,1)}, bf16[2,6,64,64,256]{4,3,2,1,0:T(8,128)(2,1)}, bf16[2,6,64,64,256]{4,3,2,1,0:T(8,128)(2,1)}) custom-call(bf16[256,768]{1,0:T(8,128)(2,1)} %refs_0_.5, s32[1,256]{1,0:T(1,128)} %bitcast.32, f32[3,2,768]{2,1,0:T(2,128)} %bitcast.24, f32[6,64]{1,0:T(8,128)} %refs_5_.3, ...), custom_call_target="tpu_custom_call", output_to_operand_aliasing={{1}: (10, {}), {2}: (11, {})} | custom-call | flops 1258291200 | bytes 25165824 | tf_op jit(solution)/shard_map/self0_1/pallas_call | solution.py:248
  25.2 0.0 collective-permute-done.refs_2_
  25.2 0.0 copy-start.1
  25.2 0.7 copy-done.1
  25.9 20.8 %block_a.1 = (bf16[128,768]{1,0:T(8,128)(2,1)S(1)}, bf16[128,768]{1,0:T(8,128)(2,1)S(1)}, bf16[128,768]{1,0:T(8,128)(2,1)S(1)}, bf16[768,384]{1,0:T(8,128)(2,1)S...) custom-call(bf16[256,768]{1,0:T(8,128)(2,1)} %refs_0_.5, ...), custom_call_target="tpu_custom_call" | custom-call | flops 20000000000 | bytes 20971520 | tf_op jit(solution)/shard_map/block_a/pallas_call | solution.py:469
  46.7 0.0 copy-start
  46.7 1.3 %collective-permute-start.1 = (bf16[128,768]{1,0:T(8,128)(2,1)S(1)}, bf16[128,768]{1,0:T(8,128)(2,1)S(1)}, u32[]{:S(2)}, u32[]{:S(2)}) collective-permute-start(bf16[128,768]{1,0:T(8,128)(2,1)S(1)} %get-tuple-element.41.refs_1_), channel_id=1, source_target_pairs={{0,4},{4,0},{1,5},{5,1},{2,6},{6,2},{3,7},{7,3}} | collective-permute-start | bytes 589832 | tf_op jit(solution)/shard_map/ppermute | solution.py:712
  48.0 8.8 %self1_0.1 = (bf16[128,768]{1,0:T(8,128)(2,1)}, bf16[2,6,64,64,256]{4,3,2,1,0:T(8,128)(2,1)}, bf16[2,6,64,64,256]{4,3,2,1,0:T(8,128)(2,1)}) custom-call(bf16[128,768]{1,0:T(8,128)(2,1)S(1)} %get-tuple-element.39.refs_0_, s32[1,256]{1,0:T(1,128)} %bitcast.33, f32[3,2,768]{2,1,0:T(2,128)} %bitcast.26, ...), custom_call_target="tpu_custom_call", output_to_operand_aliasing={{1}: (10, {}), {2}: (11, {})} | custom-call | flops 1258291200 | bytes 25165824 | tf_op jit(solution)/shard_map/self1_0/pallas_call | solution.py:248
  56.8 0.0 copy-done
  56.8 0.7 collective-permute-start.2
  57.5 0.0 collective-permute-done.1.refs_2_
  57.5 8.9 %self1_1.1 = (bf16[128,768]{1,0:T(8,128)(2,1)}, bf16[128,768]{1,0:T(8,128)(2,1)}, bf16[2,6,64,64,256]{4,3,2,1,0:T(8,128)(2,1)}, bf16[2,6,64,64,256]{4,3,2,1,0:T(8,128)(2,1)}) custom-call(bf16[128,768]{1,0:T(8,128)(2,1)S(1)} %get-tuple-element.40.refs_0_, ...), custom_call_target="tpu_custom_call", output_to_operand_aliasing={{2}: (12, {}), {3}: (13, {})} | custom-call | flops 1258291200 | bytes 25165824 | tf_op jit(solution)/shard_map/self1_1/pallas_call | solution.py:248
  66.4 0.0 collective-permute-done.2.refs_3_
  66.4 0.0 copy-start.2
  66.4 0.7 copy-done.2
  67.1 52.0 %block_b.1 = bf16[256,768]{1,0:T(8,128)(2,1)} custom-call(bf16[128,768]{1,0:T(8,128)(2,1)} %copy-done, bf16[128,768]{1,0:T(8,128)(2,1)} %get-tuple-element.54.refs_1_, bf16[128,768]{1,0:T(8,128)(2,1)} %get-tuple-element.55.refs_2_, bf16[128,768]{1,0:T(8,128)(2,1)} %copy-done.2, bf16[128,768]{1,0:T(8,128)(2,1)} %get-tuple-element.56.refs_4_, ...), custom_call_target="tpu_custom_call" | custom-call | flops 40000000000 | bytes 73400320 | tf_op jit(solution)/shard_map/block_b/pallas_call | solution.py:699
  119.1 1.8 %copy.39 = bf16[256,768]{1,0:T(8,128)(2,1)} copy(bf16[256,768]{1,0:T(8,128)(2,1)} %block_b.1) | data formatting | bytes 786432
Async XLA Ops:
  11.5 13.7 %collective-permute-start = (bf16[128,768]{1,0:T(8,128)(2,1)}, bf16[128,768]{1,0:T(8,128)(2,1)S(1)}, u32[]{:S(2)}, u32[]{:S(2)}) collective-permute-start(bf16[128,768]{1,0:T(8,128)(2,1)} %get-tuple-element.31.refs_1_), channel_id=1, source_target_pairs={{0,4},{4,0},{1,5},{5,1},{2,6},{6,2},{3,7},{7,3}} | collective-permute-start | bytes 589832 | tf_op jit(solution)/shard_map/ppermute | solution.py:712
  25.2 0.7 copy-start.1
  46.7 10.1 %copy-start = (bf16[128,768]{1,0:T(8,128)(2,1)}, bf16[128,768]{1,0:T(8,128)(2,1)S(1)}, u32[]{:S(2)}) copy-start(bf16[128,768]{1,0:T(8,128)(2,1)S(1)} %get-tuple-element.39.refs_0_) | copy-start | bytes 589828
  46.7 10.9 %collective-permute-start.1 = (bf16[128,768]{1,0:T(8,128)(2,1)S(1)}, bf16[128,768]{1,0:T(8,128)(2,1)S(1)}, u32[]{:S(2)}, u32[]{:S(2)}) collective-permute-start(bf16[128,768]{1,0:T(8,128)(2,1)S(1)} %get-tuple-element.41.refs_1_), channel_id=1, source_target_pairs={{0,4},{4,0},{1,5},{5,1},{2,6},{6,2},{3,7},{7,3}} | collective-permute-start | bytes 589832 | tf_op jit(solution)/shard_map/ppermute | solution.py:712
  56.8 9.6 %collective-permute-start.2 = (bf16[128,768]{1,0:T(8,128)(2,1)}, bf16[128,768]{1,0:T(8,128)(2,1)S(1)}, u32[]{:S(2)}, u32[]{:S(2)}) collective-permute-start(bf16[128,768]{1,0:T(8,128)(2,1)} %get-tuple-element.55.refs_2_), channel_id=1, source_target_pairs={{0,4},{4,0},{1,5},{5,1},{2,6},{6,2},{3,7},{7,3}} | collective-permute-start | bytes 589832 | tf_op jit(solution)/shard_map/ppermute | solution.py:712
  66.4 0.7 copy-start.2

commit v5 on v4

--- a/solution.py
+++ b/solution.py
@@ -600,12 +600,21 @@
         slot = lax.rem(i, ring)
         copies = fetch(i)
         x = t.xin[i]
-        copies[0].wait()
-        gate_in = jax.nn.gelu(project(x, t.wg_ring[slot]))
-        copies[1].wait()
-        product = (gate_in * project(x, t.wu_ring[slot])).astype(BF16)
-        copies[2].wait()
-        result = project(product, t.wd_ring[slot]).astype(BF16)
+        for copy in copies:
+            copy.wait()
+        total_out = None
+        for f in range(0, t.wg_ring.shape[2], 768):
+            cols = slice(f, f + 768)
+            gate_in = jax.nn.gelu(project(x, t.wg_ring[slot, :, cols]))
+            product = (gate_in * project(x, t.wu_ring[slot, :, cols])).astype(BF16)
+            piece = project(product, t.wd_ring[slot, cols, :])
+            total_out = piece if total_out is None else total_out + piece
+        result = total_out.astype(BF16)
+        @pl.when(i + ring < local)
+        def _():
+            for copy in fetch(i + ring):
+                copy.start()
+
         low, high = result[:, :half], result[:, half:]
         t.ysum[i] = jnp.where(tp == 0, low, high)
         t.yout[i] = jnp.where(tp == 0, high, low)
@@ -614,11 +623,6 @@
         @pl.when(i >= lag)
         def _():
             give_back(i - lag)
-
-        @pl.when(i + ring < local)
-        def _():
-            for copy in fetch(i + ring):
-                copy.start()
 
     @pl.loop(local - lag, local)
     def _(i):

time: 121 us -> 119 us (0.983)
  Pallas kernels: 112 us -> 110 us
    pallas_call x1, Pallas kernels: 52 us -> 50 us  [block_b_call(): pl.pallas_call(functools.partial(block_b_kernel, names), in_specs=[HBM_SP...]
  transfers between devices with their start and end apart: 3 -> 3, of which waited for: 0 -> 0; matrix products, arithmetic and copies ran while one was open for 0% -> 0% of each run, Pallas kernels for 23% -> 24%
where the time goes in v5:
time: 119 us
  Pallas kernels  110 us (92%)
  starting transfers between devices  5.46 us (5%)
  local copies, waits for them, and re-layouts  3.11 us (3%)
    pallas_call x1, Pallas kernels, block_b_call(): pl.pallas_call(functools.partial(block_b_kernel, names), in_specs=[HBM_SP...  50 us
    pallas_call x4, Pallas kernels, self_call(): pl.pallas_call(functools.partial(self_kernel, layer, chunk, ahead_first,...  38.8 us
    pallas_call x1, Pallas kernels, block_a_call(): pl.pallas_call(functools.partial(block_a_kernel, names), in_specs=[HBM_SP...  20.8 us
    ppermute x3, starting transfers between devices, swap(): return (part, lax.ppermute(part, 'tp', SWAP))  5.46 us
    unnamed x7, local copies, waits for them, and re-layouts  3.11 us
  transfers between devices with their start and end apart: 3, of which 0 were waited for; matrix products, arithmetic and copies ran while one was open for 0% of the time, Pallas kernels for 24%

profile of v5, /device:TPU:0, one launch (start us, length us, event | category | flops | bytes accessed | tf_op | source)
XLA Modules:
  0.0 118.9 jit_solution(15864032039738871676)
XLA Ops:
  0.6 10.8 %self0_0.1 = (bf16[128,768]{1,0:T(8,128)(2,1)}, bf16[768,384]{1,0:T(8,128)(2,1)S(1)}, bf16[768,384]{1,0:T(8,128)(2,1)S(1)}, bf16[768,384]{1,0:T(8,128)(2,1)S(1)}...) custom-call(bf16[256,768]{1,0:T(8,128)(2,1)} %refs_0_.5, ...), custom_call_target="tpu_custom_call" | custom-call | flops 1258291200 | bytes 25165824 | tf_op jit(solution)/shard_map/self0_0/pallas_call | solution.py:248
  11.5 3.4 %collective-permute-start = (bf16[128,768]{1,0:T(8,128)(2,1)}, bf16[128,768]{1,0:T(8,128)(2,1)S(1)}, u32[]{:S(2)}, u32[]{:S(2)}) collective-permute-start(bf16[128,768]{1,0:T(8,128)(2,1)} %get-tuple-element.31.refs_1_), channel_id=1, source_target_pairs={{0,4},{4,0},{1,5},{5,1},{2,6},{6,2},{3,7},{7,3}} | collective-permute-start | bytes 589832 | tf_op jit(solution)/shard_map/ppermute | solution.py:716
  14.9 10.3 %self0_1.1 = (bf16[128,768]{1,0:T(8,128)(2,1)}, bf16[2,6,64,64,256]{4,3,2,1,0:T(8,128)(2,1)}, bf16[2,6,64,64,256]{4,3,2,1,0:T(8,128)(2,1)}) custom-call(bf16[256,768]{1,0:T(8,128)(2,1)} %refs_0_.5, s32[1,256]{1,0:T(1,128)} %bitcast.32, f32[3,2,768]{2,1,0:T(2,128)} %bitcast.24, f32[6,64]{1,0:T(8,128)} %refs_5_.3, ...), custom_call_target="tpu_custom_call", output_to_operand_aliasing={{1}: (10, {}), {2}: (11, {})} | custom-call | flops 1258291200 | bytes 25165824 | tf_op jit(solution)/shard_map/self0_1/pallas_call | solution.py:248
  25.2 0.0 collective-permute-done.refs_2_
  25.2 0.0 copy-start.1
  25.2 0.7 copy-done.1
  25.9 20.8 %block_a.1 = (bf16[128,768]{1,0:T(8,128)(2,1)S(1)}, bf16[128,768]{1,0:T(8,128)(2,1)S(1)}, bf16[128,768]{1,0:T(8,128)(2,1)S(1)}, bf16[768,384]{1,0:T(8,128)(2,1)S...) custom-call(bf16[256,768]{1,0:T(8,128)(2,1)} %refs_0_.5, ...), custom_call_target="tpu_custom_call" | custom-call | flops 20000000000 | bytes 20971520 | tf_op jit(solution)/shard_map/block_a/pallas_call | solution.py:469
  46.7 0.0 copy-start
  46.7 1.3 %collective-permute-start.1 = (bf16[128,768]{1,0:T(8,128)(2,1)S(1)}, bf16[128,768]{1,0:T(8,128)(2,1)S(1)}, u32[]{:S(2)}, u32[]{:S(2)}) collective-permute-start(bf16[128,768]{1,0:T(8,128)(2,1)S(1)} %get-tuple-element.41.refs_1_), channel_id=1, source_target_pairs={{0,4},{4,0},{1,5},{5,1},{2,6},{6,2},{3,7},{7,3}} | collective-permute-start | bytes 589832 | tf_op jit(solution)/shard_map/ppermute | solution.py:716
  48.0 8.8 %self1_0.1 = (bf16[128,768]{1,0:T(8,128)(2,1)}, bf16[2,6,64,64,256]{4,3,2,1,0:T(8,128)(2,1)}, bf16[2,6,64,64,256]{4,3,2,1,0:T(8,128)(2,1)}) custom-call(bf16[128,768]{1,0:T(8,128)(2,1)S(1)} %get-tuple-element.39.refs_0_, s32[1,256]{1,0:T(1,128)} %bitcast.33, f32[3,2,768]{2,1,0:T(2,128)} %bitcast.26, ...), custom_call_target="tpu_custom_call", output_to_operand_aliasing={{1}: (10, {}), {2}: (11, {})} | custom-call | flops 1258291200 | bytes 25165824 | tf_op jit(solution)/shard_map/self1_0/pallas_call | solution.py:248
  56.8 0.0 copy-done
  56.8 0.7 collective-permute-start.2
  57.5 0.0 collective-permute-done.1.refs_2_
  57.5 8.9 %self1_1.1 = (bf16[128,768]{1,0:T(8,128)(2,1)}, bf16[128,768]{1,0:T(8,128)(2,1)}, bf16[2,6,64,64,256]{4,3,2,1,0:T(8,128)(2,1)}, bf16[2,6,64,64,256]{4,3,2,1,0:T(8,128)(2,1)}) custom-call(bf16[128,768]{1,0:T(8,128)(2,1)S(1)} %get-tuple-element.40.refs_0_, ...), custom_call_target="tpu_custom_call", output_to_operand_aliasing={{2}: (12, {}), {3}: (13, {})} | custom-call | flops 1258291200 | bytes 25165824 | tf_op jit(solution)/shard_map/self1_1/pallas_call | solution.py:248
  66.4 0.0 collective-permute-done.2.refs_3_
  66.4 0.0 copy-start.2
  66.4 0.7 copy-done.2
  67.1 50.0 %block_b.1 = bf16[256,768]{1,0:T(8,128)(2,1)} custom-call(bf16[128,768]{1,0:T(8,128)(2,1)} %copy-done, bf16[128,768]{1,0:T(8,128)(2,1)} %get-tuple-element.54.refs_1_, bf16[128,768]{1,0:T(8,128)(2,1)} %get-tuple-element.55.refs_2_, bf16[128,768]{1,0:T(8,128)(2,1)} %copy-done.2, bf16[128,768]{1,0:T(8,128)(2,1)} %get-tuple-element.56.refs_4_, ...), custom_call_target="tpu_custom_call" | custom-call | flops 40000000000 | bytes 73400320 | tf_op jit(solution)/shard_map/block_b/pallas_call | solution.py:703
  117.1 1.8 %copy.39 = bf16[256,768]{1,0:T(8,128)(2,1)} copy(bf16[256,768]{1,0:T(8,128)(2,1)} %block_b.1) | data formatting | bytes 786432
Async XLA Ops:
  11.5 13.7 %collective-permute-start = (bf16[128,768]{1,0:T(8,128)(2,1)}, bf16[128,768]{1,0:T(8,128)(2,1)S(1)}, u32[]{:S(2)}, u32[]{:S(2)}) collective-permute-start(bf16[128,768]{1,0:T(8,128)(2,1)} %get-tuple-element.31.refs_1_), channel_id=1, source_target_pairs={{0,4},{4,0},{1,5},{5,1},{2,6},{6,2},{3,7},{7,3}} | collective-permute-start | bytes 589832 | tf_op jit(solution)/shard_map/ppermute | solution.py:716
  25.2 0.7 copy-start.1
  46.7 10.1 %copy-start = (bf16[128,768]{1,0:T(8,128)(2,1)}, bf16[128,768]{1,0:T(8,128)(2,1)S(1)}, u32[]{:S(2)}) copy-start(bf16[128,768]{1,0:T(8,128)(2,1)S(1)} %get-tuple-element.39.refs_0_) | copy-start | bytes 589828
  46.7 10.9 %collective-permute-start.1 = (bf16[128,768]{1,0:T(8,128)(2,1)S(1)}, bf16[128,768]{1,0:T(8,128)(2,1)S(1)}, u32[]{:S(2)}, u32[]{:S(2)}) collective-permute-start(bf16[128,768]{1,0:T(8,128)(2,1)S(1)} %get-tuple-element.41.refs_1_), channel_id=1, source_target_pairs={{0,4},{4,0},{1,5},{5,1},{2,6},{6,2},{3,7},{7,3}} | collective-permute-start | bytes 589832 | tf_op jit(solution)/shard_map/ppermute | solution.py:716
  56.8 9.6 %collective-permute-start.2 = (bf16[128,768]{1,0:T(8,128)(2,1)}, bf16[128,768]{1,0:T(8,128)(2,1)S(1)}, u32[]{:S(2)}, u32[]{:S(2)}) collective-permute-start(bf16[128,768]{1,0:T(8,128)(2,1)} %get-tuple-element.55.refs_2_), channel_id=1, source_target_pairs={{0,4},{4,0},{1,5},{5,1},{2,6},{6,2},{3,7},{7,3}} | collective-permute-start | bytes 589832 | tf_op jit(solution)/shard_map/ppermute | solution.py:716
  66.4 0.7 copy-start.2
